TPU v7x, 32 devices: a whole 2x2x4 slice. The times are simulated.
32 devices in a mesh: data: 2 (over x), tp: 4 (over z), ep: 4 (over y, core).
Axes of the slice: x: 2, y: 2, z: 4, core: 2. Of those that a mesh axis runs over, the one named last changes fastest.
Arguments:
- tokens: bfloat16 [8192, 2048], P(('data', 'ep', 'tp')), parts along dimension 0
- expert_ids: int32 [8192, 6], P(('data', 'ep', 'tp')), parts along dimension 0
- gate_vals: float32 [8192, 6], P(('data', 'ep', 'tp')), parts along dimension 0
- slot_ids: int32 [8192, 6], P(('data', 'ep', 'tp')), parts along dimension 0
- send_counts: int32 [32, 64], P(('data', 'ep', 'tp')), parts along dimension 0
- shared_w1: bfloat16 [2048, 2816], P(None, 'tp')
- shared_w3: bfloat16 [2048, 2816], P(None, 'tp')
- shared_w2: bfloat16 [2816, 2048], P('tp')
- expert_w1: bfloat16 [64, 2048, 1408], P('ep')
- expert_w3: bfloat16 [64, 2048, 1408], P('ep')
- expert_w2: bfloat16 [64, 1408, 2048], P('ep')
Outputs:
- output: bfloat16 [8192, 2048], P(('data', 'ep', 'tp')), parts along dimension 0
There are 2 independent parts. A program takes and returns all parts, laid end to end along the dimension named above; an argument that names none is the same for every part.
All inputs are finite; a program needn't handle non-finite values.
Results may differ from a plain program's by a relative error of at most 0.00128.
Values are sent between devices in bfloat16 or wider.
A program may use at most 1.25 GiB of HBM per device.

v0:
```python
import jax
import jax.numpy as jnp
from jax import lax
from jax.sharding import PartitionSpec as P

CAP_FACTOR = 4


def capacity_rows(n_tok, top_k, n_exp):
    return min(n_tok, ((CAP_FACTOR * n_tok * top_k // n_exp + 7) // 8) * 8)


def solution(mesh):
    ep_size = mesh.shape["ep"]
    row_spec = P(("data", "ep", "tp"), None)
    expert_spec = P("ep", None, None)

    def layer_body(tokens, expert_ids, gate_vals, slot_ids, send_counts, shared_w1, shared_w3, shared_w2, expert_w1, expert_w3, expert_w2):
        n_tok, d_model = tokens.shape
        top_k = expert_ids.shape[1]
        n_local = expert_w1.shape[0]
        n_exp = n_local * ep_size
        capacity = capacity_rows(n_tok, top_k, n_exp)
        n_rows = n_exp * capacity

        gathered = lax.all_gather(tokens, "tp", axis=0, tiled=True)
        pre_gate = jnp.dot(gathered, shared_w1, preferred_element_type=jnp.float32)
        pre_up = jnp.dot(gathered, shared_w3, preferred_element_type=jnp.float32)
        shared_hidden = (jax.nn.silu(pre_gate) * pre_up).astype(jnp.bfloat16)
        part_sum = jnp.dot(shared_hidden, shared_w2, preferred_element_type=jnp.float32)
        shared_out = lax.psum_scatter(part_sum, "tp", scatter_dimension=0, tiled=True)

        row_limit = jnp.take(send_counts[0], expert_ids, axis=0)
        kept_mask = (slot_ids >= 0) & (slot_ids < row_limit)
        dest_row = jnp.where(kept_mask, expert_ids * capacity + slot_ids, n_rows)
        tok_ids = jnp.broadcast_to(jnp.arange(n_tok, dtype=jnp.int32)[:, None], (n_tok, top_k)).reshape(-1)
        owner_ids = jnp.full((n_rows,), n_tok, jnp.int32).at[dest_row.reshape(-1)].set(tok_ids, mode="drop")
        send_buf = jnp.take(tokens, owner_ids, axis=0, mode="fill", fill_value=0)
        send_buf = send_buf.reshape(ep_size, n_local, capacity, d_model)
        recv_buf = lax.all_to_all(send_buf, "ep", 0, 2, tiled=True)
        recv_buf = recv_buf.reshape(n_local, ep_size * capacity, d_model)

        exp_gate = jnp.einsum("erd,edf->erf", recv_buf, expert_w1, preferred_element_type=jnp.float32)
        exp_up = jnp.einsum("erd,edf->erf", recv_buf, expert_w3, preferred_element_type=jnp.float32)
        exp_hidden = (jax.nn.silu(exp_gate) * exp_up).astype(jnp.bfloat16)
        exp_out = jnp.einsum("erf,efd->erd", exp_hidden, expert_w2, preferred_element_type=jnp.float32).astype(jnp.bfloat16)
        back_buf = lax.all_to_all(exp_out.reshape(1, n_local, ep_size * capacity, d_model), "ep", 2, 0, tiled=True)

        back_rows = back_buf.reshape(n_rows, d_model)
        picked = jnp.take(back_rows, dest_row, axis=0, mode="fill", fill_value=0)
        gate_eff = jnp.where(kept_mask, gate_vals, 0.0)
        routed_sum = jnp.sum(gate_eff[:, :, None] * picked.astype(jnp.float32), axis=1)
        return (tokens.astype(jnp.float32) + shared_out + routed_sum).astype(jnp.bfloat16)

    return jax.shard_map(
        layer_body,
        mesh=mesh,
        in_specs=(row_spec, row_spec, row_spec, row_spec, row_spec, P(None, "tp"), P(None, "tp"), P("tp", None), expert_spec, expert_spec, expert_spec),
        out_specs=row_spec,
        check_vma=False,
    )
```

profile of v0, /device:TPU:0, one launch (start us, length us, event | category | flops | bytes accessed | tf_op | source)
XLA Modules:
  0.0 941.8 jit_solution(12905316323157057850)
XLA Ops:
  6.5 0.0 copy-start
  6.5 0.0 copy-start.1
  6.5 0.9 compare_select_fusion.3
  7.4 0.1 copy.46
  7.5 0.1 reshape.75
  7.7 0.0 copy-done.1
  7.7 0.0 copy-start.4
  7.7 0.0 copy-start.8
  7.7 9.0 gather_fusion
  16.8 0.1 reshape.74
  16.9 0.1 copy.47
  17.0 0.0 copy-done.4
  17.0 0.0 copy-done.8
  17.0 0.6 compare_and_fusion.1
  17.6 0.0 copy-start.2
  17.6 0.1 copy.50
  17.8 0.1 reshape.68
  18.0 0.1 reshape.101
  18.1 6.2 scatter_custom_fusion
  24.4 0.1 broadcast_in_dim.60
  24.5 47.7 %gather_fusion.1 = bf16[6144,2048]{1,0:T(8,128)(2,1)} fusion(bf16[256,2048]{1,0:T(8,128)(2,1)} %param.11, s32[6144]{0:T(1024)S(1)} %fusion.1), kind=kCustom, calls=%fused_computation.1 | custom fusion | bytes 50356224 | tf_op jit(solution)/shard_map/jit(_take)/gather | solution.py:38
  72.2 0.0 copy-done.2
  72.2 20.8 %broadcast_select_fusion = bf16[4,16,96,2048]{3,2,1,0:T(8,128)(2,1)} fusion(bf16[4,16,96,2048]{3,2,1,0:T(8,128)(2,1)} %bitcast.41, pred[4,16,96]{2,1,0:T(8,128)(4,1)S(1)} %broadcast_in_dim.60), kind=kLoop, calls=%fused_computation.6 | loop fusion | flops 12582912 | bytes 50337792 | tf_op jit(solution)/shard_map/jit(_take)/select_n | solution.py:38
  93.0 8.4 all-to-all-start
  101.5 0.2 all-gather.2.cloned.1.call-start
  101.7 0.5 all-gather.2.cloned.1.call-update
  102.2 272.5 %all-to-all-done = bf16[4,16,96,2048]{3,2,1,0:T(8,128)(2,1)} async-done(((bf16[4,16,96,2048]{3,2,1,0:T(8,128)(2,1)}), bf16[4,16,96,2048]{3,2,1,0:T(8,128)(2,1)}, u32[]{:S(2)}, u32[]{:S(2)}) %all-to-all-start) | async-done | bytes 25165856 | tf_op jit(solution)/shard_map/all_to_all | solution.py:40
  374.7 21.0 %copy.51 = bf16[1,16,4,96,2048]{4,3,2,1,0:T(8,128)(2,1)} copy(bf16[1,16,4,96,2048]{4,3,1,2,0:T(8,128)(2,1)} %bitcast.3) | data formatting | bytes 50331648 | tf_op jit(solution)/shard_map/all_to_all | solution.py:40
  395.7 58.9 %fusion.9 = f32[16,384,1408]{2,1,0:T(8,128)} fusion(bf16[16,384,2048]{2,1,0:T(8,128)(2,1)} %bitcast.42, bf16[16,2048,1408]{2,1,0:T(8,128)(2,1)} %param.19), kind=kOutput, calls=%fused_computation.29 | convolution fusion | flops 35433480192 | bytes 152043520 | tf_op jit(solution)/shard_map/erd,edf->erf/dot_general | solution.py:43
  454.6 94.8 %convert_bitcast_fusion = bf16[1,16,384,2048]{3,2,1,0:T(8,128)(2,1)} fusion(bf16[16,1408,2048]{2,1,0:T(8,128)(2,1)} %param.21, f32[16,384,1408]{2,1,0:T(8,128)} %fusion.9, bf16[16,384,2048]{2,1,0:T(8,128)(2,1)} %bitcast.43, bf16[16,2048,1408]{2,1,0:T(8,128)(2,1)} %param.20), kind=kOutput, calls=%fused_computation.5 | convolution fusion | flops 70931447808 | bytes 269484032 | tf_op jit(solution)/shard_map/erf,efd->erd/dot_general | solution.py:46
  549.4 26.8 %copy.52 = bf16[1,16,384,2048]{3,1,0,2:T(8,128)(2,1)} copy(bf16[1,16,384,2048]{3,2,1,0:T(8,128)(2,1)} %convert_bitcast_fusion) | data formatting | bytes 50331648 | tf_op jit(solution)/shard_map/reshape | solution.py:47
  576.2 8.4 all-to-all-start.1
  584.6 0.0 reduce-scatter.2.cloned.1.call-start
  584.7 0.0 all-gather.2.cloned.1.call-done
  584.7 7.9 fusion.8
  592.6 0.0 copy-done
  592.6 0.0 copy-start.3
  592.6 0.0 copy-start.6
  592.6 0.0 copy-start.7
  592.6 0.0 copy-start.5
  592.6 12.0 %fusion = f32[1024,2048]{1,0:T(8,128)} fusion(bf16[704,2048]{1,0:T(8,128)(2,1)S(1)} %copy-done, f32[1024,704]{0,1:T(8,128)} %fusion.8, bf16[1024,2048]{1,0:T(8,128)(2,1)} %all-gather.2.cloned.1.call-done, bf16[2048,704]{0,1:T(8,128)(2,1)} %param.17), kind=kOutput, calls=%fused_computation.10 | convolution fusion | flops 5909905408 | bytes 21233664 | tf_op jit(solution)/shard_map/dot_general | solution.py:30
  604.6 0.0 reduce-scatter.2.cloned.1.call-update
  604.6 0.0 copy-done.3
  604.6 0.1 copy.54
  604.8 0.1 reshape.91
  604.9 0.0 copy-done.6
  604.9 0.0 copy-done.7
  605.0 0.1 copy.48
  605.1 0.0 copy-done.5
  605.1 0.2 copy.49
  605.3 251.9 %all-to-all-done.1 = bf16[1,16,384,2048]{3,1,0,2:T(8,128)(2,1)} async-done(((bf16[1,16,384,2048]{3,1,0,2:T(8,128)(2,1)}), bf16[1,16,384,2048]{3,1,0,2:T(8,128)(2,1)}, u32[]{:S(2)}, u32[]{:S(2)}) %all-to-all-start.1) | async-done | bytes 25165856 | tf_op jit(solution)/shard_map/all_to_all | solution.py:47
  857.2 26.8 %copy.53 = bf16[1,16,4,96,2048]{4,3,1,2,0:T(8,128)(2,1)} copy(bf16[1,16,4,96,2048]{4,1,3,2,0:T(8,128)(2,1)} %bitcast.6) | data formatting | bytes 50331648 | tf_op jit(solution)/shard_map/all_to_all | solution.py:47
  884.0 24.1 %gather_fusion.2 = bf16[1536,2048]{1,0:T(8,128)(2,1)} fusion(bf16[6144,2048]{1,0:T(8,128)(2,1)} %bitcast.40, s32[2048]{0:T(1024)S(1)} %pad_clamp_fusion), kind=kCustom, calls=%fused_computation.2 | custom fusion | bytes 12589056 | tf_op jit(solution)/shard_map/jit(_take)/gather | solution.py:50
  908.1 11.0 %reshape.90 = bf16[256,6,2048]{2,1,0:T(8,128)(2,1)} reshape(bf16[1536,2048]{1,0:T(8,128)(2,1)} %gather_fusion.2) | data formatting | bytes 12582912 | tf_op jit(solution)/shard_map/jit(_take)/gather | solution.py:50
  919.1 11.9 %multiply_reduce_fusion = f32[256,2048]{1,0:T(8,128)} fusion(bf16[256,6,2048]{2,1,0:T(8,128)(2,1)} %reshape.90, f32[256,6]{1,0:T(8,128)S(1)} %copy.48, pred[256,6]{1,0:T(8,128)(4,1)S(1)} %copy.49), kind=kLoop, calls=%fused_computation.7 | loop fusion | flops 12058624 | bytes 8396288 | tf_op jit(solution)/shard_map/reduce_sum | solution.py:52
  931.0 0.0 reduce-scatter.2.cloned.1.call-done
  931.0 3.9 add_convert_fusion
  (8 shorter events, 0.1 us)
Async XLA Ops:
  6.5 586.0 %copy-start = (bf16[704,2048]{1,0:T(8,128)(2,1)S(1)}, bf16[704,2048]{1,0:T(8,128)(2,1)}, u32[]{:S(2)}) copy-start(bf16[704,2048]{1,0:T(8,128)(2,1)} %param.18) | copy-start | bytes 8650756
  6.5 1.2 copy-start.1
  7.7 9.3 copy-start.4
  7.7 9.3 copy-start.8
  17.6 54.6 %copy-start.2 = (s32[256,6]{0,1:T(8,128)}, s32[256,6]{0,1:T(8,128)S(1)}, u32[]{:S(2)}) copy-start(s32[256,6]{0,1:T(8,128)S(1)} %get-tuple-element.6) | copy-start | bytes 18436
  93.0 281.7 %all-to-all-start = ((bf16[4,16,96,2048]{3,2,1,0:T(8,128)(2,1)}), bf16[4,16,96,2048]{3,2,1,0:T(8,128)(2,1)}, u32[]{:S(2)}, u32[]{:S(2)}) async-start(bf16[4,16,96,2048]{3,2,1,0:T(8,128)(2,1)} %broadcast_select_fusion), calls=%async_computation.1 | async-start | bytes 50331648 | tf_op jit(solution)/shard_map/all_to_all | solution.py:40
  101.5 483.2 %all-gather.2.cloned.1.call-start = ((), (), s32[]{:S(2)}) async-start(), calls=%async_computation.3 | async-start | bytes 5242880 | tf_op jit(solution)/shard_map/all_gather | solution.py:26
  576.2 281.0 %all-to-all-start.1 = ((bf16[1,16,384,2048]{3,1,0,2:T(8,128)(2,1)}), bf16[1,16,384,2048]{3,1,0,2:T(8,128)(2,1)}, u32[]{:S(2)}, u32[]{:S(2)}) async-start(bf16[1,16,384,2048]{3,1,0,2:T(8,128)(2,1)} %copy.52), calls=%async_computation.2 | async-start | bytes 50331648 | tf_op jit(solution)/shard_map/all_to_all | solution.py:47
  584.6 346.4 %reduce-scatter.2.cloned.1.call-start = ((), (), s32[]{:S(2)}) async-start(), calls=%async_computation.4 | async-start | bytes 10485760 | tf_op jit(solution)/shard_map/reduce_scatter | solution.py:31
  592.6 12.1 %copy-start.3 = (s32[256,6]{0,1:T(8,128)S(1)}, s32[256,6]{0,1:T(8,128)}, u32[]{:S(2)}) copy-start(s32[256,6]{0,1:T(8,128)} %copy-done.2) | copy-start | bytes 18436
  592.6 12.4 %copy-start.6 = (pred[256,6]{0,1:T(8,128)(4,1)S(1)}, pred[256,6]{0,1:T(8,128)(4,1)}, u32[]{:S(2)}) copy-start(pred[256,6]{0,1:T(8,128)(4,1)} %get-tuple-element.7) | copy-start | bytes 4612
  592.6 12.4 %copy-start.7 = (f32[256,6]{0,1:T(8,128)S(1)}, f32[256,6]{0,1:T(8,128)}, u32[]{:S(2)}) copy-start(f32[256,6]{0,1:T(8,128)} %param.13) | copy-start | bytes 18436
  592.6 12.5 %copy-start.5 = (pred[256,6]{0,1:T(8,128)(4,1)S(1)}, pred[256,6]{0,1:T(8,128)(4,1)}, u32[]{:S(2)}) copy-start(pred[256,6]{0,1:T(8,128)(4,1)} %get-tuple-element.5) | copy-start | bytes 4612
Sparse Core Ops, SparseCore 0:
  103.9 83.3 all-gather.1
  604.7 146.6 reduce-scatter.1
where the time goes:
time: 943 us; the launch traced here: 942 us
  waiting for transfers between devices  525 us (56%)
  local copies, waits for them, and re-layouts  174 us (18%)
  matrix products  174 us (18%)
  other arithmetic  38.3 us (4%)
  starting transfers between devices  17.1 us (2%)
  between operations  13.7 us (1%)
    all_to_all x1, waiting for transfers between devices, layer_body(): recv_buf = lax.all_to_all(send_buf, 'ep', 0, 2, tiled=True)  273 us
    all_to_all x1, waiting for transfers between devices, layer_body(): lax.all_to_all(exp_out.reshape(1, n_local, ep_size * capacity, d_model),...  252 us
    dot_general x1, matrix products, layer_body(): jnp.einsum('erf,efd->erd', exp_hidden, expert_w2, preferred_element_type=...  94.8 us
    dot_general x1, matrix products, layer_body(): jnp.einsum('erd,edf->erf', recv_buf, expert_w1, preferred_element_type=jn...  58.9 us
    gather x1, local copies, waits for them, and re-layouts, layer_body(): send_buf = jnp.take(tokens, owner_ids, axis=0, mode='fill', fill_value=0)  47.7 us
    gather x2, local copies, waits for them, and re-layouts, layer_body(): picked = jnp.take(back_rows, dest_row, axis=0, mode='fill', fill_value=0)  35.1 us
    all_to_all x1, local copies, waits for them, and re-layouts, layer_body(): lax.all_to_all(exp_out.reshape(1, n_local, ep_size * capacity, d_model),...  26.8 us
    reshape x1, local copies, waits for them, and re-layouts, layer_body(): exp_out.reshape(1, n_local, ep_size * capacity, d_model)  26.8 us
  transfers between devices with their start and end apart: 4, of which 2 were waited for; matrix products, arithmetic and copies ran while one was open for 31% of the time, Pallas kernels for 0%

commit v1 on v0

v1 whole, which is shorter than its diff:
```python
import functools

import jax
import jax.numpy as jnp
from jax import lax
from jax.experimental import pallas as pl
from jax.experimental.pallas import tpu as pltpu
from jax.sharding import PartitionSpec as P

CAP_FACTOR = 4
GROUP = 4
N_CHUNKS = 2
VMEM_LIMIT = 66_000_000


def capacity_rows(n_tok, top_k, n_exp):
    return min(n_tok, ((CAP_FACTOR * n_tok * top_k // n_exp + 7) // 8) * 8)


def row_sizes(rows):
    return [size for size in (128, 256) if size < rows] + [rows]


def pick_rows(n_rows, rows, body):
    low = 0
    for size in row_sizes(rows):
        high = size if size < rows else rows + 1
        pl.when((n_rows > low if low else n_rows >= 0) & (n_rows <= high))(functools.partial(body, size))
        low = size


def column_pieces(width, step):
    pieces, start = [], 0
    while start < width:
        size = min(step, width - start)
        pieces.append((start, size))
        start += size
    return pieces


def up_kernel(cap, off_ref, n_ref, pick_ref, x0_ref, x1_ref, x2_ref, x3_ref, w1_ref, w3_ref, h_ref, rows_ref):
    step = pl.program_id(0)
    rows = h_ref.shape[1]
    d_model = x0_ref.shape[1]
    d_ff = w1_ref.shape[2]
    x_refs = (x0_ref, x1_ref, x2_ref, x3_ref)

    @pl.when(step % GROUP == 0)
    def _():
        for src, x_ref in enumerate(x_refs):
            chosen = pick_ref[src]
            for start, size in column_pieces(d_model, 512):
                got = jnp.dot(chosen, x_ref[:, start : start + size], preferred_element_type=jnp.float32).astype(jnp.bfloat16)
                for part in range(GROUP):
                    at = pl.multiple_of(off_ref[(step + part) * 4 + src], 16)
                    rows_ref[part, pl.ds(at, cap), start : start + size] = got[part * cap : (part + 1) * cap]

    part = step % GROUP

    def body(size):
        x = rows_ref[part, :size, :]
        full = d_ff // 256 * 256
        for start, width in column_pieces(full, 512):
            gate = jnp.dot(x, w1_ref[0, :, start : start + width], preferred_element_type=jnp.float32)
            up = jnp.dot(x, w3_ref[0, :, start : start + width], preferred_element_type=jnp.float32)
            h_ref[0, :size, start : start + width] = (jax.nn.silu(gate) * up).astype(jnp.bfloat16)
        if full < d_ff:
            tail = d_ff - full
            both = jnp.concatenate([w1_ref[0, :, full:], w3_ref[0, :, full:]], axis=1)
            pair = jnp.dot(x, both, preferred_element_type=jnp.float32)
            h_ref[0, :size, full:] = (jax.nn.silu(pair[:, :tail]) * pair[:, tail:]).astype(jnp.bfloat16)

    pick_rows(n_ref[step], rows, body)


def down_kernel(cap, off_ref, n_ref, queue_off_ref, total_ref, h_ref, w2_ref, gates_ref, own_ref, sib_ref, out_ref, queue_ref):
    step = pl.program_id(0)
    n_local = pl.num_programs(0)
    rows = h_ref.shape[1]
    width_all = w2_ref.shape[2]
    n_queue = queue_ref.shape[1]

    def body(size):
        for start, width in column_pieces(width_all, 512):
            out = jnp.dot(h_ref[0, :size, :], w2_ref[0, :, start : start + width], preferred_element_type=jnp.float32)
            out_ref[:size, start : start + width] = out.astype(jnp.bfloat16)

    pick_rows(n_ref[step], rows, body)
    for src in range(4):
        at = pl.multiple_of(off_ref[step * 4 + src], 16)
        to = pl.multiple_of(queue_off_ref[src * n_local + step], 16)
        queue_ref[src, pl.ds(to, cap), :] = out_ref[pl.ds(at, cap), :]

    @pl.when(step == n_local - 1)
    def _():
        for src in range(4):
            total = total_ref[src]
            n_tiles = (total + 255) // 256

            def clear(piece, carry):
                at = pl.multiple_of(total + piece * 16, 16)
                queue_ref[src, pl.ds(at, 16), :] = jnp.zeros((16, width_all), jnp.bfloat16)
                return carry

            lax.fori_loop(0, (n_tiles * 256 - total) // 16, clear, 0)
            into = (own_ref, sib_ref, own_ref, sib_ref)[src]
            place = src // 2
            into[place] = jnp.zeros(into.shape[1:], jnp.float32)

            def add(tile, carry):
                at = pl.multiple_of(tile * 256, 256)
                for start, width in column_pieces(width_all, 512):
                    held = queue_ref[src, pl.ds(at, 256), start : start + width]
                    new = into[place, :, start : start + width]
                    for piece in range(3):
                        new += jnp.dot(gates_ref[piece, src, :, pl.ds(at, 256)], held, preferred_element_type=jnp.float32)
                    into[place, :, start : start + width] = new
                return carry

            lax.fori_loop(0, n_tiles, add, 0)


def solution(mesh):
    ep_size = mesh.shape["ep"]
    row_spec = P(("data", "ep", "tp"), None)
    expert_spec = P("ep", None, None)
    n_rep = mesh.shape["data"] * ep_size

    def layer_body(tokens, expert_ids, gate_vals, slot_ids, send_counts, shared_w1, shared_w3, shared_w2, expert_w1, expert_w3, expert_w2):
        n_tok, d_model = tokens.shape
        top_k = expert_ids.shape[1]
        n_local, _, d_ff = expert_w1.shape
        n_exp = n_local * ep_size
        cap = capacity_rows(n_tok, top_k, n_exp)
        rows = ep_size * cap
        n_queue = n_local * cap
        me = lax.axis_index("ep")

        def swap(value, bit):
            return lax.ppermute(value, "ep", [(i, i ^ bit) for i in range(ep_size)])

        all_ids = jnp.arange(n_exp, dtype=jnp.int32)
        row_limit = jnp.sum(jnp.where(expert_ids[:, :, None] == all_ids, send_counts[0], 0), axis=-1)
        kept_mask = (slot_ids >= 0) & (slot_ids < row_limit)
        dest_row = jnp.where(kept_mask, expert_ids * cap + slot_ids, -1)
        facts = jnp.concatenate(
            [
                dest_row.astype(jnp.float32).T,
                jnp.where(kept_mask, gate_vals, 0.0).T,
                jnp.pad(send_counts.astype(jnp.float32), ((0, 0), (0, n_tok - n_exp))),
                jnp.zeros((15 - 2 * top_k, n_tok), jnp.float32),
            ],
            axis=0,
        )

        facts_sib = swap(facts, 1)
        facts_far = swap(facts, 2)
        x_far = swap(tokens, 2)
        x_sib = swap(tokens, 1)
        facts_all = jnp.stack([facts, facts_sib, facts_far, swap(facts_far, 1)])
        x_far_sib = swap(x_far, 1)

        dest_all = facts_all[:, :top_k].astype(jnp.int32) - me * n_queue
        dest_all = jnp.where((dest_all >= 0) & (dest_all < n_queue), dest_all, -1)
        gates_all = facts_all[:, top_k : 2 * top_k]
        counts_all = lax.dynamic_slice_in_dim(facts_all[:, 2 * top_k], me * n_local, n_local, 1).astype(jnp.int32)
        padded = (counts_all + 15) // 16 * 16
        off = (jnp.cumsum(padded, axis=0) - padded).T.reshape(-1)
        n_rows = jnp.sum(padded, axis=0)
        queue_off = jnp.cumsum(padded, axis=1) - padded
        total = jnp.sum(padded, axis=1)

        lanes = jnp.arange(n_queue, dtype=jnp.int32)
        pick = jnp.any(dest_all[:, :, None, :] == lanes[:, None], axis=1).astype(jnp.bfloat16)
        local = jnp.arange(n_local, dtype=jnp.int32)
        shift = jnp.sum(jnp.where((dest_all // cap)[..., None] == local, (queue_off - local * cap)[:, None, None, :], 0), axis=-1)
        queue_row = jnp.where(dest_all >= 0, dest_all + shift, -1).transpose(0, 2, 1)
        high = lax.reduce_precision(gates_all, 8, 7)
        middle = lax.reduce_precision(gates_all - high, 8, 7)
        low = lax.reduce_precision(gates_all - high - middle, 8, 7)
        pieces = jnp.stack([high, middle, low]).transpose(0, 1, 3, 2)
        gate_rows = jnp.sum(
            jnp.where(queue_row[..., None] == lanes, pieces[..., None], 0.0), axis=3
        ).astype(jnp.bfloat16)

        whole = dict(pipeline_mode=pl.Buffered(1))
        hidden = pl.pallas_call(
            functools.partial(up_kernel, cap),
            grid_spec=pltpu.PrefetchScalarGridSpec(
                num_scalar_prefetch=2,
                grid=(n_local,),
                in_specs=[
                    pl.BlockSpec((4, GROUP * cap, n_tok), lambda e, *_: (0, e // GROUP, 0)),
                    *[pl.BlockSpec((n_tok, d_model), lambda e, *_: (0, 0), **whole) for _ in range(4)],
                    pl.BlockSpec((1, d_model, d_ff), lambda e, *_: (e, 0, 0)),
                    pl.BlockSpec((1, d_model, d_ff), lambda e, *_: (e, 0, 0)),
                ],
                out_specs=pl.BlockSpec((1, rows, d_ff), lambda e, *_: (e, 0, 0)),
                scratch_shapes=[pltpu.VMEM((GROUP, rows, d_model), jnp.bfloat16)],
            ),
            out_shape=jax.ShapeDtypeStruct((n_local, rows, d_ff), jnp.bfloat16),
            compiler_params=pltpu.CompilerParams(dimension_semantics=("arbitrary",), vmem_limit_bytes=VMEM_LIMIT),
            cost_estimate=pl.CostEstimate(flops=4 * n_local * 192 * d_model * d_ff, bytes_accessed=4 * n_local * d_model * d_ff, transcendentals=0),
            name="experts_up",
        )(off, n_rows, pick, tokens, x_sib, x_far, x_far_sib, expert_w1, expert_w3)

        gathered = lax.all_gather(tokens, "tp", axis=0, tiled=True)
        gathered, hidden = lax.optimization_barrier((gathered, hidden))
        pre_gate = jnp.dot(gathered, shared_w1, preferred_element_type=jnp.float32)
        pre_up = jnp.dot(gathered, shared_w3, preferred_element_type=jnp.float32)
        shared_hidden = (jax.nn.silu(pre_gate) * pre_up).astype(jnp.bfloat16)
        shared_hidden, hidden = lax.optimization_barrier((shared_hidden, hidden))
        hidden_blocks = lax.all_to_all(shared_hidden.reshape(mesh.shape["tp"], n_tok, -1), "tp", 0, 0)

        width = shared_w2.shape[0]
        rep = lax.axis_index("data") * ep_size + me
        w2_part = lax.dynamic_slice_in_dim(shared_w2, rep * (width // n_rep), width // n_rep, 0)
        w2_all = lax.all_gather(w2_part, ("tp", "data", "ep"), axis=0, tiled=True)

        n_cols = d_model // N_CHUNKS
        routed = []
        for chunk in range(N_CHUNKS):
            sums_own, sums_sib = pl.pallas_call(
                functools.partial(down_kernel, cap),
                grid_spec=pltpu.PrefetchScalarGridSpec(
                    num_scalar_prefetch=4,
                    grid=(n_local,),
                    in_specs=[
                        pl.BlockSpec((1, rows, d_ff), lambda e, *_: (e, 0, 0)),
                        pl.BlockSpec((1, d_ff, n_cols), functools.partial(lambda c, e, *_: (e, 0, c), chunk)),
                        pl.BlockSpec((3, 4, n_tok, n_queue), lambda e, *_: (0, 0, 0, 0), **whole),
                    ],
                    out_specs=[pl.BlockSpec((2, n_tok, n_cols), lambda e, *_: (0, 0, 0), **whole) for _ in range(2)],
                    scratch_shapes=[pltpu.VMEM((rows, n_cols), jnp.bfloat16), pltpu.VMEM((4, n_queue, n_cols), jnp.bfloat16)],
                ),
                out_shape=[jax.ShapeDtypeStruct((2, n_tok, n_cols), jnp.float32) for _ in range(2)],
                compiler_params=pltpu.CompilerParams(dimension_semantics=("arbitrary",), vmem_limit_bytes=VMEM_LIMIT),
                cost_estimate=pl.CostEstimate(flops=2 * n_local * 192 * n_cols * d_ff, bytes_accessed=2 * n_local * n_cols * d_ff, transcendentals=0),
                name=f"experts_down_{chunk}",
            )(off, n_rows, queue_off.reshape(-1), total, hidden, expert_w2, gate_rows)
            from_sib = swap(sums_sib, 1)
            from_far = swap(sums_own[1] + from_sib[1], 2)
            routed.append(sums_own[0] + from_sib[0] + from_far)
        routed_sum = jnp.concatenate(routed, axis=1)

        w2_blocks = w2_all.reshape(mesh.shape["tp"], width, d_model)
        shared_out = jnp.dot(hidden_blocks[0], w2_blocks[0], preferred_element_type=jnp.float32)
        for block in range(1, mesh.shape["tp"]):
            shared_out += jnp.dot(hidden_blocks[block], w2_blocks[block], preferred_element_type=jnp.float32)
        return (tokens.astype(jnp.float32) + shared_out + routed_sum).astype(jnp.bfloat16)

    return jax.shard_map(
        layer_body,
        mesh=mesh,
        in_specs=(row_spec, row_spec, row_spec, row_spec, row_spec, P(None, "tp"), P(None, "tp"), P("tp", None), expert_spec, expert_spec, expert_spec),
        out_specs=row_spec,
        check_vma=False,
    )
```

time: 943 us -> 335 us (0.36)
  waiting for transfers between devices: 525 us -> 59.4 us
  local copies, waits for them, and re-layouts: 174 us -> 7.61 us
  matrix products: 174 us -> 19.9 us
  Pallas kernels: 0 us -> 143 us
  other arithmetic: 38.3 us -> 54.3 us
  starting transfers between devices: 17.1 us -> 32.5 us
    all_to_all x2 -> x1, waiting for transfers between devices: 524 us -> 0.01 us  [layer_body(): lax.all_to_all(shared_hidden.reshape(mesh.shape['tp'], n_tok, -1), 'tp',...]
    dot_general x3 -> x5, matrix products: 166 us -> 13.9 us  [the longest x3 6 us: layer_body(): jnp.dot(hidden_blocks[block], w2_blocks[block], preferred_element_type=jn...]
    pallas_call x0 -> x3, Pallas kernels: none -> 143 us  [the longest x2 71.8 us: layer_body(): pl.pallas_call(functools.partial(down_kernel, cap), grid_spec=pltpu.Prefe...]
    gather x6 -> x0, local copies, waits for them, and re-layouts: 92.1 us -> none  [the longest x1 47.7 us: layer_body(): send_buf = jnp.take(tokens, owner_ids, axis=0, mode='fill', fill_value=0)]
    ppermute x0 -> x10, waiting for transfers between devices: none -> 58.7 us  [swap(): return lax.ppermute(value, 'ep', [(i, i ^ bit) for i in range(ep_size)])]
    all_to_all x2 -> x0, local copies, waits for them, and re-layouts: 47.8 us -> none  [the longest x1 26.8 us: layer_body(): lax.all_to_all(exp_out.reshape(1, n_local, ep_size * capacity, d_model),...]
    ppermute x0 -> x10, starting transfers between devices: none -> 27.5 us  [swap(): return lax.ppermute(value, 'ep', [(i, i ^ bit) for i in range(ep_size)])]
    reshape x3 -> x2, local copies, waits for them, and re-layouts: 27.1 us -> 3.16 us  [the longest x1 2.56 us: layer_body(): shared_hidden.reshape(mesh.shape['tp'], n_tok, -1)]
  transfers between devices with their start and end apart: 4 -> 13, of which waited for: 2 -> 5; matrix products, arithmetic and copies ran while one was open for 31% -> 21% of each run, Pallas kernels for 0% -> 43%
where the time goes in v1:
time: 335 us; the launch traced here: 330 us
  Pallas kernels  143 us (43%)
  waiting for transfers between devices  59.4 us (18%)
  other arithmetic  54.3 us (16%)
  starting transfers between devices  32.5 us (10%)
  matrix products  19.9 us (6%)
  between operations  14 us (4%)
  local copies, waits for them, and re-layouts  7.61 us (2%)
    pallas_call x2, Pallas kernels, layer_body(): pl.pallas_call(functools.partial(down_kernel, cap), grid_spec=pltpu.Prefe...  71.8 us
    pallas_call x1, Pallas kernels, layer_body(): pl.pallas_call(functools.partial(up_kernel, cap), grid_spec=pltpu.Prefetc...  70.7 us
    ppermute x10, waiting for transfers between devices, swap(): return lax.ppermute(value, 'ep', [(i, i ^ bit) for i in range(ep_size)])  58.7 us
    ppermute x10, starting transfers between devices, swap(): return lax.ppermute(value, 'ep', [(i, i ^ bit) for i in range(ep_size)])  27.5 us
    reduce_sum x1, other arithmetic, layer_body(): jnp.sum(jnp.where(queue_row[..., None] == lanes, pieces[..., None], 0.0),...  24.4 us
    reduce_or x1, other arithmetic, layer_body(): jnp.any(dest_all[:, :, None, :] == lanes[:, None], axis=1)  8.24 us
  transfers between devices with their start and end apart: 13, of which 5 were waited for; matrix products, arithmetic and copies ran while one was open for 21% of the time, Pallas kernels for 43%

profile of v1, /device:TPU:0, one launch (start us, length us, event | category | flops | bytes accessed | tf_op | source)
XLA Modules:
  0.0 330.4 jit_solution(17181447806723542711)
XLA Ops:
  6.5 0.7 all-gather.3.cloned.1.call-update
  7.3 0.0 all-gather.5.cloned.1.call-start
  7.3 1.8 constant_dynamic-slice_fusion
  9.1 0.0 all-gather.5.cloned.1.call-update
  9.1 0.7 convert_element_type.38
  9.7 0.1 pad.17.clone
  9.8 0.8 select_reduce_fusion.2
  10.7 0.7 convert_bitcast_fusion
  11.4 0.7 select_bitcast_fusion.1
  12.1 0.1 fusion.34
  12.2 3.0 collective-permute-start.1
  15.2 0.0 collective-permute-start
  15.2 0.5 collective-permute-start.3
  15.7 0.1 collective-permute-start.4
  15.8 0.1 fusion.50
  15.9 1.1 collective-permute-done.1
  16.9 0.0 collective-permute-start.2
  16.9 0.0 collective-permute-done
  16.9 1.2 collective-permute-done.2
  18.1 0.5 broadcast.104
  18.6 0.7 fusion.43
  19.4 0.7 fusion.42
  20.1 0.2 reduce_window_sum.25
  20.3 0.2 select_reduce_fusion.1
  20.5 5.8 %iota_compare_fusion = pred[4,256,6,1536]{3,1,2,0:T(8,128)(4,1)S(1)} fusion(s32[4,256,6]{1,2,0:T(8,128)S(1)} %select_bitcast_fusion), kind=kLoop, calls=%fused_computation.1 | loop fusion | flops 9437184 | bytes 9461760 | tf_op jit(solution)/shard_map/eq | solution.py:183
  26.4 14.4 %collective-permute-done.4.x2_ref = bf16[256,2048]{1,0:T(8,128)(2,1)S(1)} collective-permute-done((bf16[256,2048]{1,0:T(8,128)(2,1)}, bf16[256,2048]{1,0:T(8,128)(2,1)S(1)}, u32[]{:S(2)}, u32[]{:S(2)}) %collective-permute-start.4) | collective-permute-done | bytes 1048608 | tf_op jit(solution)/shard_map/ppermute | solution.py:140
  40.8 0.0 collective-permute-start.5
  40.8 24.4 %select_reduce_fusion.gates_ref = bf16[3,4,256,1536]{3,2,1,0:T(8,128)(2,1)} fusion(f32[3,4,256,6]{2,3,1,0:T(8,128)S(1)} %maximum_bitcast_fusion, pred[4,256,6,1536]{3,1,2,0:T(8,128)(4,1)S(1)} %iota_compare_fusion), kind=kLoop, calls=%fused_computation | loop fusion | flops 51904512 | bytes 18948096 | tf_op jit(solution)/shard_map/reduce_sum | solution.py:182
  65.2 0.1 reduce_window_sum.26
  65.3 0.1 copy.21
  65.3 0.6 reshape.76.off_ref
  65.9 0.1 add.107
  66.0 8.2 %fusion = pred[4,1536,256]{2,1,0:T(8,128)(4,1)S(1)} fusion(s32[4,6,256]{2,1,0:T(8,128)S(1)} %get-tuple-element.24), kind=kLoop, calls=%fused_computation.3 | loop fusion | flops 17301504 | bytes 1597440 | tf_op jit(solution)/shard_map/reduce_or | solution.py:174
  74.3 2.2 convert_element_type.41.pick_ref
  76.5 0.5 multiply_subtract_fusion.queue_off_ref
  77.0 0.0 collective-permute-done.3.x1_ref
  77.0 0.0 collective-permute-done.5.x3_ref
  77.0 1.0 copy-done.5
  78.0 70.7 %experts_up.1.h_ref = bf16[16,384,1408]{2,1,0:T(8,128)(2,1)} custom-call(s32[64]{0:T(128)} %reshape.76.off_ref, s32[16]{0:T(128)} %get-tuple-element.22.n_ref, bf16[4,1536,256]{2,1,0:T(8,128)(2,1)} %convert_element_type.41.pick_ref, bf16[256,2048]{1,0:T(8,128)(2,1)} %x0_ref.1, bf16[256,2048]{1,0:T(8,128)(2,1)} %collective-permute-done.3.x1_ref, ...), custom_call_target="tpu_custom_call" | custom-call | flops 35433480192 | bytes 184549376 | tf_op jit(solution)/shard_map/experts_up/pallas_call | solution.py:187
  148.8 6.0 %fusion.45 = f32[1024,704]{0,1:T(8,128)S(1)} fusion(bf16[1024,2048]{1,0:T(8,128)(2,1)} %all-gather.3.cloned.1.call-done, bf16[2048,704]{0,1:T(8,128)(2,1)} %param.16), kind=kOutput, calls=%fused_computation.89 | convolution fusion | flops 2952790016 | bytes 9961472 | tf_op jit(solution)/shard_map/dot_general | solution.py:209
  154.8 4.4 %multiply_convert_fusion = bf16[1024,704]{0,1:T(8,128)(2,1)} fusion(f32[1024,704]{0,1:T(8,128)S(1)} %fusion.45, bf16[1024,2048]{1,0:T(8,128)(2,1)S(1)} %copy-done.8, bf16[2048,704]{0,1:T(8,128)(2,1)S(1)} %copy-done.9), kind=kOutput, calls=%fused_computation.12 | convolution fusion | flops 2957115392 | bytes 11403264 | tf_op jit(solution)/shard_map/dot_general | solution.py:210
  159.3 36.0 %experts_down_1.1 = (f32[2,256,1024]{2,1,0:T(8,128)}, f32[2,256,1024]{2,1,0:T(8,128)}) custom-call(s32[64]{0:T(128)} %reshape.76.off_ref, s32[16]{0:T(128)} %get-tuple-element.22.n_ref, s32[64]{0:T(128)} %multiply_subtract_fusion.queue_off_ref, s32[4]{0:T(128)} %get-tuple-element.21.total_ref, bf16[16,384,1408]{2,1,0:T(8,128)(2,1)} %experts_up.1.h_ref, ...), custom_call_target="tpu_custom_call" | custom-call | flops 8858370048 | bytes 46137344 | tf_op jit(solution)/shard_map/experts_down_1/pallas_call | solution.py:223
  195.3 0.5 collective-permute-start.8
  195.7 35.8 %experts_down_0.1 = (f32[2,256,1024]{2,1,0:T(8,128)}, f32[2,256,1024]{2,1,0:T(8,128)}) custom-call(s32[64]{0:T(128)} %reshape.76.off_ref, s32[16]{0:T(128)} %get-tuple-element.22.n_ref, s32[64]{0:T(128)} %multiply_subtract_fusion.queue_off_ref, s32[4]{0:T(128)} %get-tuple-element.21.total_ref, bf16[16,384,1408]{2,1,0:T(8,128)(2,1)} %experts_up.1.h_ref, ...), custom_call_target="tpu_custom_call" | custom-call | flops 8858370048 | bytes 46137344 | tf_op jit(solution)/shard_map/experts_down_0/pallas_call | solution.py:223
  231.6 0.0 collective-permute-start.6
  231.6 2.6 copy.25
  234.1 4.9 %all-to-all-start = ((bf16[4,256,704]{1,2,0:T(8,128)(2,1)}), bf16[4,256,704]{1,2,0:T(8,128)(2,1)S(1)}, u32[]{:S(2)}, u32[]{:S(2)}) async-start(bf16[4,256,704]{1,2,0:T(8,128)(2,1)} %bitcast.54), calls=%async_computation | async-start | bytes 2883584 | tf_op jit(solution)/shard_map/all_to_all | solution.py:213
  239.1 1.8 fusion.24
  240.9 23.3 %collective-permute-start.9 = (f32[256,1024]{1,0:T(8,128)S(1)}, f32[256,1024]{1,0:T(8,128)S(1)}, u32[]{:S(2)}, u32[]{:S(2)}) collective-permute-start(f32[256,1024]{1,0:T(8,128)S(1)} %fusion.24), channel_id=1, source_target_pairs={{0,2},{1,3},{2,0},{3,1},{4,6},{5,7},{6,4},{7,5},{8,10},{9,11},{10,... | collective-permute-start | bytes 3145736 | tf_op jit(solution)/shard_map/ppermute | solution.py:140
  264.3 1.4 fusion.27
  265.6 0.1 collective-permute-start.7
  265.7 22.5 %collective-permute-done.9 = f32[256,1024]{1,0:T(8,128)S(1)} collective-permute-done((f32[256,1024]{1,0:T(8,128)S(1)}, f32[256,1024]{1,0:T(8,128)S(1)}, u32[]{:S(2)}, u32[]{:S(2)}) %collective-permute-start.9) | collective-permute-done | bytes 1048608 | tf_op jit(solution)/shard_map/ppermute | solution.py:140
  288.3 2.5 fusion.26
  290.7 19.5 %collective-permute-done.7 = f32[256,1024]{1,0:T(8,128)S(1)} collective-permute-done((f32[256,1024]{1,0:T(8,128)S(1)}, f32[256,1024]{1,0:T(8,128)S(1)}, u32[]{:S(2)}, u32[]{:S(2)}) %collective-permute-start.7) | collective-permute-done | bytes 1048608 | tf_op jit(solution)/shard_map/ppermute | solution.py:140
  310.3 2.5 fusion.29
  312.8 3.0 fusion.5
  315.7 3.5 %fusion.9 = f32[256,2048]{1,0:T(8,128)S(1)} fusion(f32[256,2048]{1,0:T(8,128)S(1)} %fusion.5, bf16[2816,2048]{1,0:T(8,128)(2,1)} %all-gather.5.cloned.1.call-done, bf16[4,256,704]{1,2,0:T(8,128)(2,1)S(1)} %all-to-all-done), kind=kOutput, calls=%fused_computation.13 | convolution fusion | flops 738721792 | bytes 7438336 | tf_op jit(solution)/shard_map/dot_general | solution.py:247
  319.2 0.0 copy-start.1
  319.2 0.0 copy-start.6
  319.3 1.0 fusion.12
  320.3 0.2 copy-done.1
  320.5 0.3 copy-done.6
  320.8 0.3 copy-done.7
  321.1 2.0 fusion.21
  (29 shorter events, 0.2 us)
Async XLA Ops:
  6.5 142.2 %all-gather.3.cloned.1.call-start = ((), (), s32[]{:S(2)}) async-start(), calls=%async_computation.1 | async-start | bytes 5242880 | tf_op jit(solution)/shard_map/all_gather | solution.py:207
  7.3 305.5 %all-gather.5.cloned.1.call-start = ((), (), s32[]{:S(2)}) async-start(), calls=%async_computation.2 | async-start | bytes 11894784 | tf_op jit(solution)/shard_map/all_gather | solution.py:218
  12.2 4.8 %collective-permute-start.1 = (f32[16,256]{1,0:T(8,128)S(1)}, f32[16,256]{1,0:T(8,128)S(1)}, u32[]{:S(2)}, u32[]{:S(2)}) collective-permute-start(f32[16,256]{1,0:T(8,128)S(1)} %fusion.34), channel_id=1, source_target_pairs={{0,2},{1,3},{2,0},{3,1},{4,6},{5,7},{6,4},{7,5},{8,10},{9,11},{10,... | collective-permute-start | bytes 49160 | tf_op jit(solution)/shard_map/ppermute | solution.py:140
  15.2 1.7 collective-permute-start
  15.2 61.8 %collective-permute-start.3 = (bf16[256,2048]{1,0:T(8,128)(2,1)}, bf16[256,2048]{1,0:T(8,128)(2,1)}, u32[]{:S(2)}, u32[]{:S(2)}) collective-permute-start(bf16[256,2048]{1,0:T(8,128)(2,1)} %x0_ref.1), channel_id=1, source_target_pairs={{0,1},{1,0},{2,3},{3,2},{4,5},{5,4},{6,7},{7,6},{8,9},{9,8},{10,11... | collective-permute-start | bytes 3145736 | tf_op jit(solution)/shard_map/ppermute | solution.py:140
  15.7 25.1 %collective-permute-start.4 = (bf16[256,2048]{1,0:T(8,128)(2,1)}, bf16[256,2048]{1,0:T(8,128)(2,1)S(1)}, u32[]{:S(2)}, u32[]{:S(2)}) collective-permute-start(bf16[256,2048]{1,0:T(8,128)(2,1)} %x0_ref.1), channel_id=1, source_target_pairs={{0,2},{1,3},{2,0},{3,1},{4,6},{5,7},{6,4},{7,5},{8,10},{9,11},{10,... | collective-permute-start | bytes 3145736 | tf_op jit(solution)/shard_map/ppermute | solution.py:140
  16.9 1.2 collective-permute-start.2
  40.8 24.4 %copy-start.4 = (bf16[256,2048]{1,0:T(8,128)(2,1)}, bf16[256,2048]{1,0:T(8,128)(2,1)S(1)}, u32[]{:S(2)}) copy-start(bf16[256,2048]{1,0:T(8,128)(2,1)S(1)} %collective-permute-done.4.x2_ref) | copy-start | bytes 3145732
  40.8 36.2 %collective-permute-start.5 = (bf16[256,2048]{1,0:T(8,128)(2,1)S(1)}, bf16[256,2048]{1,0:T(8,128)(2,1)S(1)}, u32[]{:S(2)}, u32[]{:S(2)}) collective-permute-start(bf16[256,2048]{1,0:T(8,128)(2,1)S(1)} %collective-permute-done.4.x2_ref), channel_id=1, source_target_pairs={{0,1},{1,0},{2,3},{3,2},{4,5},{5,4},{6,7},{7,6},{8,9},{9,8},{10,11... | collective-permute-start | bytes 3145736 | tf_op jit(solution)/shard_map/ppermute | solution.py:140
  77.0 1.0 copy-start.5
  148.8 6.0 %copy-start.9 = (bf16[2048,704]{0,1:T(8,128)(2,1)S(1)}, bf16[2048,704]{0,1:T(8,128)(2,1)}, u32[]{:S(2)}) copy-start(bf16[2048,704]{0,1:T(8,128)(2,1)} %param.17) | copy-start | bytes 8650756
  148.8 6.0 %copy-start.8 = (bf16[1024,2048]{1,0:T(8,128)(2,1)S(1)}, bf16[1024,2048]{1,0:T(8,128)(2,1)}, u32[]{:S(2)}) copy-start(bf16[1024,2048]{1,0:T(8,128)(2,1)} %all-gather.3.cloned.1.call-done) | copy-start | bytes 12582916
  195.3 43.8 %collective-permute-start.8 = (f32[2,256,1024]{2,1,0:T(8,128)}, f32[2,256,1024]{2,1,0:T(8,128)}, u32[]{:S(2)}, u32[]{:S(2)}) collective-permute-start(f32[2,256,1024]{2,1,0:T(8,128)} %get-tuple-element.20), channel_id=1, source_target_pairs={{0,1},{1,0},{2,3},{3,2},{4,5},{5,4},{6,7},{7,6},{8,9},{9,8},{10,11... | collective-permute-start | bytes 6291464 | tf_op jit(solution)/shard_map/ppermute | solution.py:140
  231.6 32.7 %collective-permute-start.6 = (f32[2,256,1024]{2,1,0:T(8,128)}, f32[2,256,1024]{2,1,0:T(8,128)}, u32[]{:S(2)}, u32[]{:S(2)}) collective-permute-start(f32[2,256,1024]{2,1,0:T(8,128)} %get-tuple-element.18), channel_id=1, source_target_pairs={{0,1},{1,0},{2,3},{3,2},{4,5},{5,4},{6,7},{7,6},{8,9},{9,8},{10,11... | collective-permute-start | bytes 6291464 | tf_op jit(solution)/shard_map/ppermute | solution.py:140
  234.1 30.1 %copy-start.2 = (f32[2,256,1024]{2,1,0:T(8,128)S(1)}, f32[2,256,1024]{2,1,0:T(8,128)}, u32[]{:S(2)}) copy-start(f32[2,256,1024]{2,1,0:T(8,128)} %get-tuple-element.17) | copy-start | bytes 6291460
  234.1 78.6 %all-to-all-start = ((bf16[4,256,704]{1,2,0:T(8,128)(2,1)}), bf16[4,256,704]{1,2,0:T(8,128)(2,1)S(1)}, u32[]{:S(2)}, u32[]{:S(2)}) async-start(bf16[4,256,704]{1,2,0:T(8,128)(2,1)} %bitcast.54), calls=%async_computation | async-start | bytes 2883584 | tf_op jit(solution)/shard_map/all_to_all | solution.py:213
  239.1 49.2 %copy-start.3 = (f32[2,256,1024]{2,1,0:T(8,128)S(1)}, f32[2,256,1024]{2,1,0:T(8,128)}, u32[]{:S(2)}) copy-start(f32[2,256,1024]{2,1,0:T(8,128)} %get-tuple-element.19) | copy-start | bytes 6291460
  240.9 47.3 %collective-permute-start.9 = (f32[256,1024]{1,0:T(8,128)S(1)}, f32[256,1024]{1,0:T(8,128)S(1)}, u32[]{:S(2)}, u32[]{:S(2)}) collective-permute-start(f32[256,1024]{1,0:T(8,128)S(1)} %fusion.24), channel_id=1, source_target_pairs={{0,2},{1,3},{2,0},{3,1},{4,6},{5,7},{6,4},{7,5},{8,10},{9,11},{10,... | collective-permute-start | bytes 3145736 | tf_op jit(solution)/shard_map/ppermute | solution.py:140
  265.6 44.6 %collective-permute-start.7 = (f32[256,1024]{1,0:T(8,128)S(1)}, f32[256,1024]{1,0:T(8,128)S(1)}, u32[]{:S(2)}, u32[]{:S(2)}) collective-permute-start(f32[256,1024]{1,0:T(8,128)S(1)} %fusion.27), channel_id=1, source_target_pairs={{0,2},{1,3},{2,0},{3,1},{4,6},{5,7},{6,4},{7,5},{8,10},{9,11},{10,... | collective-permute-start | bytes 3145736 | tf_op jit(solution)/shard_map/ppermute | solution.py:140
  312.8 6.4 %copy-start = (bf16[2816,2048]{1,0:T(8,128)(2,1)S(1)}, bf16[2816,2048]{1,0:T(8,128)(2,1)}, u32[]{:S(2)}) copy-start(bf16[2816,2048]{1,0:T(8,128)(2,1)} %all-gather.5.cloned.1.call-done) | copy-start | bytes 34603012
  319.2 1.2 copy-start.1
  319.2 1.5 copy-start.6
  319.2 1.8 copy-start.7
Sparse Core Ops, SparseCore 0:
  8.9 82.9 all-gather.2
  94.7 89.3 all-gather.4

commit v2 on v1

v2 whole, which is shorter than its diff:
```python
import functools

import jax
import jax.numpy as jnp
from jax import lax
from jax.experimental import pallas as pl
from jax.experimental.pallas import tpu as pltpu
from jax.sharding import PartitionSpec as P


CAP_FACTOR = 4
GROUP = 4
COLUMN_CHUNKS = 2
ROW_PIECE = 128
UP_SLOTS = 3
DOWN_SLOTS = 4
VMEM_LIMIT = 66_000_000


def capacity_rows(n_tok, top_k, n_exp):
    return min(n_tok, ((CAP_FACTOR * n_tok * top_k // n_exp + 7) // 8) * 8)


def row_sizes(rows):
    return [size for size in (128, 256) if size < rows] + [rows]


def pick_rows(n_rows, rows, body):
    low = 0
    for size in row_sizes(rows):
        high = size if size < rows else rows + 1
        pl.when((n_rows > low if low else n_rows >= 0) & (n_rows <= high))(functools.partial(body, size))
        low = size


def column_pieces(width, step):
    pieces, start = [], 0
    while start < width:
        size = min(step, width - start)
        pieces.append((start, size))
        start += size
    return pieces


def prep_kernel(facts_ref, gates_in_ref, pick_ref, gates_ref):
    top_k = gates_in_ref.shape[2]
    n_tok = pick_ref.shape[2]
    step_rows = 32

    def fill(block, carry):
        at = pl.multiple_of(block * step_rows, step_rows)
        row = lax.broadcasted_iota(jnp.int32, (step_rows, n_tok), 0) + at
        chosen = jnp.zeros((step_rows, n_tok), jnp.float32)
        for j in range(top_k):
            chosen = jnp.where(facts_ref[0, j : j + 1, :] == row, 1.0, chosen)
        pick_ref[0, pl.ds(at, step_rows), :] = chosen.astype(jnp.bfloat16)
        return carry

    lax.fori_loop(0, pick_ref.shape[1] // step_rows, fill, 0)

    def tile(index, carry):
        row = lax.broadcasted_iota(jnp.int32, (256, n_tok), 0) + index * 256
        for piece in range(3):
            weight = jnp.zeros((256, n_tok), jnp.float32)
            for j in range(top_k):
                weight = jnp.where(facts_ref[0, 8 + j : 9 + j, :] == row, gates_in_ref[piece, 0, j : j + 1, :], weight)
            gates_ref[index, piece] = weight.astype(jnp.bfloat16).T
        return carry

    lax.fori_loop(0, gates_ref.shape[0], tile, 0)


def up_kernel(cap, off_ref, n_ref, at1_ref, at2_ref, pick_ref, x0_ref, x1_ref, x2_ref, x3_ref, w1_hbm, w3_hbm, h0_ref, h1_ref, h2_ref, rows_ref, w1_ring, w3_ring, sems):
    step = pl.program_id(0)
    n_steps = pl.num_programs(0)
    d_model = x0_ref.shape[1]
    d_ff = w1_ring.shape[2]
    n_slots = w1_ring.shape[0]
    x_refs = (x0_ref, x1_ref, x2_ref, x3_ref)
    h_refs = (h0_ref, h1_ref, h2_ref)

    def fetch(expert):
        slot = expert % n_slots
        return (
            pltpu.make_async_copy(w1_hbm.at[expert], w1_ring.at[slot], sems.at[0, slot]),
            pltpu.make_async_copy(w3_hbm.at[expert], w3_ring.at[slot], sems.at[1, slot]),
        )

    def start(expert):
        for copy in fetch(expert):
            copy.start()

    @pl.when(step == 0)
    def _():
        for expert in range(n_slots - 1):
            start(expert)

    @pl.when(step + n_slots - 1 < n_steps)
    def _():
        start(step + n_slots - 1)

    @pl.when(step % GROUP == 0)
    def _():
        for src, x_ref in enumerate(x_refs):
            chosen = pick_ref[src]
            for begin, size in column_pieces(d_model, 512):
                got = jnp.dot(chosen, x_ref[:, begin : begin + size], preferred_element_type=jnp.float32).astype(jnp.bfloat16)
                for part in range(GROUP):
                    at = pl.multiple_of(off_ref[(step + part) * 4 + src], 16)
                    rows_ref[part, pl.ds(at, cap), begin : begin + size] = got[part * cap : (part + 1) * cap]

    part = step % GROUP
    slot = step % n_slots
    for copy in fetch(step):
        copy.wait()

    def body(size):
        x = rows_ref[part, :size, :]

        def put(value, begin, width):
            for piece in range(size // ROW_PIECE):
                h_refs[piece][0, :, begin : begin + width] = value[piece * ROW_PIECE : (piece + 1) * ROW_PIECE]

        full = d_ff // 256 * 256
        for begin, width in column_pieces(full, 512):
            gate = jnp.dot(x, w1_ring[slot, :, begin : begin + width], preferred_element_type=jnp.float32)
            up = jnp.dot(x, w3_ring[slot, :, begin : begin + width], preferred_element_type=jnp.float32)
            put((jax.nn.silu(gate) * up).astype(jnp.bfloat16), begin, width)
        if full < d_ff:
            tail = d_ff - full
            both = jnp.concatenate([w1_ring[slot, :, full:], w3_ring[slot, :, full:]], axis=1)
            pair = jnp.dot(x, both, preferred_element_type=jnp.float32)
            put((jax.nn.silu(pair[:, :tail]) * pair[:, tail:]).astype(jnp.bfloat16), full, tail)

    pick_rows(n_ref[step], rows_ref.shape[1], body)


def down_kernel(cap, first, off_ref, n_ref, queue_off_ref, total_ref, at1_ref, at2_ref, h0_ref, h1_ref, h2_ref, w2_hbm, gates_hbm, own_ref, sib_ref, out_ref, queue_ref, w2_ring, gates_ref, w_sems, gate_sems):
    step = pl.program_id(0)
    n_local = pl.num_programs(0)
    n_slots, _, width_all = w2_ring.shape
    n_tiles_max = gates_ref.shape[0] // 4
    h_refs = (h0_ref, h1_ref, h2_ref)

    def fetch(expert):
        slot = expert % n_slots
        return pltpu.make_async_copy(w2_hbm.at[expert, :, first : first + width_all], w2_ring.at[slot], w_sems.at[slot])

    def gate_copies(act):
        for src in range(4):
            for tile in range(n_tiles_max):
                index = src * n_tiles_max + tile
                copy = pltpu.make_async_copy(gates_hbm.at[index], gates_ref.at[index], gate_sems.at[index])
                pl.when(tile * 256 < total_ref[src])(functools.partial(act, copy))

    @pl.when(step == 0)
    def _():
        for expert in range(n_slots - 1):
            fetch(expert).start()
        gate_copies(lambda copy: copy.start())

    @pl.when(step + n_slots - 1 < n_local)
    def _():
        fetch(step + n_slots - 1).start()

    fetch(step).wait()
    slot = step % n_slots

    def body(size):
        h = jnp.concatenate([h_refs[piece][0] for piece in range(size // ROW_PIECE)], axis=0)
        for begin, width in column_pieces(width_all, 512):
            out = jnp.dot(h, w2_ring[slot, :, begin : begin + width], preferred_element_type=jnp.float32)
            out_ref[:size, begin : begin + width] = out.astype(jnp.bfloat16)

    pick_rows(n_ref[step], out_ref.shape[0], body)
    for src in range(4):
        at = pl.multiple_of(off_ref[step * 4 + src], 16)
        to = pl.multiple_of(queue_off_ref[src * n_local + step], 16)
        queue_ref[src, pl.ds(to, cap), :] = out_ref[pl.ds(at, cap), :]

    @pl.when(step == n_local - 1)
    def _():
        gate_copies(lambda copy: copy.wait())
        for src in range(4):
            total = total_ref[src]
            n_tiles = (total + 255) // 256

            def clear(piece, carry):
                at = pl.multiple_of(total + piece * 16, 16)
                queue_ref[src, pl.ds(at, 16), :] = jnp.zeros((16, width_all), jnp.bfloat16)
                return carry

            lax.fori_loop(0, (n_tiles * 256 - total) // 16, clear, 0)
            into = (own_ref, sib_ref, own_ref, sib_ref)[src]
            place = src // 2
            into[place] = jnp.zeros(into.shape[1:], jnp.float32)

            def add(tile, carry):
                at = pl.multiple_of(tile * 256, 256)
                for begin, width in column_pieces(width_all, 512):
                    held = queue_ref[src, pl.ds(at, 256), begin : begin + width]
                    new = into[place, :, begin : begin + width]
                    for piece in range(3):
                        new += jnp.dot(gates_ref[src * n_tiles_max + tile, piece], held, preferred_element_type=jnp.float32)
                    into[place, :, begin : begin + width] = new
                return carry

            lax.fori_loop(0, n_tiles, add, 0)


def solution(mesh):
    ep_size = mesh.shape["ep"]
    row_spec = P(("data", "ep", "tp"), None)
    expert_spec = P("ep", None, None)
    n_rep = mesh.shape["data"] * ep_size

    def layer_body(tokens, expert_ids, gate_vals, slot_ids, send_counts, shared_w1, shared_w3, shared_w2, expert_w1, expert_w3, expert_w2):
        n_tok, d_model = tokens.shape
        top_k = expert_ids.shape[1]
        n_local, _, d_ff = expert_w1.shape
        n_exp = n_local * ep_size
        cap = capacity_rows(n_tok, top_k, n_exp)
        rows = ep_size * cap
        n_queue = n_local * cap
        me = lax.axis_index("ep")

        def swap(value, bit):
            return lax.ppermute(value, "ep", [(i, i ^ bit) for i in range(ep_size)])

        x_far = swap(tokens, 2)
        x_sib = swap(tokens, 1)
        x_far_sib = swap(x_far, 1)
        all_ids = jnp.arange(n_exp, dtype=jnp.int32)
        row_limit = jnp.sum(jnp.where(expert_ids[:, :, None] == all_ids, send_counts[0], 0), axis=-1)
        kept_mask = (slot_ids >= 0) & (slot_ids < row_limit)
        dest_row = jnp.where(kept_mask, expert_ids * cap + slot_ids, -1)
        facts = jnp.concatenate(
            [
                dest_row.astype(jnp.float32).T,
                jnp.where(kept_mask, gate_vals, 0.0).T,
                jnp.pad(send_counts.astype(jnp.float32), ((0, 0), (0, n_tok - n_exp))),
                jnp.zeros((15 - 2 * top_k, n_tok), jnp.float32),
            ],
            axis=0,
        )
        facts_far = swap(facts, 2)
        facts_sib = swap(facts, 1)
        facts_all = jnp.stack([facts, facts_sib, facts_far, swap(facts_far, 1)])

        dest_all = facts_all[:, :top_k].astype(jnp.int32) - me * n_queue
        dest_all = jnp.where((dest_all >= 0) & (dest_all < n_queue), dest_all, -1)
        gates_all = facts_all[:, top_k : 2 * top_k]
        counts_all = lax.dynamic_slice_in_dim(facts_all[:, 2 * top_k], me * n_local, n_local, 1).astype(jnp.int32)
        padded = (counts_all + 15) // 16 * 16
        local = jnp.arange(n_local, dtype=jnp.int32)
        before = local[None, :] < local[:, None]
        queue_off = jnp.sum(jnp.where(before[None], padded[:, None, :], 0), axis=2)
        total = jnp.sum(padded, axis=1)
        src = jnp.arange(4, dtype=jnp.int32)
        off = jnp.sum(jnp.where((src[None, :] < src[:, None])[None], padded.T[:, None, :], 0), axis=2).reshape(-1)
        n_rows = jnp.sum(padded, axis=0)

        def piece_home(piece):
            need = n_rows > piece * ROW_PIECE
            last = jnp.max(jnp.where(need[None, :] & (local[None, :] <= local[:, None]), local[None, :], -1), axis=1)
            first = jnp.min(jnp.where(need, local, n_local))
            return jnp.where(last >= 0, last, jnp.where(first < n_local, first, 0))

        at1, at2 = piece_home(1), piece_home(2)
        shift = jnp.sum(jnp.where((dest_all // cap)[..., None] == local, (queue_off - local * cap)[:, None, None, :], 0), axis=-1)
        queue_row = jnp.where(dest_all >= 0, dest_all + shift, -1)
        pad_rows = jnp.full((4, 8 - top_k, n_tok), -1, jnp.int32)
        places = jnp.concatenate([dest_all, pad_rows, queue_row, pad_rows], axis=1)
        high = lax.reduce_precision(gates_all, 8, 7)
        middle = lax.reduce_precision(gates_all - high, 8, 7)
        low = lax.reduce_precision(gates_all - high - middle, 8, 7)
        n_tiles = n_queue // 256
        pick, gate_tiles = pl.pallas_call(
            prep_kernel,
            grid=(4,),
            in_specs=[
                pl.BlockSpec((1, 16, n_tok), lambda s: (s, 0, 0)),
                pl.BlockSpec((3, 1, top_k, n_tok), lambda s: (0, s, 0, 0)),
            ],
            out_specs=[
                pl.BlockSpec((1, n_queue, n_tok), lambda s: (s, 0, 0)),
                pl.BlockSpec((n_tiles, 3, n_tok, 256), lambda s: (s, 0, 0, 0)),
            ],
            out_shape=[
                jax.ShapeDtypeStruct((4, n_queue, n_tok), jnp.bfloat16),
                jax.ShapeDtypeStruct((4 * n_tiles, 3, n_tok, 256), jnp.bfloat16),
            ],
            compiler_params=pltpu.CompilerParams(dimension_semantics=("arbitrary",), vmem_limit_bytes=40_000_000),
            cost_estimate=pl.CostEstimate(flops=10**9, bytes_accessed=4 * n_queue * n_tok * 8, transcendentals=0),
            name="prep",
        )(places, jnp.stack([high, middle, low]))

        whole = dict(pipeline_mode=pl.Buffered(1))
        any_space = pl.BlockSpec(memory_space=pl.ANY)
        hidden = pl.pallas_call(
            functools.partial(up_kernel, cap),
            grid_spec=pltpu.PrefetchScalarGridSpec(
                num_scalar_prefetch=4,
                grid=(n_local,),
                in_specs=[
                    pl.BlockSpec((4, GROUP * cap, n_tok), lambda e, *_: (0, e // GROUP, 0)),
                    *[pl.BlockSpec((n_tok, d_model), lambda e, *_: (0, 0), **whole) for _ in range(4)],
                    any_space,
                    any_space,
                ],
                out_specs=[
                    pl.BlockSpec((1, ROW_PIECE, d_ff), lambda e, off, n, at1, at2: (e, 0, 0)),
                    pl.BlockSpec((1, ROW_PIECE, d_ff), lambda e, off, n, at1, at2: (at1[e], 0, 0)),
                    pl.BlockSpec((1, ROW_PIECE, d_ff), lambda e, off, n, at1, at2: (at2[e], 0, 0)),
                ],
                scratch_shapes=[
                    pltpu.VMEM((GROUP, rows, d_model), jnp.bfloat16),
                    pltpu.VMEM((UP_SLOTS, d_model, d_ff), jnp.bfloat16),
                    pltpu.VMEM((UP_SLOTS, d_model, d_ff), jnp.bfloat16),
                    pltpu.SemaphoreType.DMA((2, UP_SLOTS)),
                ],
            ),
            out_shape=[jax.ShapeDtypeStruct((n_local, ROW_PIECE, d_ff), jnp.bfloat16)] * 3,
            compiler_params=pltpu.CompilerParams(dimension_semantics=("arbitrary",), vmem_limit_bytes=VMEM_LIMIT),
            cost_estimate=pl.CostEstimate(flops=4 * n_local * 192 * d_model * d_ff, bytes_accessed=4 * n_local * d_model * d_ff, transcendentals=0),
            name="experts_up",
        )(off, n_rows, at1, at2, pick, tokens, x_sib, x_far, x_far_sib, expert_w1, expert_w3)

        n_cols = d_model // COLUMN_CHUNKS

        def down(chunk, held):
            return pl.pallas_call(
                functools.partial(down_kernel, cap, chunk * n_cols),
                grid_spec=pltpu.PrefetchScalarGridSpec(
                    num_scalar_prefetch=6,
                    grid=(n_local,),
                    in_specs=[
                        pl.BlockSpec((1, ROW_PIECE, d_ff), lambda e, *_: (e, 0, 0)),
                        pl.BlockSpec((1, ROW_PIECE, d_ff), lambda e, off, n, qo, tot, at1, at2: (at1[e], 0, 0)),
                        pl.BlockSpec((1, ROW_PIECE, d_ff), lambda e, off, n, qo, tot, at1, at2: (at2[e], 0, 0)),
                        any_space,
                        any_space,
                    ],
                    out_specs=[pl.BlockSpec((2, n_tok, n_cols), lambda e, *_: (0, 0, 0), **whole) for _ in range(2)],
                    scratch_shapes=[
                        pltpu.VMEM((rows, n_cols), jnp.bfloat16),
                        pltpu.VMEM((4, n_queue, n_cols), jnp.bfloat16),
                        pltpu.VMEM((DOWN_SLOTS, d_ff, n_cols), jnp.bfloat16),
                        pltpu.VMEM(gate_tiles.shape, jnp.bfloat16),
                        pltpu.SemaphoreType.DMA((DOWN_SLOTS,)),
                        pltpu.SemaphoreType.DMA((4 * n_tiles,)),
                    ],
                ),
                out_shape=[jax.ShapeDtypeStruct((2, n_tok, n_cols), jnp.float32) for _ in range(2)],
                compiler_params=pltpu.CompilerParams(dimension_semantics=("arbitrary",), vmem_limit_bytes=VMEM_LIMIT),
                cost_estimate=pl.CostEstimate(flops=2 * n_local * 192 * n_cols * d_ff, bytes_accessed=2 * n_local * n_cols * d_ff, transcendentals=0),
            )(off, n_rows, queue_off.reshape(-1), total, at1, at2, *held, expert_w2, gate_tiles)

        gathered = lax.all_gather(tokens, "tp", axis=0, tiled=True)
        sums_own, sums_sib, returned = [], [], []
        for chunk in range(COLUMN_CHUNKS):
            own, sib = down(chunk, hidden)
            from_sib = swap(sib, 1)
            if chunk == 0:
                gathered, own = lax.optimization_barrier((gathered, own))
                pre_gate = jnp.dot(gathered, shared_w1, preferred_element_type=jnp.float32)
                pre_up = jnp.dot(gathered, shared_w3, preferred_element_type=jnp.float32)
                shared_hidden = (jax.nn.silu(pre_gate) * pre_up).astype(jnp.bfloat16)
            passed_on = own[1] + from_sib[1]
            passed_on, shared_hidden, *hidden = lax.optimization_barrier((passed_on, shared_hidden, *hidden))
            returned.append(swap(passed_on, 2))
            if chunk == 0:
                hidden_blocks = lax.all_to_all(shared_hidden.reshape(mesh.shape["tp"], n_tok, -1), "tp", 0, 0)
            sums_own.append(own[0])
            sums_sib.append(from_sib[0])

        width = shared_w2.shape[0]
        rep = lax.axis_index("data") * ep_size + me
        w2_part = lax.dynamic_slice_in_dim(shared_w2, rep * (width // n_rep), width // n_rep, 0)
        w2_all = lax.all_gather(w2_part, ("tp", "data", "ep"), axis=0, tiled=True)
        w2_all, passed_on = lax.optimization_barrier((w2_all, passed_on))
        w2_blocks = w2_all.reshape(mesh.shape["tp"], width, d_model)
        shared_out = jnp.dot(hidden_blocks[0], w2_blocks[0], preferred_element_type=jnp.float32)
        for block in range(1, mesh.shape["tp"]):
            shared_out += jnp.dot(hidden_blocks[block], w2_blocks[block], preferred_element_type=jnp.float32)
        base = tokens.astype(jnp.float32) + shared_out
        parts = []
        for chunk in range(COLUMN_CHUNKS):
            routed = sums_own[chunk] + sums_sib[chunk] + returned[chunk]
            parts.append((base[:, chunk * n_cols : (chunk + 1) * n_cols] + routed).astype(jnp.bfloat16))
        return jnp.concatenate(parts, axis=1)


    return jax.shard_map(
        layer_body,
        mesh=mesh,
        in_specs=(row_spec, row_spec, row_spec, row_spec, row_spec, P(None, "tp"), P(None, "tp"), P("tp", None), expert_spec, expert_spec, expert_spec),
        out_specs=row_spec,
        check_vma=False,
    )
```

time: 335 us -> 305 us (0.910); the launches traced: 330 us -> 305 us
  other arithmetic: 54.3 us -> 15.1 us
  Pallas kernels: 143 us -> 167 us
  starting transfers between devices: 32.5 us -> 10.7 us
  local copies, waits for them, and re-layouts: 7.61 us -> 13.3 us
  waiting for transfers between devices: 59.4 us -> 63.9 us
    all_to_all x1, waiting for transfers between devices: 0.01 us -> 30.4 us  [layer_body(): lax.all_to_all(shared_hidden.reshape(mesh.shape['tp'], n_tok, -1), 'tp',...]
    ppermute x10, waiting for transfers between devices: 58.7 us -> 32.8 us  [swap(): return lax.ppermute(value, 'ep', [(i, i ^ bit) for i in range(ep_size)])]
    reduce_sum x1 -> x2, other arithmetic: 24.4 us -> 0.23 us  [the longest x1 0.14 us: layer_body(): queue_off = jnp.sum(jnp.where(before[None], padded[:, None, :], 0), axis=2)]
    ppermute x10, starting transfers between devices: 27.5 us -> 5.68 us  [swap(): return lax.ppermute(value, 'ep', [(i, i ^ bit) for i in range(ep_size)])]
    pallas_call x2 -> x3, Pallas kernels: 71.8 us -> 91 us  [the longest x2 77.9 us: down(): pl.pallas_call(functools.partial(down_kernel, cap, chunk * n_cols), grid_...]
    reduce_or x1 -> x0, other arithmetic: 8.24 us -> none  [layer_body(): jnp.any(dest_all[:, :, None, :] == lanes[:, None], axis=1)]
    eq x1 -> x0, other arithmetic: 5.84 us -> none  [layer_body(): queue_row[..., None] == lanes]
    pallas_call x1, Pallas kernels: 70.7 us -> 76.4 us  [layer_body(): pl.pallas_call(functools.partial(up_kernel, cap), grid_spec=pltpu.Prefetc...]
  transfers between devices with their start and end apart: 13 -> 13, of which waited for: 5 -> 6; matrix products, arithmetic and copies ran while one was open for 21% -> 12% of each run, Pallas kernels for 43% -> 55%
where the time goes in v2:
time: 305 us
  Pallas kernels  167 us (55%)
  waiting for transfers between devices  63.9 us (21%)
  matrix products  18.1 us (6%)
  between operations  16.3 us (5%)
  other arithmetic  15.1 us (5%)
  local copies, waits for them, and re-layouts  13.3 us (4%)
  starting transfers between devices  10.7 us (4%)
    pallas_call x2, Pallas kernels, down(): pl.pallas_call(functools.partial(down_kernel, cap, chunk * n_cols), grid_...  77.9 us
    pallas_call x1, Pallas kernels, layer_body(): pl.pallas_call(functools.partial(up_kernel, cap), grid_spec=pltpu.Prefetc...  76.4 us
    ppermute x10, waiting for transfers between devices, swap(): return lax.ppermute(value, 'ep', [(i, i ^ bit) for i in range(ep_size)])  32.8 us
    all_to_all x1, waiting for transfers between devices, layer_body(): lax.all_to_all(shared_hidden.reshape(mesh.shape['tp'], n_tok, -1), 'tp',...  30.4 us
    pallas_call x1, Pallas kernels, layer_body(): pl.pallas_call(prep_kernel, grid=(4,), in_specs=[pl.BlockSpec((1, 16, n_t...  13.1 us
    unnamed x30, local copies, waits for them, and re-layouts  7.36 us
  transfers between devices with their start and end apart: 13, of which 6 were waited for; matrix products, arithmetic and copies ran while one was open for 12% of the time, Pallas kernels for 55%

profile of v2, /device:TPU:0, one launch (start us, length us, event | category | flops | bytes accessed | tf_op | source)
XLA Modules:
  0.0 304.6 jit_solution(17616302843049294269)
XLA Ops:
  6.5 0.7 all-gather.3.cloned.1.call-update
  7.3 0.0 all-gather.5.cloned.1.call-start
  7.3 1.8 constant_dynamic-slice_fusion
  9.1 0.0 all-gather.5.cloned.1.call-update
  9.1 0.7 convert_element_type.30
  9.8 0.1 pad.21.clone
  9.8 0.8 select_reduce_fusion.1
  10.7 0.7 convert_bitcast_fusion
  11.4 0.7 select_bitcast_fusion
  12.1 0.1 fusion.34
  12.2 3.0 collective-permute-start.1
  15.2 0.2 collective-permute-start.4
  15.3 0.4 collective-permute-start.3
  15.7 0.1 fusion.52
  15.8 1.1 collective-permute-done.1
  16.9 0.0 collective-permute-start.2
  16.9 0.0 collective-permute-done
  16.9 1.3 collective-permute-done.2
  18.2 0.1 fusion.43
  18.3 0.7 fusion.45
  19.0 0.1 select_reduce_fusion.5
  19.1 0.1 select_reduce_fusion.2
  19.3 0.2 select_reduce_fusion
  19.5 21.5 %collective-permute-done.4.x2_ref = bf16[256,2048]{1,0:T(8,128)(2,1)S(1)} collective-permute-done((bf16[256,2048]{1,0:T(8,128)(2,1)}, bf16[256,2048]{1,0:T(8,128)(2,1)S(1)}, u32[]{:S(2)}, u32[]{:S(2)}) %collective-permute-start.4) | collective-permute-done | bytes 1048608 | tf_op jit(solution)/shard_map/ppermute | solution.py:228
  41.0 0.0 collective-permute-start.5
  41.0 0.8 select_reduce_fusion.6
  41.8 0.7 reshape.79.queue_off_ref
  45.0 0.1 copy.17
  45.1 0.6 reshape.78.off_ref
  45.8 13.1 %prep.1 = (bf16[4,1536,256]{2,1,0:T(8,128)(2,1)S(1)}, bf16[24,3,256,256]{3,2,1,0:T(8,128)(2,1)S(1)}) custom-call(s32[4,16,256]{2,1,0:T(8,128)S(1)} %pad_add_fusion.facts_ref, f32[3,4,6,256]{3,2,1,0:T(8,128)S(1)} %pad_maximum_fusion.1.gates_in_ref), custom_call_target="tpu_custom_call" | custom-call | flops 1000000000 | bytes 12582912 | tf_op jit(solution)/shard_map/prep/pallas_call | solution.py:278
  58.9 3.5 %copy-done = bf16[24,3,256,256]{3,2,1,0:T(8,128)(2,1)} copy-done((bf16[24,3,256,256]{3,2,1,0:T(8,128)(2,1)}, bf16[24,3,256,256]{3,2,1,0:T(8,128)(2,1)S(1)}, u32[]{:S(2)}) %copy-start) | copy-done | bytes 9437208
  62.4 1.6 copy-done.1
  64.0 0.1 select_reduce_fusion.3
  64.1 0.1 select_reduce_fusion.4
  64.2 0.6 compare_select_fusion.3
  64.8 0.0 collective-permute-done.3.x1_ref
  64.8 0.0 collective-permute-done.5.x3_ref
  64.8 1.0 copy-done.9
  65.8 1.0 copy-done.10
  66.8 76.4 %experts_up.1 = (bf16[16,128,1408]{2,1,0:T(8,128)(2,1)}, bf16[16,128,1408]{2,1,0:T(8,128)(2,1)}, bf16[16,128,1408]{2,1,0:T(8,128)(2,1)}) custom-call(s32[64]{0:T(128)} %reshape.78.off_ref, s32[16]{0:T(128)} %copy-done.11, s32[16]{0:T(128)} %get-tuple-element.60.at1_ref, s32[16]{0:T(128)} %get-tuple-element.59.at2_ref, bf16[4,1536,256]{2,1,0:T(8,128)(2,1)} %copy-done.1, ...), custom_call_target="tpu_custom_call" | custom-call | flops 35433480192 | bytes 184549376 | tf_op jit(solution)/shard_map/experts_up/pallas_call | solution.py:300
  143.2 39.9 %shard_map.109 = (f32[2,256,1024]{2,1,0:T(8,128)}, f32[2,256,1024]{2,1,0:T(8,128)}) custom-call(s32[64]{0:T(128)} %reshape.78.off_ref, s32[16]{0:T(128)} %copy-done.11, s32[64]{0:T(128)} %reshape.79.queue_off_ref, s32[4]{0:T(128)} %get-tuple-element.41.total_ref, s32[16]{0:T(128)} %get-tuple-element.60.at1_ref, s32[16]{0:T(128)} %get-tuple-element.59.at2_ref, ...), custom_call_target="tpu_custom_call" | custom-call | flops 8858370048 | bytes 46137344 | tf_op jit(solution)/shard_map/pallas_call | solution.py:332
  183.0 0.1 collective-permute-start.6
  183.1 0.0 all-gather.3.cloned.1.call-done
  183.1 0.0 copy-start.13
  183.2 4.3 %collective-permute-done.6 = f32[2,256,1024]{2,1,0:T(8,128)S(1)} collective-permute-done((f32[2,256,1024]{2,1,0:T(8,128)}, f32[2,256,1024]{2,1,0:T(8,128)S(1)}, u32[]{:S(2)}, u32[]{:S(2)}) %collective-permute-start.6) | collective-permute-done | bytes 2097184 | tf_op jit(solution)/shard_map/ppermute | solution.py:228
  187.5 3.1 %fusion.29 = f32[256,1024]{1,0:T(8,128)} fusion(f32[2,256,1024]{2,1,0:T(8,128)S(1)} %collective-permute-done.6, f32[2,256,1024]{2,1,0:T(8,128)} %get-tuple-element.29), kind=kLoop, calls=%fused_computation.27 | loop fusion | flops 262144 | bytes 3145728 | tf_op jit(solution)/shard_map/add | solution.py:369
  190.6 5.2 %fusion.47 = f32[1024,704]{0,1:T(8,128)S(1)} fusion(bf16[1024,2048]{1,0:T(8,128)(2,1)} %all-gather.3.cloned.1.call-done, bf16[2048,704]{0,1:T(8,128)(2,1)S(1)} %copy-done.13), kind=kOutput, calls=%fused_computation.102 | convolution fusion | flops 2952790016 | bytes 9961472 | tf_op jit(solution)/shard_map/dot_general | solution.py:366
  195.8 4.5 %multiply_convert_fusion = bf16[1024,704]{0,1:T(8,128)(2,1)} fusion(f32[1024,704]{0,1:T(8,128)S(1)} %fusion.47, bf16[1024,2048]{1,0:T(8,128)(2,1)S(1)} %copy-done.12, bf16[2048,704]{0,1:T(8,128)(2,1)S(1)} %copy-done.14), kind=kOutput, calls=%fused_computation.8 | convolution fusion | flops 2957115392 | bytes 11403264 | tf_op jit(solution)/shard_map/dot_general | solution.py:367
  200.2 38.0 %shard_map.110 = (f32[2,256,1024]{2,1,0:T(8,128)}, f32[2,256,1024]{2,1,0:T(8,128)}) custom-call(s32[64]{0:T(128)} %reshape.78.off_ref, s32[16]{0:T(128)} %copy-done.11, s32[64]{0:T(128)} %reshape.79.queue_off_ref, s32[4]{0:T(128)} %get-tuple-element.41.total_ref, s32[16]{0:T(128)} %get-tuple-element.60.at1_ref, s32[16]{0:T(128)} %get-tuple-element.59.at2_ref, ...), custom_call_target="tpu_custom_call" | custom-call | flops 8858370048 | bytes 46137344 | tf_op jit(solution)/shard_map/pallas_call | solution.py:332
  238.3 0.1 collective-permute-start.7
  238.3 2.7 copy.21
  241.1 5.0 %all-to-all-start = ((bf16[4,256,704]{1,2,0:T(8,128)(2,1)}), bf16[4,256,704]{1,2,0:T(8,128)(2,1)S(1)}, u32[]{:S(2)}, u32[]{:S(2)}) async-start(bf16[4,256,704]{1,2,0:T(8,128)(2,1)} %bitcast.58), calls=%async_computation | async-start | bytes 2883584 | tf_op jit(solution)/shard_map/all_to_all | solution.py:373
  246.1 2.3 fusion.28
  248.4 2.0 collective-permute-start.9
  250.4 30.4 %all-to-all-done = bf16[4,256,704]{1,2,0:T(8,128)(2,1)S(1)} async-done(((bf16[4,256,704]{1,2,0:T(8,128)(2,1)}), bf16[4,256,704]{1,2,0:T(8,128)(2,1)S(1)}, u32[]{:S(2)}, u32[]{:S(2)}) %all-to-all-start) | async-done | bytes 1441824 | tf_op jit(solution)/shard_map/all_to_all | solution.py:373
  280.8 3.0 fusion.4
  283.8 3.5 %fusion.8 = f32[256,2048]{1,0:T(8,128)S(1)} fusion(f32[256,2048]{1,0:T(8,128)S(1)} %fusion.4, bf16[2816,2048]{1,0:T(8,128)(2,1)} %all-gather.5.cloned.1.call-done, bf16[4,256,704]{1,2,0:T(8,128)(2,1)S(1)} %all-to-all-done), kind=kOutput, calls=%fused_computation.9 | convolution fusion | flops 738721792 | bytes 7438336 | tf_op jit(solution)/shard_map/dot_general | solution.py:383
  287.3 0.0 copy-start.3
  287.3 1.0 fusion.11
  288.3 0.2 copy-done.3
  288.5 1.0 fusion.17
  289.6 4.5 %collective-permute-done.9 = f32[256,1024]{1,0:T(8,128)} collective-permute-done((f32[256,1024]{1,0:T(8,128)}, f32[256,1024]{1,0:T(8,128)}, u32[]{:S(2)}, u32[]{:S(2)}) %collective-permute-start.9) | collective-permute-done | bytes 1048608 | tf_op jit(solution)/shard_map/ppermute | solution.py:228
  294.1 2.6 fusion.27
  296.7 1.1 pad_maximum_fusion
  (42 shorter events, 0.2 us)
Async XLA Ops:
  6.5 176.6 %all-gather.3.cloned.1.call-start = ((), (), s32[]{:S(2)}) async-start(), calls=%async_computation.1 | async-start | bytes 5242880 | tf_op jit(solution)/shard_map/all_gather | solution.py:359
  7.3 243.2 %all-gather.5.cloned.1.call-start = ((), (), s32[]{:S(2)}) async-start(), calls=%async_computation.2 | async-start | bytes 11894784 | tf_op jit(solution)/shard_map/all_gather | solution.py:380
  12.2 4.7 %collective-permute-start.1 = (f32[16,256]{1,0:T(8,128)S(1)}, f32[16,256]{1,0:T(8,128)S(1)}, u32[]{:S(2)}, u32[]{:S(2)}) collective-permute-start(f32[16,256]{1,0:T(8,128)S(1)} %fusion.34), channel_id=1, source_target_pairs={{0,2},{1,3},{2,0},{3,1},{4,6},{5,7},{6,4},{7,5},{8,10},{9,11},{10,... | collective-permute-start | bytes 49160 | tf_op jit(solution)/shard_map/ppermute | solution.py:228
  15.2 1.7 collective-permute-start
  15.2 25.8 %collective-permute-start.4 = (bf16[256,2048]{1,0:T(8,128)(2,1)}, bf16[256,2048]{1,0:T(8,128)(2,1)S(1)}, u32[]{:S(2)}, u32[]{:S(2)}) collective-permute-start(bf16[256,2048]{1,0:T(8,128)(2,1)} %x0_ref.1), channel_id=1, source_target_pairs={{0,2},{1,3},{2,0},{3,1},{4,6},{5,7},{6,4},{7,5},{8,10},{9,11},{10,... | collective-permute-start | bytes 3145736 | tf_op jit(solution)/shard_map/ppermute | solution.py:228
  15.3 49.5 %collective-permute-start.3 = (bf16[256,2048]{1,0:T(8,128)(2,1)}, bf16[256,2048]{1,0:T(8,128)(2,1)S(1)}, u32[]{:S(2)}, u32[]{:S(2)}) collective-permute-start(bf16[256,2048]{1,0:T(8,128)(2,1)} %x0_ref.1), channel_id=1, source_target_pairs={{0,1},{1,0},{2,3},{3,2},{4,5},{5,4},{6,7},{7,6},{8,9},{9,8},{10,11... | collective-permute-start | bytes 3145736 | tf_op jit(solution)/shard_map/ppermute | solution.py:228
  16.9 1.3 collective-permute-start.2
  19.0 47.8 %copy-start.11 = (s32[16]{0:T(128)}, s32[16]{0:T(128)S(1)}, u32[]{:S(2)}) copy-start(s32[16]{0:T(128)S(1)} %get-tuple-element.42.n_ref) | copy-start | bytes 196
  41.0 17.9 %copy-start.8 = (bf16[256,2048]{1,0:T(8,128)(2,1)}, bf16[256,2048]{1,0:T(8,128)(2,1)S(1)}, u32[]{:S(2)}) copy-start(bf16[256,2048]{1,0:T(8,128)(2,1)S(1)} %collective-permute-done.4.x2_ref) | copy-start | bytes 3145732
  41.0 23.9 %collective-permute-start.5 = (bf16[256,2048]{1,0:T(8,128)(2,1)S(1)}, bf16[256,2048]{1,0:T(8,128)(2,1)S(1)}, u32[]{:S(2)}, u32[]{:S(2)}) collective-permute-start(bf16[256,2048]{1,0:T(8,128)(2,1)S(1)} %collective-permute-done.4.x2_ref), channel_id=1, source_target_pairs={{0,1},{1,0},{2,3},{3,2},{4,5},{5,4},{6,7},{7,6},{8,9},{9,8},{10,11... | collective-permute-start | bytes 3145736 | tf_op jit(solution)/shard_map/ppermute | solution.py:228
  58.9 3.5 %copy-start = (bf16[24,3,256,256]{3,2,1,0:T(8,128)(2,1)}, bf16[24,3,256,256]{3,2,1,0:T(8,128)(2,1)S(1)}, u32[]{:S(2)}) copy-start(bf16[24,3,256,256]{3,2,1,0:T(8,128)(2,1)S(1)} %get-tuple-element.27.gates_hbm) | copy-start | bytes 28311556
  62.4 1.6 copy-start.1
  64.8 1.0 copy-start.9
  65.8 1.0 copy-start.10
  183.0 4.4 %collective-permute-start.6 = (f32[2,256,1024]{2,1,0:T(8,128)}, f32[2,256,1024]{2,1,0:T(8,128)S(1)}, u32[]{:S(2)}, u32[]{:S(2)}) collective-permute-start(f32[2,256,1024]{2,1,0:T(8,128)} %get-tuple-element.30), channel_id=1, source_target_pairs={{0,1},{1,0},{2,3},{3,2},{4,5},{5,4},{6,7},{7,6},{8,9},{9,8},{10,11... | collective-permute-start | bytes 6291464 | tf_op jit(solution)/shard_map/ppermute | solution.py:228
  183.1 7.4 %copy-start.13 = (bf16[2048,704]{0,1:T(8,128)(2,1)S(1)}, bf16[2048,704]{0,1:T(8,128)(2,1)}, u32[]{:S(2)}) copy-start(bf16[2048,704]{0,1:T(8,128)(2,1)} %param.16) | copy-start | bytes 8650756
  187.5 8.3 %copy-start.5 = (f32[2,256,1024]{2,1,0:T(8,128)}, f32[2,256,1024]{2,1,0:T(8,128)S(1)}, u32[]{:S(2)}) copy-start(f32[2,256,1024]{2,1,0:T(8,128)S(1)} %collective-permute-done.6) | copy-start | bytes 6291460
  190.6 5.2 %copy-start.12 = (bf16[1024,2048]{1,0:T(8,128)(2,1)S(1)}, bf16[1024,2048]{1,0:T(8,128)(2,1)}, u32[]{:S(2)}) copy-start(bf16[1024,2048]{1,0:T(8,128)(2,1)} %all-gather.3.cloned.1.call-done) | copy-start | bytes 12582916
  190.6 5.2 %copy-start.14 = (bf16[2048,704]{0,1:T(8,128)(2,1)S(1)}, bf16[2048,704]{0,1:T(8,128)(2,1)}, u32[]{:S(2)}) copy-start(bf16[2048,704]{0,1:T(8,128)(2,1)} %param.17) | copy-start | bytes 8650756
  238.3 7.8 %collective-permute-start.7 = (f32[2,256,1024]{2,1,0:T(8,128)}, f32[2,256,1024]{2,1,0:T(8,128)}, u32[]{:S(2)}, u32[]{:S(2)}) collective-permute-start(f32[2,256,1024]{2,1,0:T(8,128)} %get-tuple-element.37), channel_id=1, source_target_pairs={{0,1},{1,0},{2,3},{3,2},{4,5},{5,4},{6,7},{7,6},{8,9},{9,8},{10,11... | collective-permute-start | bytes 6291464 | tf_op jit(solution)/shard_map/ppermute | solution.py:228
  238.3 7.7 %copy-start.7 = (f32[2,256,1024]{2,1,0:T(8,128)S(1)}, f32[2,256,1024]{2,1,0:T(8,128)}, u32[]{:S(2)}) copy-start(f32[2,256,1024]{2,1,0:T(8,128)} %get-tuple-element.36) | copy-start | bytes 6291460
  241.1 39.8 %all-to-all-start = ((bf16[4,256,704]{1,2,0:T(8,128)(2,1)}), bf16[4,256,704]{1,2,0:T(8,128)(2,1)S(1)}, u32[]{:S(2)}, u32[]{:S(2)}) async-start(bf16[4,256,704]{1,2,0:T(8,128)(2,1)} %bitcast.58), calls=%async_computation | async-start | bytes 2883584 | tf_op jit(solution)/shard_map/all_to_all | solution.py:373
  246.0 43.5 %collective-permute-start.8 = (f32[256,1024]{1,0:T(8,128)}, f32[256,1024]{1,0:T(8,128)}, u32[]{:S(2)}, u32[]{:S(2)}) collective-permute-start(f32[256,1024]{1,0:T(8,128)} %fusion.29), channel_id=1, source_target_pairs={{0,2},{1,3},{2,0},{3,1},{4,6},{5,7},{6,4},{7,5},{8,10},{9,11},{10,... | collective-permute-start | bytes 3145736 | tf_op jit(solution)/shard_map/ppermute | solution.py:228
  248.4 45.7 %collective-permute-start.9 = (f32[256,1024]{1,0:T(8,128)}, f32[256,1024]{1,0:T(8,128)}, u32[]{:S(2)}, u32[]{:S(2)}) collective-permute-start(f32[256,1024]{1,0:T(8,128)} %fusion.28), channel_id=1, source_target_pairs={{0,2},{1,3},{2,0},{3,1},{4,6},{5,7},{6,4},{7,5},{8,10},{9,11},{10,... | collective-permute-start | bytes 3145736 | tf_op jit(solution)/shard_map/ppermute | solution.py:228
  280.8 6.4 %copy-start.2 = (bf16[2816,2048]{1,0:T(8,128)(2,1)S(1)}, bf16[2816,2048]{1,0:T(8,128)(2,1)}, u32[]{:S(2)}) copy-start(bf16[2816,2048]{1,0:T(8,128)(2,1)} %all-gather.5.cloned.1.call-done) | copy-start | bytes 34603012
  287.3 1.2 copy-start.3
  288.5 5.6 %copy-start.4 = (f32[2,256,1024]{2,1,0:T(8,128)S(1)}, f32[2,256,1024]{2,1,0:T(8,128)}, u32[]{:S(2)}) copy-start(f32[2,256,1024]{2,1,0:T(8,128)} %get-tuple-element.29) | copy-start | bytes 6291460
  288.5 5.6 %copy-start.6 = (f32[2,256,1024]{2,1,0:T(8,128)S(1)}, f32[2,256,1024]{2,1,0:T(8,128)}, u32[]{:S(2)}) copy-start(f32[2,256,1024]{2,1,0:T(8,128)} %copy-done.5) | copy-start | bytes 6291460
Sparse Core Ops, SparseCore 0:
  8.9 83.4 all-gather.2
  95.2 89.2 all-gather.4

commit v3 on v2

--- a/solution.py
+++ b/solution.py
@@ -135,16 +135,20 @@
     pick_rows(n_ref[step], rows_ref.shape[1], body)
 
 
-def down_kernel(cap, first, off_ref, n_ref, queue_off_ref, total_ref, at1_ref, at2_ref, h0_ref, h1_ref, h2_ref, w2_hbm, gates_hbm, own_ref, sib_ref, out_ref, queue_ref, w2_ring, gates_ref, w_sems, gate_sems):
+def down_kernel(cap, first, off_ref, n_ref, queue_off_ref, total_ref, h0_hbm, h1_hbm, h2_hbm, w2_hbm, gates_hbm, own_ref, sib_ref, out_ref, queue_ref, w2_ring, h_ring, gates_ref, w_sems, h_sems, gate_sems):
     step = pl.program_id(0)
     n_local = pl.num_programs(0)
     n_slots, _, width_all = w2_ring.shape
     n_tiles_max = gates_ref.shape[0] // 4
-    h_refs = (h0_ref, h1_ref, h2_ref)
-
-    def fetch(expert):
+    h_hbm = (h0_hbm, h1_hbm, h2_hbm)
+
+    def fetch(expert, act):
         slot = expert % n_slots
-        return pltpu.make_async_copy(w2_hbm.at[expert, :, first : first + width_all], w2_ring.at[slot], w_sems.at[slot])
+        for piece, source in enumerate(h_hbm):
+            into = h_ring.at[slot, piece * ROW_PIECE : (piece + 1) * ROW_PIECE]
+            copy = pltpu.make_async_copy(source.at[expert], into, h_sems.at[piece, slot])
+            pl.when(n_ref[expert] > piece * ROW_PIECE)(functools.partial(act, copy))
+        act(pltpu.make_async_copy(w2_hbm.at[expert, :, first : first + width_all], w2_ring.at[slot], w_sems.at[slot]))
 
     def gate_copies(act):
         for src in range(4):
@@ -156,18 +160,21 @@
     @pl.when(step == 0)
     def _():
         for expert in range(n_slots - 1):
-            fetch(expert).start()
+            fetch(expert, lambda copy: copy.start())
+
+    @pl.when(step + n_slots - 1 < n_local)
+    def _():
+        fetch(step + n_slots - 1, lambda copy: copy.start())
+
+    @pl.when(step == 0)
+    def _():
         gate_copies(lambda copy: copy.start())
 
-    @pl.when(step + n_slots - 1 < n_local)
-    def _():
-        fetch(step + n_slots - 1).start()
-
-    fetch(step).wait()
+    fetch(step, lambda copy: copy.wait())
     slot = step % n_slots
 
     def body(size):
-        h = jnp.concatenate([h_refs[piece][0] for piece in range(size // ROW_PIECE)], axis=0)
+        h = h_ring[slot, :size, :]
         for begin, width in column_pieces(width_all, 512):
             out = jnp.dot(h, w2_ring[slot, :, begin : begin + width], preferred_element_type=jnp.float32)
             out_ref[:size, begin : begin + width] = out.astype(jnp.bfloat16)
@@ -332,29 +339,25 @@
             return pl.pallas_call(
                 functools.partial(down_kernel, cap, chunk * n_cols),
                 grid_spec=pltpu.PrefetchScalarGridSpec(
-                    num_scalar_prefetch=6,
+                    num_scalar_prefetch=4,
                     grid=(n_local,),
-                    in_specs=[
-                        pl.BlockSpec((1, ROW_PIECE, d_ff), lambda e, *_: (e, 0, 0)),
-                        pl.BlockSpec((1, ROW_PIECE, d_ff), lambda e, off, n, qo, tot, at1, at2: (at1[e], 0, 0)),
-                        pl.BlockSpec((1, ROW_PIECE, d_ff), lambda e, off, n, qo, tot, at1, at2: (at2[e], 0, 0)),
-                        any_space,
-                        any_space,
-                    ],
+                    in_specs=[any_space] * 5,
                     out_specs=[pl.BlockSpec((2, n_tok, n_cols), lambda e, *_: (0, 0, 0), **whole) for _ in range(2)],
                     scratch_shapes=[
                         pltpu.VMEM((rows, n_cols), jnp.bfloat16),
                         pltpu.VMEM((4, n_queue, n_cols), jnp.bfloat16),
                         pltpu.VMEM((DOWN_SLOTS, d_ff, n_cols), jnp.bfloat16),
+                        pltpu.VMEM((DOWN_SLOTS, rows, d_ff), jnp.bfloat16),
                         pltpu.VMEM(gate_tiles.shape, jnp.bfloat16),
                         pltpu.SemaphoreType.DMA((DOWN_SLOTS,)),
+                        pltpu.SemaphoreType.DMA((3, DOWN_SLOTS)),
                         pltpu.SemaphoreType.DMA((4 * n_tiles,)),
                     ],
                 ),
                 out_shape=[jax.ShapeDtypeStruct((2, n_tok, n_cols), jnp.float32) for _ in range(2)],
                 compiler_params=pltpu.CompilerParams(dimension_semantics=("arbitrary",), vmem_limit_bytes=VMEM_LIMIT),
                 cost_estimate=pl.CostEstimate(flops=2 * n_local * 192 * n_cols * d_ff, bytes_accessed=2 * n_local * n_cols * d_ff, transcendentals=0),
-            )(off, n_rows, queue_off.reshape(-1), total, at1, at2, *held, expert_w2, gate_tiles)
+            )(off, n_rows, queue_off.reshape(-1), total, *held, expert_w2, gate_tiles)
 
         gathered = lax.all_gather(tokens, "tp", axis=0, tiled=True)
         sums_own, sums_sib, returned = [], [], []

time: 305 us -> 302 us (level)
    pallas_call x2, Pallas kernels: 77.9 us -> 74.2 us  [down(): pl.pallas_call(functools.partial(down_kernel, cap, chunk * n_cols), grid_...]
  transfers between devices with their start and end apart: 13 -> 13, of which waited for: 6 -> 6; matrix products, arithmetic and copies ran while one was open for 12% -> 12% of each run, Pallas kernels for 55% -> 54%
where the time goes in v3:
time: 302 us; the launch traced here: 301 us
  Pallas kernels  164 us (54%)
  waiting for transfers between devices  65.5 us (22%)
  matrix products  18.1 us (6%)
  between operations  16.3 us (5%)
  other arithmetic  15.1 us (5%)
  local copies, waits for them, and re-layouts  13.3 us (4%)
  starting transfers between devices  9.54 us (3%)
    pallas_call x1, Pallas kernels, layer_body(): pl.pallas_call(functools.partial(up_kernel, cap), grid_spec=pltpu.Prefetc...  76.4 us
    pallas_call x2, Pallas kernels, down(): pl.pallas_call(functools.partial(down_kernel, cap, chunk * n_cols), grid_...  74.2 us
    ppermute x10, waiting for transfers between devices, swap(): return lax.ppermute(value, 'ep', [(i, i ^ bit) for i in range(ep_size)])  34.3 us
    all_to_all x1, waiting for transfers between devices, layer_body(): lax.all_to_all(shared_hidden.reshape(mesh.shape['tp'], n_tok, -1), 'tp',...  30.4 us
    pallas_call x1, Pallas kernels, layer_body(): pl.pallas_call(prep_kernel, grid=(4,), in_specs=[pl.BlockSpec((1, 16, n_t...  13.1 us
    unnamed x30, local copies, waits for them, and re-layouts  7.36 us
  transfers between devices with their start and end apart: 13, of which 6 were waited for; matrix products, arithmetic and copies ran while one was open for 12% of the time, Pallas kernels for 54%

profile of v3, /device:TPU:0, one launch (start us, length us, event | category | flops | bytes accessed | tf_op | source)
XLA Modules:
  0.0 301.4 jit_solution(17438099792354300547)
XLA Ops:
  6.5 0.7 all-gather.3.cloned.1.call-update
  7.3 0.0 all-gather.5.cloned.1.call-start
  7.3 1.8 constant_dynamic-slice_fusion
  9.1 0.0 all-gather.5.cloned.1.call-update
  9.1 0.7 convert_element_type.30
  9.8 0.1 pad.21.clone
  9.8 0.8 select_reduce_fusion.1
  10.7 0.7 convert_bitcast_fusion
  11.4 0.7 select_bitcast_fusion
  12.1 0.1 fusion.34
  12.2 3.0 collective-permute-start.1
  15.2 0.2 collective-permute-start.4
  15.3 0.4 collective-permute-start.3
  15.7 0.1 fusion.52
  15.8 1.1 collective-permute-done.1
  16.9 0.0 collective-permute-start.2
  16.9 0.0 collective-permute-done
  16.9 1.3 collective-permute-done.2
  18.2 0.1 fusion.43
  18.3 0.7 fusion.45
  19.0 0.1 select_reduce_fusion.5
  19.1 0.1 select_reduce_fusion.2
  19.3 0.2 select_reduce_fusion
  19.5 21.5 %collective-permute-done.4.x2_ref = bf16[256,2048]{1,0:T(8,128)(2,1)S(1)} collective-permute-done((bf16[256,2048]{1,0:T(8,128)(2,1)}, bf16[256,2048]{1,0:T(8,128)(2,1)S(1)}, u32[]{:S(2)}, u32[]{:S(2)}) %collective-permute-start.4) | collective-permute-done | bytes 1048608 | tf_op jit(solution)/shard_map/ppermute | solution.py:235
  41.0 0.0 collective-permute-start.5
  41.0 0.8 select_reduce_fusion.6
  41.8 0.7 reshape.79.queue_off_ref
  45.0 0.1 copy.17
  45.1 0.6 reshape.78.off_ref
  45.8 13.1 %prep.1 = (bf16[4,1536,256]{2,1,0:T(8,128)(2,1)S(1)}, bf16[24,3,256,256]{3,2,1,0:T(8,128)(2,1)S(1)}) custom-call(s32[4,16,256]{2,1,0:T(8,128)S(1)} %pad_add_fusion.facts_ref, f32[3,4,6,256]{3,2,1,0:T(8,128)S(1)} %pad_maximum_fusion.1.gates_in_ref), custom_call_target="tpu_custom_call" | custom-call | flops 1000000000 | bytes 12582912 | tf_op jit(solution)/shard_map/prep/pallas_call | solution.py:285
  58.9 3.5 %copy-done = bf16[24,3,256,256]{3,2,1,0:T(8,128)(2,1)} copy-done((bf16[24,3,256,256]{3,2,1,0:T(8,128)(2,1)}, bf16[24,3,256,256]{3,2,1,0:T(8,128)(2,1)S(1)}, u32[]{:S(2)}) %copy-start) | copy-done | bytes 9437208
  62.4 1.6 copy-done.1
  64.0 0.1 select_reduce_fusion.3
  64.1 0.1 select_reduce_fusion.4
  64.2 0.6 compare_select_fusion.3
  64.9 0.0 collective-permute-done.5.x3_ref
  64.9 1.0 copy-done.9
  65.8 1.0 copy-done.10
  66.8 76.4 %experts_up.1 = (bf16[16,128,1408]{2,1,0:T(8,128)(2,1)}, bf16[16,128,1408]{2,1,0:T(8,128)(2,1)}, bf16[16,128,1408]{2,1,0:T(8,128)(2,1)}) custom-call(s32[64]{0:T(128)} %reshape.78.off_ref, s32[16]{0:T(128)} %copy-done.11, s32[16]{0:T(128)} %get-tuple-element.60.at1_ref, s32[16]{0:T(128)} %get-tuple-element.59.at2_ref, bf16[4,1536,256]{2,1,0:T(8,128)(2,1)} %copy-done.1, ...), custom_call_target="tpu_custom_call" | custom-call | flops 35433480192 | bytes 184549376 | tf_op jit(solution)/shard_map/experts_up/pallas_call | solution.py:307
  143.2 38.1 %shard_map.109 = (f32[2,256,1024]{2,1,0:T(8,128)}, f32[2,256,1024]{2,1,0:T(8,128)}) custom-call(s32[64]{0:T(128)} %reshape.78.off_ref, s32[16]{0:T(128)} %copy-done.11, s32[64]{0:T(128)} %reshape.79.queue_off_ref, s32[4]{0:T(128)} %get-tuple-element.41.total_ref, bf16[16,128,1408]{2,1,0:T(8,128)(2,1)} %get-tuple-element.33.h0_hbm, ...), custom_call_target="tpu_custom_call" | custom-call | flops 8858370048 | bytes 46137344 | tf_op jit(solution)/shard_map/pallas_call | solution.py:339
  181.3 0.1 collective-permute-start.6
  181.4 0.0 all-gather.3.cloned.1.call-done
  181.4 0.0 copy-start.13
  181.4 5.6 %collective-permute-done.6 = f32[2,256,1024]{2,1,0:T(8,128)S(1)} collective-permute-done((f32[2,256,1024]{2,1,0:T(8,128)}, f32[2,256,1024]{2,1,0:T(8,128)S(1)}, u32[]{:S(2)}, u32[]{:S(2)}) %collective-permute-start.6) | collective-permute-done | bytes 2097184 | tf_op jit(solution)/shard_map/ppermute | solution.py:235
  187.0 3.1 %fusion.29 = f32[256,1024]{1,0:T(8,128)} fusion(f32[2,256,1024]{2,1,0:T(8,128)S(1)} %collective-permute-done.6, f32[2,256,1024]{2,1,0:T(8,128)} %get-tuple-element.29), kind=kLoop, calls=%fused_computation.27 | loop fusion | flops 262144 | bytes 3145728 | tf_op jit(solution)/shard_map/add | solution.py:372
  190.1 5.2 %fusion.47 = f32[1024,704]{0,1:T(8,128)S(1)} fusion(bf16[1024,2048]{1,0:T(8,128)(2,1)} %all-gather.3.cloned.1.call-done, bf16[2048,704]{0,1:T(8,128)(2,1)S(1)} %copy-done.13), kind=kOutput, calls=%fused_computation.102 | convolution fusion | flops 2952790016 | bytes 9961472 | tf_op jit(solution)/shard_map/dot_general | solution.py:369
  195.3 4.5 %multiply_convert_fusion = bf16[1024,704]{0,1:T(8,128)(2,1)} fusion(f32[1024,704]{0,1:T(8,128)S(1)} %fusion.47, bf16[1024,2048]{1,0:T(8,128)(2,1)S(1)} %copy-done.12, bf16[2048,704]{0,1:T(8,128)(2,1)S(1)} %copy-done.14), kind=kOutput, calls=%fused_computation.8 | convolution fusion | flops 2957115392 | bytes 11403264 | tf_op jit(solution)/shard_map/dot_general | solution.py:370
  199.7 36.2 %shard_map.110 = (f32[2,256,1024]{2,1,0:T(8,128)}, f32[2,256,1024]{2,1,0:T(8,128)}) custom-call(s32[64]{0:T(128)} %reshape.78.off_ref, s32[16]{0:T(128)} %copy-done.11, s32[64]{0:T(128)} %reshape.79.queue_off_ref, s32[4]{0:T(128)} %get-tuple-element.41.total_ref, bf16[16,128,1408]{2,1,0:T(8,128)(2,1)} %get-tuple-element.33.h0_hbm, ...), custom_call_target="tpu_custom_call" | custom-call | flops 8858370048 | bytes 46137344 | tf_op jit(solution)/shard_map/pallas_call | solution.py:339
  235.9 0.1 collective-permute-start.7
  236.0 2.7 copy.21
  238.7 3.8 %all-to-all-start = ((bf16[4,256,704]{1,2,0:T(8,128)(2,1)}), bf16[4,256,704]{1,2,0:T(8,128)(2,1)S(1)}, u32[]{:S(2)}, u32[]{:S(2)}) async-start(bf16[4,256,704]{1,2,0:T(8,128)(2,1)} %bitcast.58), calls=%async_computation | async-start | bytes 2883584 | tf_op jit(solution)/shard_map/all_to_all | solution.py:376
  242.5 0.1 collective-permute-start.8
  242.6 2.3 fusion.28
  244.9 2.0 collective-permute-start.9
  246.9 30.4 %all-to-all-done = bf16[4,256,704]{1,2,0:T(8,128)(2,1)S(1)} async-done(((bf16[4,256,704]{1,2,0:T(8,128)(2,1)}), bf16[4,256,704]{1,2,0:T(8,128)(2,1)S(1)}, u32[]{:S(2)}, u32[]{:S(2)}) %all-to-all-start) | async-done | bytes 1441824 | tf_op jit(solution)/shard_map/all_to_all | solution.py:376
  277.3 3.0 fusion.4
  280.3 3.5 %fusion.8 = f32[256,2048]{1,0:T(8,128)S(1)} fusion(f32[256,2048]{1,0:T(8,128)S(1)} %fusion.4, bf16[2816,2048]{1,0:T(8,128)(2,1)} %all-gather.5.cloned.1.call-done, bf16[4,256,704]{1,2,0:T(8,128)(2,1)S(1)} %all-to-all-done), kind=kOutput, calls=%fused_computation.9 | convolution fusion | flops 738721792 | bytes 7438336 | tf_op jit(solution)/shard_map/dot_general | solution.py:386
  283.8 0.0 copy-start.3
  283.8 1.0 fusion.11
  284.8 0.2 copy-done.3
  285.0 1.0 fusion.17
  286.0 4.9 %collective-permute-done.9 = f32[256,1024]{1,0:T(8,128)} collective-permute-done((f32[256,1024]{1,0:T(8,128)}, f32[256,1024]{1,0:T(8,128)}, u32[]{:S(2)}, u32[]{:S(2)}) %collective-permute-start.9) | collective-permute-done | bytes 1048608 | tf_op jit(solution)/shard_map/ppermute | solution.py:235
  290.9 2.6 fusion.27
  293.5 1.1 pad_maximum_fusion
  (42 shorter events, 0.2 us)
Async XLA Ops:
  6.5 174.9 %all-gather.3.cloned.1.call-start = ((), (), s32[]{:S(2)}) async-start(), calls=%async_computation.1 | async-start | bytes 5242880 | tf_op jit(solution)/shard_map/all_gather | solution.py:362
  7.3 239.7 %all-gather.5.cloned.1.call-start = ((), (), s32[]{:S(2)}) async-start(), calls=%async_computation.2 | async-start | bytes 11894784 | tf_op jit(solution)/shard_map/all_gather | solution.py:383
  12.2 4.7 %collective-permute-start.1 = (f32[16,256]{1,0:T(8,128)S(1)}, f32[16,256]{1,0:T(8,128)S(1)}, u32[]{:S(2)}, u32[]{:S(2)}) collective-permute-start(f32[16,256]{1,0:T(8,128)S(1)} %fusion.34), channel_id=1, source_target_pairs={{0,2},{1,3},{2,0},{3,1},{4,6},{5,7},{6,4},{7,5},{8,10},{9,11},{10,... | collective-permute-start | bytes 49160 | tf_op jit(solution)/shard_map/ppermute | solution.py:235
  15.2 1.7 collective-permute-start
  15.2 25.8 %collective-permute-start.4 = (bf16[256,2048]{1,0:T(8,128)(2,1)}, bf16[256,2048]{1,0:T(8,128)(2,1)S(1)}, u32[]{:S(2)}, u32[]{:S(2)}) collective-permute-start(bf16[256,2048]{1,0:T(8,128)(2,1)} %x0_ref.1), channel_id=1, source_target_pairs={{0,2},{1,3},{2,0},{3,1},{4,6},{5,7},{6,4},{7,5},{8,10},{9,11},{10,... | collective-permute-start | bytes 3145736 | tf_op jit(solution)/shard_map/ppermute | solution.py:235
  15.3 49.5 %collective-permute-start.3 = (bf16[256,2048]{1,0:T(8,128)(2,1)}, bf16[256,2048]{1,0:T(8,128)(2,1)S(1)}, u32[]{:S(2)}, u32[]{:S(2)}) collective-permute-start(bf16[256,2048]{1,0:T(8,128)(2,1)} %x0_ref.1), channel_id=1, source_target_pairs={{0,1},{1,0},{2,3},{3,2},{4,5},{5,4},{6,7},{7,6},{8,9},{9,8},{10,11... | collective-permute-start | bytes 3145736 | tf_op jit(solution)/shard_map/ppermute | solution.py:235
  16.9 1.3 collective-permute-start.2
  19.0 47.8 %copy-start.11 = (s32[16]{0:T(128)}, s32[16]{0:T(128)S(1)}, u32[]{:S(2)}) copy-start(s32[16]{0:T(128)S(1)} %get-tuple-element.42.n_ref) | copy-start | bytes 196
  41.0 17.9 %copy-start.8 = (bf16[256,2048]{1,0:T(8,128)(2,1)}, bf16[256,2048]{1,0:T(8,128)(2,1)S(1)}, u32[]{:S(2)}) copy-start(bf16[256,2048]{1,0:T(8,128)(2,1)S(1)} %collective-permute-done.4.x2_ref) | copy-start | bytes 3145732
  41.0 23.9 %collective-permute-start.5 = (bf16[256,2048]{1,0:T(8,128)(2,1)S(1)}, bf16[256,2048]{1,0:T(8,128)(2,1)S(1)}, u32[]{:S(2)}, u32[]{:S(2)}) collective-permute-start(bf16[256,2048]{1,0:T(8,128)(2,1)S(1)} %collective-permute-done.4.x2_ref), channel_id=1, source_target_pairs={{0,1},{1,0},{2,3},{3,2},{4,5},{5,4},{6,7},{7,6},{8,9},{9,8},{10,11... | collective-permute-start | bytes 3145736 | tf_op jit(solution)/shard_map/ppermute | solution.py:235
  58.9 3.5 %copy-start = (bf16[24,3,256,256]{3,2,1,0:T(8,128)(2,1)}, bf16[24,3,256,256]{3,2,1,0:T(8,128)(2,1)S(1)}, u32[]{:S(2)}) copy-start(bf16[24,3,256,256]{3,2,1,0:T(8,128)(2,1)S(1)} %get-tuple-element.27.gates_hbm) | copy-start | bytes 28311556
  62.4 1.6 copy-start.1
  64.8 1.0 copy-start.9
  65.8 1.0 copy-start.10
  181.3 5.7 %collective-permute-start.6 = (f32[2,256,1024]{2,1,0:T(8,128)}, f32[2,256,1024]{2,1,0:T(8,128)S(1)}, u32[]{:S(2)}, u32[]{:S(2)}) collective-permute-start(f32[2,256,1024]{2,1,0:T(8,128)} %get-tuple-element.30), channel_id=1, source_target_pairs={{0,1},{1,0},{2,3},{3,2},{4,5},{5,4},{6,7},{7,6},{8,9},{9,8},{10,11... | collective-permute-start | bytes 6291464 | tf_op jit(solution)/shard_map/ppermute | solution.py:235
  181.4 8.7 %copy-start.13 = (bf16[2048,704]{0,1:T(8,128)(2,1)S(1)}, bf16[2048,704]{0,1:T(8,128)(2,1)}, u32[]{:S(2)}) copy-start(bf16[2048,704]{0,1:T(8,128)(2,1)} %param.16) | copy-start | bytes 8650756
  187.0 8.3 %copy-start.5 = (f32[2,256,1024]{2,1,0:T(8,128)}, f32[2,256,1024]{2,1,0:T(8,128)S(1)}, u32[]{:S(2)}) copy-start(f32[2,256,1024]{2,1,0:T(8,128)S(1)} %collective-permute-done.6) | copy-start | bytes 6291460
  190.1 5.2 %copy-start.12 = (bf16[1024,2048]{1,0:T(8,128)(2,1)S(1)}, bf16[1024,2048]{1,0:T(8,128)(2,1)}, u32[]{:S(2)}) copy-start(bf16[1024,2048]{1,0:T(8,128)(2,1)} %all-gather.3.cloned.1.call-done) | copy-start | bytes 12582916
  190.1 5.2 %copy-start.14 = (bf16[2048,704]{0,1:T(8,128)(2,1)S(1)}, bf16[2048,704]{0,1:T(8,128)(2,1)}, u32[]{:S(2)}) copy-start(bf16[2048,704]{0,1:T(8,128)(2,1)} %param.17) | copy-start | bytes 8650756
  235.9 6.7 %collective-permute-start.7 = (f32[2,256,1024]{2,1,0:T(8,128)}, f32[2,256,1024]{2,1,0:T(8,128)}, u32[]{:S(2)}, u32[]{:S(2)}) collective-permute-start(f32[2,256,1024]{2,1,0:T(8,128)} %get-tuple-element.37), channel_id=1, source_target_pairs={{0,1},{1,0},{2,3},{3,2},{4,5},{5,4},{6,7},{7,6},{8,9},{9,8},{10,11... | collective-permute-start | bytes 6291464 | tf_op jit(solution)/shard_map/ppermute | solution.py:235
  236.0 6.6 %copy-start.7 = (f32[2,256,1024]{2,1,0:T(8,128)S(1)}, f32[2,256,1024]{2,1,0:T(8,128)}, u32[]{:S(2)}) copy-start(f32[2,256,1024]{2,1,0:T(8,128)} %get-tuple-element.36) | copy-start | bytes 6291460
  238.7 38.6 %all-to-all-start = ((bf16[4,256,704]{1,2,0:T(8,128)(2,1)}), bf16[4,256,704]{1,2,0:T(8,128)(2,1)S(1)}, u32[]{:S(2)}, u32[]{:S(2)}) async-start(bf16[4,256,704]{1,2,0:T(8,128)(2,1)} %bitcast.58), calls=%async_computation | async-start | bytes 2883584 | tf_op jit(solution)/shard_map/all_to_all | solution.py:376
  242.5 43.5 %collective-permute-start.8 = (f32[256,1024]{1,0:T(8,128)}, f32[256,1024]{1,0:T(8,128)}, u32[]{:S(2)}, u32[]{:S(2)}) collective-permute-start(f32[256,1024]{1,0:T(8,128)} %fusion.29), channel_id=1, source_target_pairs={{0,2},{1,3},{2,0},{3,1},{4,6},{5,7},{6,4},{7,5},{8,10},{9,11},{10,... | collective-permute-start | bytes 3145736 | tf_op jit(solution)/shard_map/ppermute | solution.py:235
  244.9 46.0 %collective-permute-start.9 = (f32[256,1024]{1,0:T(8,128)}, f32[256,1024]{1,0:T(8,128)}, u32[]{:S(2)}, u32[]{:S(2)}) collective-permute-start(f32[256,1024]{1,0:T(8,128)} %fusion.28), channel_id=1, source_target_pairs={{0,2},{1,3},{2,0},{3,1},{4,6},{5,7},{6,4},{7,5},{8,10},{9,11},{10,... | collective-permute-start | bytes 3145736 | tf_op jit(solution)/shard_map/ppermute | solution.py:235
  277.3 6.4 %copy-start.2 = (bf16[2816,2048]{1,0:T(8,128)(2,1)S(1)}, bf16[2816,2048]{1,0:T(8,128)(2,1)}, u32[]{:S(2)}) copy-start(bf16[2816,2048]{1,0:T(8,128)(2,1)} %all-gather.5.cloned.1.call-done) | copy-start | bytes 34603012
  283.8 1.2 copy-start.3
  285.0 5.9 %copy-start.4 = (f32[2,256,1024]{2,1,0:T(8,128)S(1)}, f32[2,256,1024]{2,1,0:T(8,128)}, u32[]{:S(2)}) copy-start(f32[2,256,1024]{2,1,0:T(8,128)} %get-tuple-element.29) | copy-start | bytes 6291460
  285.0 5.9 %copy-start.6 = (f32[2,256,1024]{2,1,0:T(8,128)S(1)}, f32[2,256,1024]{2,1,0:T(8,128)}, u32[]{:S(2)}) copy-start(f32[2,256,1024]{2,1,0:T(8,128)} %copy-done.5) | copy-start | bytes 6291460
Sparse Core Ops, SparseCore 0:
  8.9 83.4 all-gather.2
  95.2 90.7 all-gather.4

commit v4 on v3

--- a/solution.py
+++ b/solution.py
@@ -10,7 +10,8 @@
 
 CAP_FACTOR = 4
 GROUP = 4
-COLUMN_CHUNKS = 2
+COLUMN_SHARES = (3, 1)
+TOKEN_SHARES = (1, 2, 1)
 ROW_PIECE = 128
 UP_SLOTS = 3
 DOWN_SLOTS = 4
@@ -22,7 +23,7 @@
 
 
 def row_sizes(rows):
-    return [size for size in (128, 256) if size < rows] + [rows]
+    return [size for size in (64, 128, 256) if size < rows] + [rows]
 
 
 def pick_rows(n_rows, rows, body):
@@ -70,13 +71,14 @@
     lax.fori_loop(0, gates_ref.shape[0], tile, 0)
 
 
-def up_kernel(cap, off_ref, n_ref, at1_ref, at2_ref, pick_ref, x0_ref, x1_ref, x2_ref, x3_ref, w1_hbm, w3_hbm, h0_ref, h1_ref, h2_ref, rows_ref, w1_ring, w3_ring, sems):
+def up_kernel(cap, off_ref, n_ref, at1_ref, at2_ref, pick_ref, x0_ref, x1_ref, x2a_ref, x2b_ref, x2c_ref, x3a_ref, x3b_ref, x3c_ref, w1_hbm, w3_hbm, h0_ref, h1_ref, h2_ref, rows_ref, w1_ring, w3_ring, sems):
     step = pl.program_id(0)
     n_steps = pl.num_programs(0)
     d_model = x0_ref.shape[1]
     d_ff = w1_ring.shape[2]
     n_slots = w1_ring.shape[0]
-    x_refs = (x0_ref, x1_ref, x2_ref, x3_ref)
+    x_refs = ((x0_ref,), (x1_ref,), (x2a_ref, x2b_ref, x2c_ref), (x3a_ref, x3b_ref, x3c_ref))
+    piece_step = min(512, d_model // sum(TOKEN_SHARES))
     h_refs = (h0_ref, h1_ref, h2_ref)
 
     def fetch(expert):
@@ -101,13 +103,16 @@
 
     @pl.when(step % GROUP == 0)
     def _():
-        for src, x_ref in enumerate(x_refs):
+        for src, pieces in enumerate(x_refs):
             chosen = pick_ref[src]
-            for begin, size in column_pieces(d_model, 512):
-                got = jnp.dot(chosen, x_ref[:, begin : begin + size], preferred_element_type=jnp.float32).astype(jnp.bfloat16)
-                for part in range(GROUP):
-                    at = pl.multiple_of(off_ref[(step + part) * 4 + src], 16)
-                    rows_ref[part, pl.ds(at, cap), begin : begin + size] = got[part * cap : (part + 1) * cap]
+            base = 0
+            for x_ref in pieces:
+                for begin, size in column_pieces(x_ref.shape[1], piece_step):
+                    got = jnp.dot(chosen, x_ref[:, begin : begin + size], preferred_element_type=jnp.float32).astype(jnp.bfloat16)
+                    for part in range(GROUP):
+                        at = pl.multiple_of(off_ref[(step + part) * 4 + src], 16)
+                        rows_ref[part, pl.ds(at, cap), base + begin : base + begin + size] = got[part * cap : (part + 1) * cap]
+                base += x_ref.shape[1]
 
     part = step % GROUP
     slot = step % n_slots
@@ -118,8 +123,9 @@
         x = rows_ref[part, :size, :]
 
         def put(value, begin, width):
-            for piece in range(size // ROW_PIECE):
-                h_refs[piece][0, :, begin : begin + width] = value[piece * ROW_PIECE : (piece + 1) * ROW_PIECE]
+            for piece in range(-(-size // ROW_PIECE)):
+                part_rows = min(size - piece * ROW_PIECE, ROW_PIECE)
+                h_refs[piece][0, :part_rows, begin : begin + width] = value[piece * ROW_PIECE : piece * ROW_PIECE + part_rows]
 
         full = d_ff // 256 * 256
         for begin, width in column_pieces(full, 512):
@@ -183,7 +189,14 @@
     for src in range(4):
         at = pl.multiple_of(off_ref[step * 4 + src], 16)
         to = pl.multiple_of(queue_off_ref[src * n_local + step], 16)
-        queue_ref[src, pl.ds(to, cap), :] = out_ref[pl.ds(at, cap), :]
+        end = off_ref[step * 4 + src + 1] if src < 3 else n_ref[step]
+
+        def keep(size, at=at, to=to, src=src):
+            queue_ref[src, pl.ds(to, size), :] = out_ref[pl.ds(at, size), :]
+
+        few = min(32, cap)
+        pl.when(end - at <= few)(functools.partial(keep, few))
+        pl.when(end - at > few)(functools.partial(keep, cap))
 
     @pl.when(step == n_local - 1)
     def _():
@@ -234,9 +247,13 @@
         def swap(value, bit):
             return lax.ppermute(value, "ep", [(i, i ^ bit) for i in range(ep_size)])
 
-        x_far = swap(tokens, 2)
+        x_far, x_far_sib, begin = [], [], 0
+        for share in TOKEN_SHARES:
+            size = d_model * share // sum(TOKEN_SHARES)
+            x_far.append(swap(tokens[:, begin : begin + size], 2))
+            x_far_sib.append(swap(x_far[-1], 1))
+            begin += size
         x_sib = swap(tokens, 1)
-        x_far_sib = swap(x_far, 1)
         all_ids = jnp.arange(n_exp, dtype=jnp.int32)
         row_limit = jnp.sum(jnp.where(expert_ids[:, :, None] == all_ids, send_counts[0], 0), axis=-1)
         kept_mask = (slot_ids >= 0) & (slot_ids < row_limit)
@@ -294,8 +311,8 @@
                 pl.BlockSpec((n_tiles, 3, n_tok, 256), lambda s: (s, 0, 0, 0)),
             ],
             out_shape=[
-                jax.ShapeDtypeStruct((4, n_queue, n_tok), jnp.bfloat16),
-                jax.ShapeDtypeStruct((4 * n_tiles, 3, n_tok, 256), jnp.bfloat16),
+                pltpu.HBM((4, n_queue, n_tok), jnp.bfloat16),
+                pltpu.HBM((4 * n_tiles, 3, n_tok, 256), jnp.bfloat16),
             ],
             compiler_params=pltpu.CompilerParams(dimension_semantics=("arbitrary",), vmem_limit_bytes=40_000_000),
             cost_estimate=pl.CostEstimate(flops=10**9, bytes_accessed=4 * n_queue * n_tok * 8, transcendentals=0),
@@ -311,7 +328,7 @@
                 grid=(n_local,),
                 in_specs=[
                     pl.BlockSpec((4, GROUP * cap, n_tok), lambda e, *_: (0, e // GROUP, 0)),
-                    *[pl.BlockSpec((n_tok, d_model), lambda e, *_: (0, 0), **whole) for _ in range(4)],
+                    *[pl.BlockSpec(x.shape, lambda e, *_: (0, 0), **whole) for x in (tokens, x_sib, *x_far, *x_far_sib)],
                     any_space,
                     any_space,
                 ],
@@ -331,13 +348,16 @@
             compiler_params=pltpu.CompilerParams(dimension_semantics=("arbitrary",), vmem_limit_bytes=VMEM_LIMIT),
             cost_estimate=pl.CostEstimate(flops=4 * n_local * 192 * d_model * d_ff, bytes_accessed=4 * n_local * d_model * d_ff, transcendentals=0),
             name="experts_up",
-        )(off, n_rows, at1, at2, pick, tokens, x_sib, x_far, x_far_sib, expert_w1, expert_w3)
-
-        n_cols = d_model // COLUMN_CHUNKS
+        )(off, n_rows, at1, at2, pick, tokens, x_sib, *x_far, *x_far_sib, expert_w1, expert_w3)
+
+        widths = [d_model * share // sum(COLUMN_SHARES) for share in COLUMN_SHARES]
+        starts = [sum(widths[:chunk]) for chunk in range(len(widths))]
 
         def down(chunk, held):
+            n_cols = widths[chunk]
+            slots = 3 if n_cols > d_model // 2 else DOWN_SLOTS
             return pl.pallas_call(
-                functools.partial(down_kernel, cap, chunk * n_cols),
+                functools.partial(down_kernel, cap, starts[chunk]),
                 grid_spec=pltpu.PrefetchScalarGridSpec(
                     num_scalar_prefetch=4,
                     grid=(n_local,),
@@ -346,11 +366,11 @@
                     scratch_shapes=[
                         pltpu.VMEM((rows, n_cols), jnp.bfloat16),
                         pltpu.VMEM((4, n_queue, n_cols), jnp.bfloat16),
-                        pltpu.VMEM((DOWN_SLOTS, d_ff, n_cols), jnp.bfloat16),
-                        pltpu.VMEM((DOWN_SLOTS, rows, d_ff), jnp.bfloat16),
+                        pltpu.VMEM((slots, d_ff, n_cols), jnp.bfloat16),
+                        pltpu.VMEM((slots, rows, d_ff), jnp.bfloat16),
                         pltpu.VMEM(gate_tiles.shape, jnp.bfloat16),
-                        pltpu.SemaphoreType.DMA((DOWN_SLOTS,)),
-                        pltpu.SemaphoreType.DMA((3, DOWN_SLOTS)),
+                        pltpu.SemaphoreType.DMA((slots,)),
+                        pltpu.SemaphoreType.DMA((3, slots)),
                         pltpu.SemaphoreType.DMA((4 * n_tiles,)),
                     ],
                 ),
@@ -361,21 +381,20 @@
 
         gathered = lax.all_gather(tokens, "tp", axis=0, tiled=True)
         sums_own, sums_sib, returned = [], [], []
-        for chunk in range(COLUMN_CHUNKS):
+        for chunk in range(len(widths)):
             own, sib = down(chunk, hidden)
             from_sib = swap(sib, 1)
+            passed_on = own[1] + from_sib[1]
+            returned.append(swap(passed_on, 2))
+            sums_own.append(own[0])
+            sums_sib.append(from_sib[0])
             if chunk == 0:
-                gathered, own = lax.optimization_barrier((gathered, own))
+                gathered, passed_on = lax.optimization_barrier((gathered, passed_on))
                 pre_gate = jnp.dot(gathered, shared_w1, preferred_element_type=jnp.float32)
                 pre_up = jnp.dot(gathered, shared_w3, preferred_element_type=jnp.float32)
                 shared_hidden = (jax.nn.silu(pre_gate) * pre_up).astype(jnp.bfloat16)
-            passed_on = own[1] + from_sib[1]
-            passed_on, shared_hidden, *hidden = lax.optimization_barrier((passed_on, shared_hidden, *hidden))
-            returned.append(swap(passed_on, 2))
-            if chunk == 0:
+                shared_hidden, *hidden = lax.optimization_barrier((shared_hidden, *hidden))
                 hidden_blocks = lax.all_to_all(shared_hidden.reshape(mesh.shape["tp"], n_tok, -1), "tp", 0, 0)
-            sums_own.append(own[0])
-            sums_sib.append(from_sib[0])
 
         width = shared_w2.shape[0]
         rep = lax.axis_index("data") * ep_size + me
@@ -388,9 +407,9 @@
             shared_out += jnp.dot(hidden_blocks[block], w2_blocks[block], preferred_element_type=jnp.float32)
         base = tokens.astype(jnp.float32) + shared_out
         parts = []
-        for chunk in range(COLUMN_CHUNKS):
+        for chunk, (first, n_cols) in enumerate(zip(starts, widths)):
             routed = sums_own[chunk] + sums_sib[chunk] + returned[chunk]
-            parts.append((base[:, chunk * n_cols : (chunk + 1) * n_cols] + routed).astype(jnp.bfloat16))
+            parts.append((base[:, first : first + n_cols] + routed).astype(jnp.bfloat16))
         return jnp.concatenate(parts, axis=1)
 
 

time: 302 us -> 299 us (0.990)
  local copies, waits for them, and re-layouts: 13.3 us -> 8.89 us
    all_to_all x1, waiting for transfers between devices: 30.4 us -> 6.33 us  [layer_body(): lax.all_to_all(shared_hidden.reshape(mesh.shape['tp'], n_tok, -1), 'tp',...]
    ppermute x10 -> x14, waiting for transfers between devices: 34.3 us -> 56.2 us  [swap(): return lax.ppermute(value, 'ep', [(i, i ^ bit) for i in range(ep_size)])]
    unnamed x30 -> x34, local copies, waits for them, and re-layouts: 7.36 us -> 2.66 us
    ppermute x10 -> x14, starting transfers between devices: 5.73 us -> 6.64 us  [swap(): return lax.ppermute(value, 'ep', [(i, i ^ bit) for i in range(ep_size)])]
  transfers between devices with their start and end apart: 13 -> 17, of which waited for: 6 -> 7; matrix products, arithmetic and copies ran while one was open for 12% -> 12% of each run, Pallas kernels for 54% -> 56%
where the time goes in v4:
time: 299 us
  Pallas kernels  166 us (56%)
  waiting for transfers between devices  63.3 us (21%)
  matrix products  19.4 us (6%)
  between operations  16.3 us (5%)
  other arithmetic  12.8 us (4%)
  starting transfers between devices  11.5 us (4%)
  local copies, waits for them, and re-layouts  8.89 us (3%)
    pallas_call x1, Pallas kernels, layer_body(): pl.pallas_call(functools.partial(up_kernel, cap), grid_spec=pltpu.Prefetc...  76.5 us
    pallas_call x2, Pallas kernels, down(): pl.pallas_call(functools.partial(down_kernel, cap, starts[chunk]), grid_s...  75.3 us
    ppermute x14, waiting for transfers between devices, swap(): return lax.ppermute(value, 'ep', [(i, i ^ bit) for i in range(ep_size)])  56.2 us
    pallas_call x1, Pallas kernels, layer_body(): pl.pallas_call(prep_kernel, grid=(4,), in_specs=[pl.BlockSpec((1, 16, n_t...  14.7 us
    dot_general x3, matrix products, layer_body(): jnp.dot(hidden_blocks[block], w2_blocks[block], preferred_element_type=jn...  7.32 us
    ppermute x14, starting transfers between devices, swap(): return lax.ppermute(value, 'ep', [(i, i ^ bit) for i in range(ep_size)])  6.64 us
    all_to_all x1, waiting for transfers between devices, layer_body(): lax.all_to_all(shared_hidden.reshape(mesh.shape['tp'], n_tok, -1), 'tp',...  6.33 us
  transfers between devices with their start and end apart: 17, of which 7 were waited for; matrix products, arithmetic and copies ran while one was open for 12% of the time, Pallas kernels for 56%

profile of v4, /device:TPU:0, one launch (start us, length us, event | category | flops | bytes accessed | tf_op | source)
XLA Modules:
  0.0 298.7 jit_solution(9465445572489404365)
XLA Ops:
  6.5 0.7 all-gather.3.cloned.1.call-update
  7.3 0.0 all-gather.5.cloned.1.call-start
  7.3 1.8 constant_dynamic-slice_fusion
  9.1 0.7 convert_element_type.30
  9.8 0.1 pad.21.clone
  9.8 0.8 select_reduce_fusion.1
  10.7 0.7 convert_bitcast_fusion
  11.4 0.7 select_bitcast_fusion
  12.1 0.1 fusion.34
  12.2 3.0 %collective-permute-start.1 = (f32[16,256]{1,0:T(8,128)S(1)}, f32[16,256]{1,0:T(8,128)S(1)}, u32[]{:S(2)}, u32[]{:S(2)}) collective-permute-start(f32[16,256]{1,0:T(8,128)S(1)} %fusion.34), channel_id=1, source_target_pairs={{0,2},{1,3},{2,0},{3,1},{4,6},{5,7},{6,4},{7,5},{8,10},{9,11},{10,... | collective-permute-start | bytes 49160 | tf_op jit(solution)/shard_map/ppermute | solution.py:248
  15.2 0.5 collective-permute-start.3
  15.7 1.8 fusion.47
  17.5 0.1 collective-permute-start.4
  17.5 1.9 collective-permute-start.6
  19.5 0.1 fusion.53
  19.6 0.1 collective-permute-start.2
  19.7 0.1 collective-permute-start.5
  19.9 0.9 collective-permute-done.2
  20.8 0.1 fusion.43
  20.9 0.1 select_reduce_fusion.2
  21.1 0.6 fusion.45
  21.7 0.1 select_reduce_fusion.5
  21.9 0.2 select_reduce_fusion
  22.0 0.1 select_reduce_fusion.3
  22.2 0.1 select_reduce_fusion.4
  22.3 20.4 %collective-permute-done.5.x2b_ref = bf16[256,1024]{1,0:T(8,128)(2,1)S(1)} collective-permute-done((bf16[256,1024]{1,0:T(8,128)(2,1)S(1)}, bf16[256,1024]{1,0:T(8,128)(2,1)S(1)}, u32[]{:S(2)}, u32[]{:S(2)}) %collective-permute-start.5) | collective-permute-done | bytes 524320 | tf_op jit(solution)/shard_map/ppermute | solution.py:248
  42.8 0.7 select_reduce_fusion.6
  43.5 0.5 collective-permute-start.7
  44.0 0.1 collective-permute-start.9
  44.1 14.7 %prep.1 = (bf16[4,1536,256]{2,1,0:T(8,128)(2,1)}, bf16[24,3,256,256]{3,2,1,0:T(8,128)(2,1)}) custom-call(s32[4,16,256]{2,1,0:T(8,128)S(1)} %pad_add_fusion.facts_ref, f32[3,4,6,256]{3,2,1,0:T(8,128)S(1)} %pad_maximum_fusion.1.gates_in_ref), custom_call_target="tpu_custom_call" | custom-call | flops 1000000000 | bytes 12582912 | tf_op jit(solution)/shard_map/prep/pallas_call | solution.py:302
  58.8 0.7 reshape.79.queue_off_ref
  62.0 0.1 copy.17
  62.0 0.6 reshape.78.off_ref
  62.7 0.5 compare_select_fusion.3
  63.2 0.8 copy-done.8
  64.1 0.0 copy-done.11
  64.1 0.1 copy-done.12
  64.2 76.5 %experts_up.1 = (bf16[16,128,1408]{2,1,0:T(8,128)(2,1)}, bf16[16,128,1408]{2,1,0:T(8,128)(2,1)}, bf16[16,128,1408]{2,1,0:T(8,128)(2,1)}) custom-call(s32[64]{0:T(128)} %reshape.78.off_ref, s32[16]{0:T(128)} %copy-done.13, s32[16]{0:T(128)} %get-tuple-element.54.at1_ref, s32[16]{0:T(128)} %get-tuple-element.53.at2_ref, ...), custom_call_target="tpu_custom_call" | custom-call | flops 35433480192 | bytes 184549376 | tf_op jit(solution)/shard_map/experts_up/pallas_call | solution.py:324
  140.7 51.2 %shard_map.109 = (f32[2,256,1536]{2,1,0:T(8,128)}, f32[2,256,1536]{2,1,0:T(8,128)}) custom-call(s32[64]{0:T(128)} %reshape.78.off_ref, s32[16]{0:T(128)} %copy-done.13, s32[64]{0:T(128)} %reshape.79.queue_off_ref, s32[4]{0:T(128)} %get-tuple-element.35.total_ref, bf16[16,128,1408]{2,1,0:T(8,128)(2,1)} %get-tuple-element.29.h0_hbm, ...), custom_call_target="tpu_custom_call" | custom-call | flops 13287555072 | bytes 69206016 | tf_op jit(solution)/shard_map/pallas_call | solution.py:359
  192.0 0.1 collective-permute-start.10
  192.0 5.9 %collective-permute-done.10 = f32[2,256,1536]{2,1,0:T(8,128)S(1)} collective-permute-done((f32[2,256,1536]{2,1,0:T(8,128)}, f32[2,256,1536]{2,1,0:T(8,128)S(1)}, u32[]{:S(2)}, u32[]{:S(2)}) %collective-permute-start.10) | collective-permute-done | bytes 3145760 | tf_op jit(solution)/shard_map/ppermute | solution.py:248
  197.9 1.7 copy-done.4
  199.6 2.8 fusion.24
  202.4 5.1 %fusion.48 = f32[1024,704]{0,1:T(8,128)S(1)} fusion(bf16[1024,2048]{1,0:T(8,128)(2,1)} %all-gather.3.cloned.1.call-done, bf16[2048,704]{0,1:T(8,128)(2,1)S(1)} %copy-done.15), kind=kOutput, calls=%fused_computation.103 | convolution fusion | flops 2952790016 | bytes 9961472 | tf_op jit(solution)/shard_map/dot_general | solution.py:393
  207.6 3.4 %multiply_convert_fusion = bf16[1024,704]{0,1:T(8,128)(2,1)S(1)} fusion(f32[1024,704]{0,1:T(8,128)S(1)} %fusion.48, bf16[1024,2048]{1,0:T(8,128)(2,1)S(1)} %copy-done.14, bf16[2048,704]{0,1:T(8,128)(2,1)S(1)} %copy-done.16), kind=kOutput, calls=%fused_computation.8 | convolution fusion | flops 2957115392 | bytes 11403264 | tf_op jit(solution)/shard_map/dot_general | solution.py:394
  211.0 1.2 copy.21
  212.1 4.8 %all-to-all-start = ((bf16[4,256,704]{1,2,0:T(8,128)(2,1)}), bf16[4,256,704]{1,2,0:T(8,128)(2,1)}, u32[]{:S(2)}, u32[]{:S(2)}) async-start(bf16[4,256,704]{1,2,0:T(8,128)(2,1)} %bitcast.58), calls=%async_computation | async-start | bytes 2883584 | tf_op jit(solution)/shard_map/all_to_all | solution.py:397
  217.0 24.0 %shard_map.110 = (f32[2,256,512]{2,1,0:T(8,128)}, f32[2,256,512]{2,1,0:T(8,128)}) custom-call(s32[64]{0:T(128)} %reshape.78.off_ref, s32[16]{0:T(128)} %copy-done.13, s32[64]{0:T(128)} %reshape.79.queue_off_ref, s32[4]{0:T(128)} %get-tuple-element.35.total_ref, bf16[16,128,1408]{2,1,0:T(8,128)(2,1)} %get-tuple-element.29.h0_hbm, ...), custom_call_target="tpu_custom_call" | custom-call | flops 4429185024 | bytes 23068672 | tf_op jit(solution)/shard_map/pallas_call | solution.py:359
  241.0 0.1 collective-permute-start.11
  241.1 0.1 collective-permute-start.12
  241.2 2.8 collective-permute-done.11
  244.0 1.1 fusion.29
  245.1 0.1 collective-permute-start.13
  245.2 0.0 all-gather.5.cloned.1.call-done
  245.2 6.3 %all-to-all-done = bf16[4,256,704]{1,2,0:T(8,128)(2,1)} async-done(((bf16[4,256,704]{1,2,0:T(8,128)(2,1)}), bf16[4,256,704]{1,2,0:T(8,128)(2,1)}, u32[]{:S(2)}, u32[]{:S(2)}) %all-to-all-start) | async-done | bytes 1441824 | tf_op jit(solution)/shard_map/all_to_all | solution.py:397
  251.5 3.1 %fusion.4 = f32[256,2048]{1,0:T(8,128)S(1)} fusion(bf16[2816,2048]{1,0:T(8,128)(2,1)} %all-gather.5.cloned.1.call-done, bf16[4,256,704]{1,2,0:T(8,128)(2,1)} %all-to-all-done), kind=kOutput, calls=%fused_computation.4 | convolution fusion | flops 738197504 | bytes 5341184 | tf_op jit(solution)/shard_map/dot_general | solution.py:407
  254.6 3.6 %fusion.8 = f32[256,2048]{1,0:T(8,128)S(1)} fusion(f32[256,2048]{1,0:T(8,128)S(1)} %fusion.4, bf16[2816,2048]{1,0:T(8,128)(2,1)} %all-gather.5.cloned.1.call-done, bf16[4,256,704]{1,2,0:T(8,128)(2,1)} %all-to-all-done), kind=kOutput, calls=%fused_computation.9 | convolution fusion | flops 738721792 | bytes 7438336 | tf_op jit(solution)/shard_map/dot_general | solution.py:405
  258.2 2.1 fusion.11
  260.3 2.2 fusion.17
  262.5 16.1 %collective-permute-done.12 = f32[256,1536]{1,0:T(8,128)S(1)} collective-permute-done((f32[256,1536]{1,0:T(8,128)}, f32[256,1536]{1,0:T(8,128)S(1)}, u32[]{:S(2)}, u32[]{:S(2)}) %collective-permute-start.12) | collective-permute-done | bytes 1572896 | tf_op jit(solution)/shard_map/ppermute | solution.py:248
  278.7 0.7 fusion.23
  279.4 10.1 %collective-permute-done.13 = f32[256,512]{1,0:T(8,128)} collective-permute-done((f32[256,512]{1,0:T(8,128)S(1)}, f32[256,512]{1,0:T(8,128)}, u32[]{:S(2)}, u32[]{:S(2)}) %collective-permute-start.13) | collective-permute-done | bytes 524320 | tf_op jit(solution)/shard_map/ppermute | solution.py:248
  289.5 1.2 fusion.28
  290.7 1.1 pad_maximum_fusion
  (57 shorter events, 0.3 us)
Async XLA Ops:
  6.5 13.1 %copy-start = (bf16[256,2048]{1,0:T(8,128)(2,1)S(1)}, bf16[256,2048]{1,0:T(8,128)(2,1)}, u32[]{:S(2)}) copy-start(bf16[256,2048]{1,0:T(8,128)(2,1)} %x0_ref.1) | copy-start | bytes 3145732
  6.5 195.9 %all-gather.3.cloned.1.call-start = ((), (), s32[]{:S(2)}) async-start(), calls=%async_computation.1 | async-start | bytes 5242880 | tf_op jit(solution)/shard_map/all_gather | solution.py:382
  7.3 237.9 %all-gather.5.cloned.1.call-start = ((), (), s32[]{:S(2)}) async-start(), calls=%async_computation.2 | async-start | bytes 11894784 | tf_op jit(solution)/shard_map/all_gather | solution.py:402
  12.2 7.4 %collective-permute-start.1 = (f32[16,256]{1,0:T(8,128)S(1)}, f32[16,256]{1,0:T(8,128)S(1)}, u32[]{:S(2)}, u32[]{:S(2)}) collective-permute-start(f32[16,256]{1,0:T(8,128)S(1)} %fusion.34), channel_id=1, source_target_pairs={{0,2},{1,3},{2,0},{3,1},{4,6},{5,7},{6,4},{7,5},{8,10},{9,11},{10,... | collective-permute-start | bytes 49160 | tf_op jit(solution)/shard_map/ppermute | solution.py:248
  15.2 4.5 %collective-permute-start = (f32[16,256]{1,0:T(8,128)S(1)}, f32[16,256]{1,0:T(8,128)S(1)}, u32[]{:S(2)}, u32[]{:S(2)}) collective-permute-start(f32[16,256]{1,0:T(8,128)S(1)} %fusion.34), channel_id=1, source_target_pairs={{0,1},{1,0},{2,3},{3,2},{4,5},{5,4},{6,7},{7,6},{8,9},{9,8},{10,11... | collective-permute-start | bytes 49160 | tf_op jit(solution)/shard_map/ppermute | solution.py:248
  15.2 48.9 %collective-permute-start.3 = (bf16[256,2048]{1,0:T(8,128)(2,1)}, bf16[256,2048]{1,0:T(8,128)(2,1)}, u32[]{:S(2)}, u32[]{:S(2)}) collective-permute-start(bf16[256,2048]{1,0:T(8,128)(2,1)} %x0_ref.1), channel_id=1, source_target_pairs={{0,1},{1,0},{2,3},{3,2},{4,5},{5,4},{6,7},{7,6},{8,9},{9,8},{10,11... | collective-permute-start | bytes 3145736 | tf_op jit(solution)/shard_map/ppermute | solution.py:248
  17.5 26.0 %collective-permute-start.4 = (bf16[256,512]{1,0:T(8,128)(2,1)}, bf16[256,512]{1,0:T(8,128)(2,1)S(1)}, u32[]{:S(2)}, u32[]{:S(2)}) collective-permute-start(bf16[256,512]{1,0:T(8,128)(2,1)} %get-tuple-element.47), channel_id=1, source_target_pairs={{0,2},{1,3},{2,0},{3,1},{4,6},{5,7},{6,4},{7,5},{8,10},{9,11},{10,... | collective-permute-start | bytes 786440 | tf_op jit(solution)/shard_map/ppermute | solution.py:248
  17.5 26.5 %collective-permute-start.6 = (bf16[256,512]{1,0:T(8,128)(2,1)S(1)}, bf16[256,512]{1,0:T(8,128)(2,1)S(1)}, u32[]{:S(2)}, u32[]{:S(2)}) collective-permute-start(bf16[256,512]{1,0:T(8,128)(2,1)S(1)} %get-tuple-element.46), channel_id=1, source_target_pairs={{0,2},{1,3},{2,0},{3,1},{4,6},{5,7},{6,4},{7,5},{8,10},{9,11},{10,... | collective-permute-start | bytes 786440 | tf_op jit(solution)/shard_map/ppermute | solution.py:248
  19.6 1.2 collective-permute-start.2
  19.7 23.0 %collective-permute-start.5 = (bf16[256,1024]{1,0:T(8,128)(2,1)S(1)}, bf16[256,1024]{1,0:T(8,128)(2,1)S(1)}, u32[]{:S(2)}, u32[]{:S(2)}) collective-permute-start(bf16[256,1024]{1,0:T(8,128)(2,1)S(1)} %slice.80), channel_id=1, source_target_pairs={{0,2},{1,3},{2,0},{3,1},{4,6},{5,7},{6,4},{7,5},{8,10},{9,11},{10,... | collective-permute-start | bytes 1572872 | tf_op jit(solution)/shard_map/ppermute | solution.py:248
  21.7 42.5 %copy-start.13 = (s32[16]{0:T(128)}, s32[16]{0:T(128)S(1)}, u32[]{:S(2)}) copy-start(s32[16]{0:T(128)S(1)} %get-tuple-element.36.n_ref) | copy-start | bytes 196
  42.7 21.4 %copy-start.7 = (bf16[256,1024]{1,0:T(8,128)(2,1)}, bf16[256,1024]{1,0:T(8,128)(2,1)S(1)}, u32[]{:S(2)}) copy-start(bf16[256,1024]{1,0:T(8,128)(2,1)S(1)} %collective-permute-done.5.x2b_ref) | copy-start | bytes 1572868
  42.7 20.5 %collective-permute-start.8 = (bf16[256,1024]{1,0:T(8,128)(2,1)S(1)}, bf16[256,1024]{1,0:T(8,128)(2,1)S(1)}, u32[]{:S(2)}, u32[]{:S(2)}) collective-permute-start(bf16[256,1024]{1,0:T(8,128)(2,1)S(1)} %collective-permute-done.5.x2b_ref), channel_id=1, source_target_pairs={{0,1},{1,0},{2,3},{3,2},{4,5},{5,4},{6,7},{7,6},{8,9},{9,8},{10,11... | collective-permute-start | bytes 1572872 | tf_op jit(solution)/shard_map/ppermute | solution.py:248
  43.5 20.7 %copy-start.9 = (bf16[256,512]{1,0:T(8,128)(2,1)}, bf16[256,512]{1,0:T(8,128)(2,1)S(1)}, u32[]{:S(2)}) copy-start(bf16[256,512]{1,0:T(8,128)(2,1)S(1)} %collective-permute-done.4.x2a_ref) | copy-start | bytes 786436
  43.5 19.7 %collective-permute-start.7 = (bf16[256,512]{1,0:T(8,128)(2,1)S(1)}, bf16[256,512]{1,0:T(8,128)(2,1)S(1)}, u32[]{:S(2)}, u32[]{:S(2)}) collective-permute-start(bf16[256,512]{1,0:T(8,128)(2,1)S(1)} %collective-permute-done.4.x2a_ref), channel_id=1, source_target_pairs={{0,1},{1,0},{2,3},{3,2},{4,5},{5,4},{6,7},{7,6},{8,9},{9,8},{10,11... | collective-permute-start | bytes 786440 | tf_op jit(solution)/shard_map/ppermute | solution.py:248
  44.0 20.0 %copy-start.10 = (bf16[256,512]{1,0:T(8,128)(2,1)}, bf16[256,512]{1,0:T(8,128)(2,1)S(1)}, u32[]{:S(2)}) copy-start(bf16[256,512]{1,0:T(8,128)(2,1)S(1)} %collective-permute-done.6.x2c_ref) | copy-start | bytes 786436
  44.0 19.2 %collective-permute-start.9 = (bf16[256,512]{1,0:T(8,128)(2,1)S(1)}, bf16[256,512]{1,0:T(8,128)(2,1)S(1)}, u32[]{:S(2)}, u32[]{:S(2)}) collective-permute-start(bf16[256,512]{1,0:T(8,128)(2,1)S(1)} %collective-permute-done.6.x2c_ref), channel_id=1, source_target_pairs={{0,1},{1,0},{2,3},{3,2},{4,5},{5,4},{6,7},{7,6},{8,9},{9,8},{10,11... | collective-permute-start | bytes 786440 | tf_op jit(solution)/shard_map/ppermute | solution.py:248
  63.2 0.9 copy-start.11
  63.2 1.0 copy-start.12
  63.2 0.8 copy-start.8
  192.0 10.4 %copy-start.15 = (bf16[2048,704]{0,1:T(8,128)(2,1)S(1)}, bf16[2048,704]{0,1:T(8,128)(2,1)}, u32[]{:S(2)}) copy-start(bf16[2048,704]{0,1:T(8,128)(2,1)} %param.16) | copy-start | bytes 8650756
  192.0 5.9 %collective-permute-start.10 = (f32[2,256,1536]{2,1,0:T(8,128)}, f32[2,256,1536]{2,1,0:T(8,128)S(1)}, u32[]{:S(2)}, u32[]{:S(2)}) collective-permute-start(f32[2,256,1536]{2,1,0:T(8,128)} %get-tuple-element.26), channel_id=1, source_target_pairs={{0,1},{1,0},{2,3},{3,2},{4,5},{5,4},{6,7},{7,6},{8,9},{9,8},{10,11... | collective-permute-start | bytes 9437192 | tf_op jit(solution)/shard_map/ppermute | solution.py:248
  197.9 1.7 copy-start.4
  202.4 5.2 %copy-start.14 = (bf16[1024,2048]{1,0:T(8,128)(2,1)S(1)}, bf16[1024,2048]{1,0:T(8,128)(2,1)}, u32[]{:S(2)}) copy-start(bf16[1024,2048]{1,0:T(8,128)(2,1)} %all-gather.3.cloned.1.call-done) | copy-start | bytes 12582916
  202.4 5.2 %copy-start.16 = (bf16[2048,704]{0,1:T(8,128)(2,1)S(1)}, bf16[2048,704]{0,1:T(8,128)(2,1)}, u32[]{:S(2)}) copy-start(bf16[2048,704]{0,1:T(8,128)(2,1)} %param.17) | copy-start | bytes 8650756
  212.1 39.4 %all-to-all-start = ((bf16[4,256,704]{1,2,0:T(8,128)(2,1)}), bf16[4,256,704]{1,2,0:T(8,128)(2,1)}, u32[]{:S(2)}, u32[]{:S(2)}) async-start(bf16[4,256,704]{1,2,0:T(8,128)(2,1)} %bitcast.58), calls=%async_computation | async-start | bytes 2883584 | tf_op jit(solution)/shard_map/all_to_all | solution.py:397
  241.0 2.9 collective-permute-start.11
  241.1 37.5 %collective-permute-start.12 = (f32[256,1536]{1,0:T(8,128)}, f32[256,1536]{1,0:T(8,128)S(1)}, u32[]{:S(2)}, u32[]{:S(2)}) collective-permute-start(f32[256,1536]{1,0:T(8,128)} %fusion.24), channel_id=1, source_target_pairs={{0,2},{1,3},{2,0},{3,1},{4,6},{5,7},{6,4},{7,5},{8,10},{9,11},{10,... | collective-permute-start | bytes 4718600 | tf_op jit(solution)/shard_map/ppermute | solution.py:248
  245.1 44.4 %collective-permute-start.13 = (f32[256,512]{1,0:T(8,128)S(1)}, f32[256,512]{1,0:T(8,128)}, u32[]{:S(2)}, u32[]{:S(2)}) collective-permute-start(f32[256,512]{1,0:T(8,128)S(1)} %fusion.29), channel_id=1, source_target_pairs={{0,2},{1,3},{2,0},{3,1},{4,6},{5,7},{6,4},{7,5},{8,10},{9,11},{10,... | collective-permute-start | bytes 1572872 | tf_op jit(solution)/shard_map/ppermute | solution.py:248
  251.5 6.7 %copy-start.2 = (bf16[2816,2048]{1,0:T(8,128)(2,1)S(1)}, bf16[2816,2048]{1,0:T(8,128)(2,1)}, u32[]{:S(2)}) copy-start(bf16[2816,2048]{1,0:T(8,128)(2,1)} %all-gather.5.cloned.1.call-done) | copy-start | bytes 34603012
  258.2 2.1 copy-start.1
  260.3 18.3 %copy-start.3 = (f32[2,256,1536]{2,1,0:T(8,128)S(1)}, f32[2,256,1536]{2,1,0:T(8,128)}, u32[]{:S(2)}) copy-start(f32[2,256,1536]{2,1,0:T(8,128)} %get-tuple-element.25) | copy-start | bytes 9437188
  260.3 18.3 %copy-start.5 = (f32[2,256,1536]{2,1,0:T(8,128)S(1)}, f32[2,256,1536]{2,1,0:T(8,128)}, u32[]{:S(2)}) copy-start(f32[2,256,1536]{2,1,0:T(8,128)} %copy-done.4) | copy-start | bytes 9437188
  262.5 26.9 %copy-start.6 = (f32[2,256,512]{2,1,0:T(8,128)S(1)}, f32[2,256,512]{2,1,0:T(8,128)}, u32[]{:S(2)}) copy-start(f32[2,256,512]{2,1,0:T(8,128)} %get-tuple-element.32) | copy-start | bytes 3145732
Sparse Core Ops, SparseCore 0:
  8.9 83.4 all-gather.2
  95.2 89.2 all-gather.4

commit v5 on v4

--- a/solution.py
+++ b/solution.py
@@ -10,8 +10,8 @@
 
 CAP_FACTOR = 4
 GROUP = 4
-COLUMN_SHARES = (3, 1)
-TOKEN_SHARES = (1, 2, 1)
+COLUMN_SHARES = (5, 3)
+TOKEN_SHARES = (3, 1)
 ROW_PIECE = 128
 UP_SLOTS = 3
 DOWN_SLOTS = 4
@@ -71,13 +71,13 @@
     lax.fori_loop(0, gates_ref.shape[0], tile, 0)
 
 
-def up_kernel(cap, off_ref, n_ref, at1_ref, at2_ref, pick_ref, x0_ref, x1_ref, x2a_ref, x2b_ref, x2c_ref, x3a_ref, x3b_ref, x3c_ref, w1_hbm, w3_hbm, h0_ref, h1_ref, h2_ref, rows_ref, w1_ring, w3_ring, sems):
+def up_kernel(cap, off_ref, n_ref, at1_ref, at2_ref, pick_ref, x0_ref, x1_ref, x2a_ref, x2b_ref, x3a_ref, x3b_ref, w1_hbm, w3_hbm, h0_ref, h1_ref, h2_ref, rows_ref, w1_ring, w3_ring, sems):
     step = pl.program_id(0)
     n_steps = pl.num_programs(0)
     d_model = x0_ref.shape[1]
     d_ff = w1_ring.shape[2]
     n_slots = w1_ring.shape[0]
-    x_refs = ((x0_ref,), (x1_ref,), (x2a_ref, x2b_ref, x2c_ref), (x3a_ref, x3b_ref, x3c_ref))
+    x_refs = ((x0_ref,), (x1_ref,), (x2a_ref, x2b_ref), (x3a_ref, x3b_ref))
     piece_step = min(512, d_model // sum(TOKEN_SHARES))
     h_refs = (h0_ref, h1_ref, h2_ref)
 
@@ -384,17 +384,17 @@
         for chunk in range(len(widths)):
             own, sib = down(chunk, hidden)
             from_sib = swap(sib, 1)
-            passed_on = own[1] + from_sib[1]
-            returned.append(swap(passed_on, 2))
-            sums_own.append(own[0])
-            sums_sib.append(from_sib[0])
             if chunk == 0:
-                gathered, passed_on = lax.optimization_barrier((gathered, passed_on))
+                gathered, own = lax.optimization_barrier((gathered, own))
                 pre_gate = jnp.dot(gathered, shared_w1, preferred_element_type=jnp.float32)
                 pre_up = jnp.dot(gathered, shared_w3, preferred_element_type=jnp.float32)
                 shared_hidden = (jax.nn.silu(pre_gate) * pre_up).astype(jnp.bfloat16)
                 shared_hidden, *hidden = lax.optimization_barrier((shared_hidden, *hidden))
                 hidden_blocks = lax.all_to_all(shared_hidden.reshape(mesh.shape["tp"], n_tok, -1), "tp", 0, 0)
+            passed_on = own[1] + from_sib[1]
+            returned.append(swap(passed_on, 2))
+            sums_own.append(own[0])
+            sums_sib.append(from_sib[0])
 
         width = shared_w2.shape[0]
         rep = lax.axis_index("data") * ep_size + me
@@ -402,9 +402,7 @@
         w2_all = lax.all_gather(w2_part, ("tp", "data", "ep"), axis=0, tiled=True)
         w2_all, passed_on = lax.optimization_barrier((w2_all, passed_on))
         w2_blocks = w2_all.reshape(mesh.shape["tp"], width, d_model)
-        shared_out = jnp.dot(hidden_blocks[0], w2_blocks[0], preferred_element_type=jnp.float32)
-        for block in range(1, mesh.shape["tp"]):
-            shared_out += jnp.dot(hidden_blocks[block], w2_blocks[block], preferred_element_type=jnp.float32)
+        shared_out = jnp.einsum("sth,shd->td", hidden_blocks, w2_blocks, preferred_element_type=jnp.float32)
         base = tokens.astype(jnp.float32) + shared_out
         parts = []
         for chunk, (first, n_cols) in enumerate(zip(starts, widths)):

time: 299 us -> 291 us (0.973)
  waiting for transfers between devices: 63.3 us -> 59.1 us
  matrix products: 19.4 us -> 16 us
    all_to_all x1, waiting for transfers between devices: 6.33 us -> 0.01 us  [layer_body(): lax.all_to_all(shared_hidden.reshape(mesh.shape['tp'], n_tok, -1), 'tp',...]
    dot_general x4 -> x1, matrix products: 10.9 us -> 6.59 us  [layer_body(): jnp.einsum('sth,shd->td', hidden_blocks, w2_blocks, preferred_element_typ...]
    ppermute x14 -> x12, waiting for transfers between devices: 56.2 us -> 58.3 us  [swap(): return lax.ppermute(value, 'ep', [(i, i ^ bit) for i in range(ep_size)])]
    ppermute x14 -> x12, starting transfers between devices: 6.64 us -> 7.39 us  [swap(): return lax.ppermute(value, 'ep', [(i, i ^ bit) for i in range(ep_size)])]
  transfers between devices with their start and end apart: 17 -> 15, of which waited for: 7 -> 5; matrix products, arithmetic and copies ran while one was open for 12% -> 11% of each run, Pallas kernels for 56% -> 57%
where the time goes in v5:
time: 291 us
  Pallas kernels  167 us (57%)
  waiting for transfers between devices  59.1 us (20%)
  between operations  16.3 us (6%)
  matrix products  16 us (5%)
  other arithmetic  13.4 us (5%)
  starting transfers between devices  12.4 us (4%)
  local copies, waits for them, and re-layouts  6.62 us (2%)
    pallas_call x1, Pallas kernels, layer_body(): pl.pallas_call(functools.partial(up_kernel, cap), grid_spec=pltpu.Prefetc...  76.5 us
    pallas_call x2, Pallas kernels, down(): pl.pallas_call(functools.partial(down_kernel, cap, starts[chunk]), grid_s...  75.5 us
    ppermute x12, waiting for transfers between devices, swap(): return lax.ppermute(value, 'ep', [(i, i ^ bit) for i in range(ep_size)])  58.3 us
    pallas_call x1, Pallas kernels, layer_body(): pl.pallas_call(prep_kernel, grid=(4,), in_specs=[pl.BlockSpec((1, 16, n_t...  14.8 us
    ppermute x12, starting transfers between devices, swap(): return lax.ppermute(value, 'ep', [(i, i ^ bit) for i in range(ep_size)])  7.39 us
    dot_general x1, matrix products, layer_body(): jnp.einsum('sth,shd->td', hidden_blocks, w2_blocks, preferred_element_typ...  6.59 us
    dot_general x1, matrix products, layer_body(): pre_gate = jnp.dot(gathered, shared_w1, preferred_element_type=jnp.float32)  6.01 us
  transfers between devices with their start and end apart: 15, of which 5 were waited for; matrix products, arithmetic and copies ran while one was open for 11% of the time, Pallas kernels for 57%

profile of v5, /device:TPU:0, one launch (start us, length us, event | category | flops | bytes accessed | tf_op | source)
XLA Modules:
  0.0 290.5 jit_solution(12398957231762646475)
XLA Ops:
  6.5 0.7 all-gather.3.cloned.1.call-update
  7.3 0.0 all-gather.5.cloned.1.call-start
  7.3 1.8 constant_dynamic-slice_fusion
  9.1 0.0 all-gather.5.cloned.1.call-update
  9.1 0.7 convert_element_type.30
  9.8 0.1 pad.21.clone
  9.8 0.8 select_reduce_fusion.1
  10.7 0.7 convert_bitcast_fusion
  11.4 0.7 select_bitcast_fusion
  12.1 0.1 fusion.15
  12.2 3.0 %collective-permute-start.1 = (f32[16,256]{1,0:T(8,128)S(1)}, f32[16,256]{1,0:T(8,128)S(1)}, u32[]{:S(2)}, u32[]{:S(2)}) collective-permute-start(f32[16,256]{1,0:T(8,128)S(1)} %fusion.15), channel_id=1, source_target_pairs={{0,2},{1,3},{2,0},{3,1},{4,6},{5,7},{6,4},{7,5},{8,10},{9,11},{10,... | collective-permute-start | bytes 49160 | tf_op jit(solution)/shard_map/ppermute | solution.py:248
  15.2 0.0 collective-permute-start
  15.2 0.5 collective-permute-start.3
  15.7 0.1 slice.48
  15.8 0.1 collective-permute-start.4
  15.9 2.0 collective-permute-start.5
  18.0 0.1 fusion.35
  18.0 0.0 collective-permute-done.1
  18.0 0.1 collective-permute-start.2
  18.1 0.0 collective-permute-done
  18.1 1.1 collective-permute-done.2
  19.3 0.1 fusion.24
  19.4 0.1 select_reduce_fusion.2
  19.6 0.2 select_reduce_fusion
  19.8 0.7 fusion.26
  20.5 0.1 select_reduce_fusion.3
  20.6 15.6 %collective-permute-done.4.x2a_ref = bf16[256,1536]{1,0:T(8,128)(2,1)S(1)} collective-permute-done((bf16[256,1536]{1,0:T(8,128)(2,1)S(1)}, bf16[256,1536]{1,0:T(8,128)(2,1)S(1)}, u32[]{:S(2)}, u32[]{:S(2)}) %collective-permute-start.4) | collective-permute-done | bytes 786464 | tf_op jit(solution)/shard_map/ppermute | solution.py:248
  36.3 0.0 collective-permute-start.6
  36.3 0.1 select_reduce_fusion.4
  36.4 0.1 select_reduce_fusion.5
  36.5 0.7 select_reduce_fusion.6
  37.2 3.7 %collective-permute-done.5.x2b_ref = bf16[256,512]{1,0:T(8,128)(2,1)S(1)} collective-permute-done((bf16[256,512]{1,0:T(8,128)(2,1)S(1)}, bf16[256,512]{1,0:T(8,128)(2,1)S(1)}, u32[]{:S(2)}, u32[]{:S(2)}) %collective-permute-start.5) | collective-permute-done | bytes 262176 | tf_op jit(solution)/shard_map/ppermute | solution.py:248
  40.9 14.8 %prep.1 = (bf16[4,1536,256]{2,1,0:T(8,128)(2,1)}, bf16[24,3,256,256]{3,2,1,0:T(8,128)(2,1)}) custom-call(s32[4,16,256]{2,1,0:T(8,128)S(1)} %pad_add_fusion.facts_ref, f32[3,4,6,256]{3,2,1,0:T(8,128)S(1)} %pad_maximum_fusion.1.gates_in_ref), custom_call_target="tpu_custom_call" | custom-call | flops 1000000000 | bytes 12582912 | tf_op jit(solution)/shard_map/prep/pallas_call | solution.py:302
  55.7 0.6 reshape.73.queue_off_ref
  56.3 0.1 copy.18
  56.4 0.7 reshape.72.off_ref
  59.6 0.6 compare_select_fusion.3
  60.2 0.0 collective-permute-done.7.x3b_ref
  60.2 0.0 collective-permute-done.6.x3a_ref
  60.2 0.9 copy-done.7
  61.2 0.1 copy-done.9
  61.2 76.5 %experts_up.1 = (bf16[16,128,1408]{2,1,0:T(8,128)(2,1)}, bf16[16,128,1408]{2,1,0:T(8,128)(2,1)}, bf16[16,128,1408]{2,1,0:T(8,128)(2,1)}) custom-call(s32[64]{0:T(128)} %reshape.72.off_ref, s32[16]{0:T(128)} %copy-done.10, s32[16]{0:T(128)} %get-tuple-element.54.at1_ref, s32[16]{0:T(128)} %get-tuple-element.53.at2_ref, ...), custom_call_target="tpu_custom_call" | custom-call | flops 35433480192 | bytes 184549376 | tf_op jit(solution)/shard_map/experts_up/pallas_call | solution.py:324
  137.8 45.0 %shard_map.109 = (f32[2,256,1280]{2,1,0:T(8,128)}, f32[2,256,1280]{2,1,0:T(8,128)}) custom-call(s32[64]{0:T(128)} %reshape.72.off_ref, s32[16]{0:T(128)} %copy-done.10, s32[64]{0:T(128)} %reshape.73.queue_off_ref, s32[4]{0:T(128)} %get-tuple-element.37.total_ref, bf16[16,128,1408]{2,1,0:T(8,128)(2,1)} %get-tuple-element.29.h0_hbm, ...), custom_call_target="tpu_custom_call" | custom-call | flops 11072962560 | bytes 57671680 | tf_op jit(solution)/shard_map/pallas_call | solution.py:359
  182.7 0.1 collective-permute-start.9
  182.8 0.0 all-gather.3.cloned.1.call-done
  182.8 0.0 copy-start.12
  182.9 6.0 %fusion.28 = f32[1024,704]{0,1:T(8,128)S(1)} fusion(bf16[1024,2048]{1,0:T(8,128)(2,1)} %all-gather.3.cloned.1.call-done, bf16[2048,704]{0,1:T(8,128)(2,1)} %param.16), kind=kOutput, calls=%fused_computation.88 | convolution fusion | flops 2952790016 | bytes 9961472 | tf_op jit(solution)/shard_map/dot_general | solution.py:389
  188.9 3.4 %multiply_convert_fusion = bf16[1024,704]{0,1:T(8,128)(2,1)S(1)} fusion(f32[1024,704]{0,1:T(8,128)S(1)} %fusion.28, bf16[1024,2048]{1,0:T(8,128)(2,1)S(1)} %copy-done.11, bf16[2048,704]{0,1:T(8,128)(2,1)S(1)} %copy-done.12), kind=kOutput, calls=%fused_computation | convolution fusion | flops 2957115392 | bytes 11403264 | tf_op jit(solution)/shard_map/dot_general | solution.py:390
  192.3 1.2 copy.22
  193.5 4.9 %all-to-all-start = ((bf16[4,256,704]{1,2,0:T(8,128)(2,1)}), bf16[4,256,704]{1,2,0:T(8,128)(2,1)}, u32[]{:S(2)}, u32[]{:S(2)}) async-start(bf16[4,256,704]{1,2,0:T(8,128)(2,1)} %bitcast.53), calls=%async_computation | async-start | bytes 2883584 | tf_op jit(solution)/shard_map/all_to_all | solution.py:393
  198.4 30.6 %shard_map.110 = (f32[2,256,768]{2,1,0:T(8,128)}, f32[2,256,768]{2,1,0:T(8,128)}) custom-call(s32[64]{0:T(128)} %reshape.72.off_ref, s32[16]{0:T(128)} %copy-done.10, s32[64]{0:T(128)} %reshape.73.queue_off_ref, s32[4]{0:T(128)} %get-tuple-element.37.total_ref, bf16[16,128,1408]{2,1,0:T(8,128)(2,1)} %get-tuple-element.29.h0_hbm, ...), custom_call_target="tpu_custom_call" | custom-call | flops 6643777536 | bytes 34603008 | tf_op jit(solution)/shard_map/pallas_call | solution.py:359
  229.0 0.0 copy-start.1
  229.0 0.1 collective-permute-start.8
  229.1 3.1 %fusion.1 = f32[256,1280]{1,0:T(8,128)} fusion(f32[2,256,1280]{2,1,0:T(8,128)} %collective-permute-done.9, f32[2,256,1280]{2,1,0:T(8,128)} %get-tuple-element.35), kind=kLoop, calls=%fused_computation.5 | loop fusion | flops 327680 | bytes 3932160 | tf_op jit(solution)/shard_map/add | solution.py:394
  232.2 0.0 collective-permute-start.10
  232.2 0.5 collective-permute-done.8
  232.7 1.1 copy-done.4
  233.8 1.0 fusion.10
  234.8 1.5 collective-permute-start.11
  236.3 6.6 %fusion = f32[256,2048]{1,0:T(8,128)S(1)} fusion(bf16[4,256,704]{1,2,0:T(8,128)(2,1)} %all-to-all-done, bf16[4,704,2048]{2,1,0:T(8,128)(2,1)} %bitcast.54, bf16[256,2048]{1,0:T(8,128)(2,1)S(1)} %copy-done.1), kind=kOutput, calls=%fused_computation.2 | convolution fusion | flops 2953838592 | bytes 16121856 | tf_op jit(solution)/shard_map/sth,shd->td/dot_general | solution.py:405
  242.9 37.3 %collective-permute-done.11 = f32[256,768]{1,0:T(8,128)S(1)} collective-permute-done((f32[256,768]{1,0:T(8,128)}, f32[256,768]{1,0:T(8,128)S(1)}, u32[]{:S(2)}, u32[]{:S(2)}) %collective-permute-start.11) | collective-permute-done | bytes 786464 | tf_op jit(solution)/shard_map/ppermute | solution.py:248
  280.2 0.2 fusion.9
  280.5 2.1 fusion.5
  282.6 1.1 pad_maximum_fusion
  (42 shorter events, 0.2 us)
Async XLA Ops:
  6.5 9.2 %copy-start = (bf16[256,2048]{1,0:T(8,128)(2,1)S(1)}, bf16[256,2048]{1,0:T(8,128)(2,1)}, u32[]{:S(2)}) copy-start(bf16[256,2048]{1,0:T(8,128)(2,1)} %x0_ref.1) | copy-start | bytes 3145732
  6.5 176.3 %all-gather.3.cloned.1.call-start = ((), (), s32[]{:S(2)}) async-start(), calls=%async_computation.1 | async-start | bytes 5242880 | tf_op jit(solution)/shard_map/all_gather | solution.py:382
  7.3 229.0 %all-gather.5.cloned.1.call-start = ((), (), s32[]{:S(2)}) async-start(), calls=%async_computation.2 | async-start | bytes 11894784 | tf_op jit(solution)/shard_map/all_gather | solution.py:402
  12.2 5.8 %collective-permute-start.1 = (f32[16,256]{1,0:T(8,128)S(1)}, f32[16,256]{1,0:T(8,128)S(1)}, u32[]{:S(2)}, u32[]{:S(2)}) collective-permute-start(f32[16,256]{1,0:T(8,128)S(1)} %fusion.15), channel_id=1, source_target_pairs={{0,2},{1,3},{2,0},{3,1},{4,6},{5,7},{6,4},{7,5},{8,10},{9,11},{10,... | collective-permute-start | bytes 49160 | tf_op jit(solution)/shard_map/ppermute | solution.py:248
  15.2 2.9 %collective-permute-start = (f32[16,256]{1,0:T(8,128)S(1)}, f32[16,256]{1,0:T(8,128)S(1)}, u32[]{:S(2)}, u32[]{:S(2)}) collective-permute-start(f32[16,256]{1,0:T(8,128)S(1)} %fusion.15), channel_id=1, source_target_pairs={{0,1},{1,0},{2,3},{3,2},{4,5},{5,4},{6,7},{7,6},{8,9},{9,8},{10,11... | collective-permute-start | bytes 49160 | tf_op jit(solution)/shard_map/ppermute | solution.py:248
  15.2 45.0 %collective-permute-start.3 = (bf16[256,2048]{1,0:T(8,128)(2,1)}, bf16[256,2048]{1,0:T(8,128)(2,1)}, u32[]{:S(2)}, u32[]{:S(2)}) collective-permute-start(bf16[256,2048]{1,0:T(8,128)(2,1)} %x0_ref.1), channel_id=1, source_target_pairs={{0,1},{1,0},{2,3},{3,2},{4,5},{5,4},{6,7},{7,6},{8,9},{9,8},{10,11... | collective-permute-start | bytes 3145736 | tf_op jit(solution)/shard_map/ppermute | solution.py:248
  15.8 20.5 %collective-permute-start.4 = (bf16[256,1536]{1,0:T(8,128)(2,1)S(1)}, bf16[256,1536]{1,0:T(8,128)(2,1)S(1)}, u32[]{:S(2)}, u32[]{:S(2)}) collective-permute-start(bf16[256,1536]{1,0:T(8,128)(2,1)S(1)} %slice.48), channel_id=1, source_target_pairs={{0,2},{1,3},{2,0},{3,1},{4,6},{5,7},{6,4},{7,5},{8,10},{9,11},{10,... | collective-permute-start | bytes 2359304 | tf_op jit(solution)/shard_map/ppermute | solution.py:248
  15.9 25.0 %collective-permute-start.5 = (bf16[256,512]{1,0:T(8,128)(2,1)S(1)}, bf16[256,512]{1,0:T(8,128)(2,1)S(1)}, u32[]{:S(2)}, u32[]{:S(2)}) collective-permute-start(bf16[256,512]{1,0:T(8,128)(2,1)S(1)} %slice.49), channel_id=1, source_target_pairs={{0,2},{1,3},{2,0},{3,1},{4,6},{5,7},{6,4},{7,5},{8,10},{9,11},{10,... | collective-permute-start | bytes 786440 | tf_op jit(solution)/shard_map/ppermute | solution.py:248
  18.0 1.2 collective-permute-start.2
  20.5 40.8 %copy-start.10 = (s32[16]{0:T(128)}, s32[16]{0:T(128)S(1)}, u32[]{:S(2)}) copy-start(s32[16]{0:T(128)S(1)} %get-tuple-element.38.n_ref) | copy-start | bytes 196
  36.2 25.0 %copy-start.6 = (bf16[256,1536]{1,0:T(8,128)(2,1)}, bf16[256,1536]{1,0:T(8,128)(2,1)S(1)}, u32[]{:S(2)}) copy-start(bf16[256,1536]{1,0:T(8,128)(2,1)S(1)} %collective-permute-done.4.x2a_ref) | copy-start | bytes 2359300
  36.3 24.0 %collective-permute-start.6 = (bf16[256,1536]{1,0:T(8,128)(2,1)S(1)}, bf16[256,1536]{1,0:T(8,128)(2,1)S(1)}, u32[]{:S(2)}, u32[]{:S(2)}) collective-permute-start(bf16[256,1536]{1,0:T(8,128)(2,1)S(1)} %collective-permute-done.4.x2a_ref), channel_id=1, source_target_pairs={{0,1},{1,0},{2,3},{3,2},{4,5},{5,4},{6,7},{7,6},{8,9},{9,8},{10,11... | collective-permute-start | bytes 2359304 | tf_op jit(solution)/shard_map/ppermute | solution.py:248
  40.9 20.3 %copy-start.8 = (bf16[256,512]{1,0:T(8,128)(2,1)}, bf16[256,512]{1,0:T(8,128)(2,1)S(1)}, u32[]{:S(2)}) copy-start(bf16[256,512]{1,0:T(8,128)(2,1)S(1)} %collective-permute-done.5.x2b_ref) | copy-start | bytes 786436
  40.9 19.3 %collective-permute-start.7 = (bf16[256,512]{1,0:T(8,128)(2,1)S(1)}, bf16[256,512]{1,0:T(8,128)(2,1)S(1)}, u32[]{:S(2)}, u32[]{:S(2)}) collective-permute-start(bf16[256,512]{1,0:T(8,128)(2,1)S(1)} %collective-permute-done.5.x2b_ref), channel_id=1, source_target_pairs={{0,1},{1,0},{2,3},{3,2},{4,5},{5,4},{6,7},{7,6},{8,9},{9,8},{10,11... | collective-permute-start | bytes 786440 | tf_op jit(solution)/shard_map/ppermute | solution.py:248
  60.2 1.0 copy-start.9
  60.2 0.9 copy-start.7
  182.7 46.4 %collective-permute-start.9 = (f32[2,256,1280]{2,1,0:T(8,128)}, f32[2,256,1280]{2,1,0:T(8,128)}, u32[]{:S(2)}, u32[]{:S(2)}) collective-permute-start(f32[2,256,1280]{2,1,0:T(8,128)} %get-tuple-element.36), channel_id=1, source_target_pairs={{0,1},{1,0},{2,3},{3,2},{4,5},{5,4},{6,7},{7,6},{8,9},{9,8},{10,11... | collective-permute-start | bytes 7864328 | tf_op jit(solution)/shard_map/ppermute | solution.py:248
  182.8 6.0 %copy-start.11 = (bf16[1024,2048]{1,0:T(8,128)(2,1)S(1)}, bf16[1024,2048]{1,0:T(8,128)(2,1)}, u32[]{:S(2)}) copy-start(bf16[1024,2048]{1,0:T(8,128)(2,1)} %all-gather.3.cloned.1.call-done) | copy-start | bytes 12582916
  182.8 6.0 %copy-start.12 = (bf16[2048,704]{0,1:T(8,128)(2,1)S(1)}, bf16[2048,704]{0,1:T(8,128)(2,1)}, u32[]{:S(2)}) copy-start(bf16[2048,704]{0,1:T(8,128)(2,1)} %param.17) | copy-start | bytes 8650756
  193.5 42.9 %all-to-all-start = ((bf16[4,256,704]{1,2,0:T(8,128)(2,1)}), bf16[4,256,704]{1,2,0:T(8,128)(2,1)}, u32[]{:S(2)}, u32[]{:S(2)}) async-start(bf16[4,256,704]{1,2,0:T(8,128)(2,1)} %bitcast.53), calls=%async_computation | async-start | bytes 2883584 | tf_op jit(solution)/shard_map/all_to_all | solution.py:393
  229.0 4.8 %copy-start.3 = (f32[2,256,768]{2,1,0:T(8,128)S(1)}, f32[2,256,768]{2,1,0:T(8,128)}, u32[]{:S(2)}) copy-start(f32[2,256,768]{2,1,0:T(8,128)} %get-tuple-element.32) | copy-start | bytes 4718596
  229.0 7.3 %copy-start.1 = (bf16[256,2048]{1,0:T(8,128)(2,1)S(1)}, bf16[256,2048]{1,0:T(8,128)(2,1)}, u32[]{:S(2)}) copy-start(bf16[256,2048]{1,0:T(8,128)(2,1)} %x0_ref.1) | copy-start | bytes 3145732
  229.0 3.7 %collective-permute-start.8 = (f32[2,256,768]{2,1,0:T(8,128)}, f32[2,256,768]{2,1,0:T(8,128)S(1)}, u32[]{:S(2)}, u32[]{:S(2)}) collective-permute-start(f32[2,256,768]{2,1,0:T(8,128)} %get-tuple-element.33), channel_id=1, source_target_pairs={{0,1},{1,0},{2,3},{3,2},{4,5},{5,4},{6,7},{7,6},{8,9},{9,8},{10,11... | collective-permute-start | bytes 4718600 | tf_op jit(solution)/shard_map/ppermute | solution.py:248
  232.2 48.3 %collective-permute-start.10 = (f32[256,1280]{1,0:T(8,128)}, f32[256,1280]{1,0:T(8,128)}, u32[]{:S(2)}, u32[]{:S(2)}) collective-permute-start(f32[256,1280]{1,0:T(8,128)} %fusion.1), channel_id=1, source_target_pairs={{0,2},{1,3},{2,0},{3,1},{4,6},{5,7},{6,4},{7,5},{8,10},{9,11},{10,... | collective-permute-start | bytes 3932168 | tf_op jit(solution)/shard_map/ppermute | solution.py:248
  232.7 1.1 copy-start.4
  234.8 45.4 %collective-permute-start.11 = (f32[256,768]{1,0:T(8,128)}, f32[256,768]{1,0:T(8,128)S(1)}, u32[]{:S(2)}, u32[]{:S(2)}) collective-permute-start(f32[256,768]{1,0:T(8,128)} %fusion.10), channel_id=1, source_target_pairs={{0,2},{1,3},{2,0},{3,1},{4,6},{5,7},{6,4},{7,5},{8,10},{9,11},{10,... | collective-permute-start | bytes 2359304 | tf_op jit(solution)/shard_map/ppermute | solution.py:248
  236.3 43.9 %copy-start.5 = (f32[2,256,768]{2,1,0:T(8,128)S(1)}, f32[2,256,768]{2,1,0:T(8,128)}, u32[]{:S(2)}) copy-start(f32[2,256,768]{2,1,0:T(8,128)} %copy-done.4) | copy-start | bytes 4718596
  242.9 37.6 %copy-start.2 = (f32[2,256,1280]{2,1,0:T(8,128)S(1)}, f32[2,256,1280]{2,1,0:T(8,128)}, u32[]{:S(2)}) copy-start(f32[2,256,1280]{2,1,0:T(8,128)} %get-tuple-element.35) | copy-start | bytes 7864324
Sparse Core Ops, SparseCore 0:
  8.9 83.4 all-gather.2
  95.3 89.3 all-gather.4

commit v6 on v5

--- a/solution.py
+++ b/solution.py
@@ -10,7 +10,7 @@
 
 CAP_FACTOR = 4
 GROUP = 4
-COLUMN_SHARES = (5, 3)
+COLUMN_SHARES = (3, 1)
 TOKEN_SHARES = (3, 1)
 ROW_PIECE = 128
 UP_SLOTS = 3
@@ -43,7 +43,7 @@
     return pieces
 
 
-def prep_kernel(facts_ref, gates_in_ref, pick_ref, gates_ref):
+def prep_kernel(total_ref, facts_ref, gates_in_ref, pick_ref, gates_ref):
     top_k = gates_in_ref.shape[2]
     n_tok = pick_ref.shape[2]
     step_rows = 32
@@ -61,14 +61,15 @@
 
     def tile(index, carry):
         row = lax.broadcasted_iota(jnp.int32, (256, n_tok), 0) + index * 256
-        for piece in range(3):
-            weight = jnp.zeros((256, n_tok), jnp.float32)
-            for j in range(top_k):
-                weight = jnp.where(facts_ref[0, 8 + j : 9 + j, :] == row, gates_in_ref[piece, 0, j : j + 1, :], weight)
+        weights = [jnp.zeros((256, n_tok), jnp.float32) for _ in range(3)]
+        for j in range(top_k):
+            here = facts_ref[0, 8 + j : 9 + j, :] == row
+            weights = [jnp.where(here, gates_in_ref[piece, 0, j : j + 1, :], weight) for piece, weight in enumerate(weights)]
+        for piece, weight in enumerate(weights):
             gates_ref[index, piece] = weight.astype(jnp.bfloat16).T
         return carry
 
-    lax.fori_loop(0, gates_ref.shape[0], tile, 0)
+    lax.fori_loop(0, (total_ref[pl.program_id(0)] + 255) // 256, tile, 0)
 
 
 def up_kernel(cap, off_ref, n_ref, at1_ref, at2_ref, pick_ref, x0_ref, x1_ref, x2a_ref, x2b_ref, x3a_ref, x3b_ref, w1_hbm, w3_hbm, h0_ref, h1_ref, h2_ref, rows_ref, w1_ring, w3_ring, sems):
@@ -299,17 +300,21 @@
         middle = lax.reduce_precision(gates_all - high, 8, 7)
         low = lax.reduce_precision(gates_all - high - middle, 8, 7)
         n_tiles = n_queue // 256
+        places, off, n_rows, at1, at2, queue_off = lax.optimization_barrier((places, off, n_rows, at1, at2, queue_off.reshape(-1)))
         pick, gate_tiles = pl.pallas_call(
             prep_kernel,
-            grid=(4,),
-            in_specs=[
-                pl.BlockSpec((1, 16, n_tok), lambda s: (s, 0, 0)),
-                pl.BlockSpec((3, 1, top_k, n_tok), lambda s: (0, s, 0, 0)),
-            ],
-            out_specs=[
-                pl.BlockSpec((1, n_queue, n_tok), lambda s: (s, 0, 0)),
-                pl.BlockSpec((n_tiles, 3, n_tok, 256), lambda s: (s, 0, 0, 0)),
-            ],
+            grid_spec=pltpu.PrefetchScalarGridSpec(
+                num_scalar_prefetch=1,
+                grid=(4,),
+                in_specs=[
+                    pl.BlockSpec((1, 16, n_tok), lambda s, *_: (s, 0, 0)),
+                    pl.BlockSpec((3, 1, top_k, n_tok), lambda s, *_: (0, s, 0, 0)),
+                ],
+                out_specs=[
+                    pl.BlockSpec((1, n_queue, n_tok), lambda s, *_: (s, 0, 0)),
+                    pl.BlockSpec((n_tiles, 3, n_tok, 256), lambda s, *_: (s, 0, 0, 0)),
+                ],
+            ),
             out_shape=[
                 pltpu.HBM((4, n_queue, n_tok), jnp.bfloat16),
                 pltpu.HBM((4 * n_tiles, 3, n_tok, 256), jnp.bfloat16),
@@ -317,7 +322,7 @@
             compiler_params=pltpu.CompilerParams(dimension_semantics=("arbitrary",), vmem_limit_bytes=40_000_000),
             cost_estimate=pl.CostEstimate(flops=10**9, bytes_accessed=4 * n_queue * n_tok * 8, transcendentals=0),
             name="prep",
-        )(places, jnp.stack([high, middle, low]))
+        )(total, places, jnp.stack([high, middle, low]))
 
         whole = dict(pipeline_mode=pl.Buffered(1))
         any_space = pl.BlockSpec(memory_space=pl.ANY)
@@ -377,7 +382,7 @@
                 out_shape=[jax.ShapeDtypeStruct((2, n_tok, n_cols), jnp.float32) for _ in range(2)],
                 compiler_params=pltpu.CompilerParams(dimension_semantics=("arbitrary",), vmem_limit_bytes=VMEM_LIMIT),
                 cost_estimate=pl.CostEstimate(flops=2 * n_local * 192 * n_cols * d_ff, bytes_accessed=2 * n_local * n_cols * d_ff, transcendentals=0),
-            )(off, n_rows, queue_off.reshape(-1), total, *held, expert_w2, gate_tiles)
+            )(off, n_rows, queue_off, total, *held, expert_w2, gate_tiles)
 
         gathered = lax.all_gather(tokens, "tp", axis=0, tiled=True)
         sums_own, sums_sib, returned = [], [], []

time: 291 us -> 288 us (0.990)
  Pallas kernels: 167 us -> 164 us
    ppermute x12, waiting for transfers between devices: 58.3 us -> 51.6 us  [swap(): return lax.ppermute(value, 'ep', [(i, i ^ bit) for i in range(ep_size)])]
    all_to_all x1, waiting for transfers between devices: 0.01 us -> 4.22 us  [layer_body(): lax.all_to_all(shared_hidden.reshape(mesh.shape['tp'], n_tok, -1), 'tp',...]
where the time goes in v6:
time: 288 us; the launch traced here: 287 us
  Pallas kernels  164 us (57%)
  waiting for transfers between devices  56.5 us (20%)
  between operations  16.1 us (6%)
  matrix products  16 us (6%)
  other arithmetic  13.1 us (5%)
  starting transfers between devices  12.7 us (4%)
  local copies, waits for them, and re-layouts  9.12 us (3%)
    pallas_call x1, Pallas kernels, layer_body(): pl.pallas_call(functools.partial(up_kernel, cap), grid_spec=pltpu.Prefetc...  76.6 us
    pallas_call x2, Pallas kernels, down(): pl.pallas_call(functools.partial(down_kernel, cap, starts[chunk]), grid_s...  75 us
    ppermute x12, waiting for transfers between devices, swap(): return lax.ppermute(value, 'ep', [(i, i ^ bit) for i in range(ep_size)])  51.6 us
    pallas_call x1, Pallas kernels, layer_body(): pl.pallas_call(prep_kernel, grid_spec=pltpu.PrefetchScalarGridSpec(num_sc...  12.2 us
    ppermute x12, starting transfers between devices, swap(): return lax.ppermute(value, 'ep', [(i, i ^ bit) for i in range(ep_size)])  7.91 us
    dot_general x1, matrix products, layer_body(): jnp.einsum('sth,shd->td', hidden_blocks, w2_blocks, preferred_element_typ...  6.62 us
    dot_general x1, matrix products, layer_body(): pre_gate = jnp.dot(gathered, shared_w1, preferred_element_type=jnp.float32)  6.01 us
  transfers between devices with their start and end apart: 15, of which 5 were waited for; matrix products, arithmetic and copies ran while one was open for 11% of the time, Pallas kernels for 57%

profile of v6, /device:TPU:0, one launch (start us, length us, event | category | flops | bytes accessed | tf_op | source)
XLA Modules:
  0.0 287.3 jit_solution(17479974457874222839)
XLA Ops:
  6.5 0.7 all-gather.3.cloned.1.call-update
  7.3 0.0 all-gather.5.cloned.1.call-start
  7.3 1.8 constant_dynamic-slice_fusion
  9.1 0.0 all-gather.5.cloned.1.call-update
  9.1 0.7 convert_element_type.30
  9.7 0.1 pad.21.clone
  9.8 0.8 select_reduce_fusion.1
  10.7 0.7 convert_bitcast_fusion
  11.4 0.7 select_bitcast_fusion
  12.1 0.1 fusion.15
  12.2 3.0 %collective-permute-start.1 = (f32[16,256]{1,0:T(8,128)S(1)}, f32[16,256]{1,0:T(8,128)S(1)}, u32[]{:S(2)}, u32[]{:S(2)}) collective-permute-start(f32[16,256]{1,0:T(8,128)S(1)} %fusion.15), channel_id=1, source_target_pairs={{0,2},{1,3},{2,0},{3,1},{4,6},{5,7},{6,4},{7,5},{8,10},{9,11},{10,... | collective-permute-start | bytes 49160 | tf_op jit(solution)/shard_map/ppermute | solution.py:249
  15.2 0.0 collective-permute-start
  15.2 0.5 collective-permute-start.3
  15.7 1.2 slice.48
  16.9 0.1 collective-permute-start.4
  17.0 1.0 slice.49
  18.0 2.0 collective-permute-start.5
  20.0 0.1 fusion.35
  20.1 0.0 collective-permute-done.1
  20.1 0.1 collective-permute-start.2
  20.2 0.0 collective-permute-done
  20.2 1.1 collective-permute-done.2
  21.3 0.1 fusion.24
  21.4 0.1 fusion.26
  21.6 0.1 select_reduce_fusion.3
  21.7 0.1 select_reduce_fusion.2
  21.9 0.2 select_reduce_fusion
  22.1 0.6 select_reduce_fusion.6
  25.1 0.1 select_reduce_fusion.4
  25.2 12.1 %collective-permute-done.4.x2a_ref = bf16[256,1536]{1,0:T(8,128)(2,1)S(1)} collective-permute-done((bf16[256,1536]{1,0:T(8,128)(2,1)S(1)}, bf16[256,1536]{1,0:T(8,128)(2,1)S(1)}, u32[]{:S(2)}, u32[]{:S(2)}) %collective-permute-start.4) | collective-permute-done | bytes 786464 | tf_op jit(solution)/shard_map/ppermute | solution.py:249
  37.4 0.0 collective-permute-start.6
  37.4 0.6 compare_select_fusion.3
  38.0 4.0 %collective-permute-done.5.x2b_ref = bf16[256,512]{1,0:T(8,128)(2,1)S(1)} collective-permute-done((bf16[256,512]{1,0:T(8,128)(2,1)S(1)}, bf16[256,512]{1,0:T(8,128)(2,1)S(1)}, u32[]{:S(2)}, u32[]{:S(2)}) %collective-permute-start.5) | collective-permute-done | bytes 262176 | tf_op jit(solution)/shard_map/ppermute | solution.py:249
  42.0 0.0 collective-permute-start.7
  42.0 0.1 select_reduce_fusion.5
  42.1 0.6 reshape.72.queue_off_ref
  42.8 0.1 copy.18
  42.8 0.6 reshape.71.off_ref
  43.4 12.2 %prep.1 = (bf16[4,1536,256]{2,1,0:T(8,128)(2,1)}, bf16[24,3,256,256]{3,2,1,0:T(8,128)(2,1)}) custom-call(s32[4]{0:T(128)S(1)} %get-tuple-element.49.total_ref, s32[4,16,256]{2,1,0:T(8,128)S(1)} %pad_add_fusion.facts_ref, f32[3,4,6,256]{3,2,1,0:T(8,128)S(1)} %pad_maximum_fusion.1.gates_in_ref), custom_call_target="tpu_custom_call" | custom-call | flops 1000000000 | bytes 12582912 | tf_op jit(solution)/shard_map/prep/pallas_call | solution.py:304
  55.6 0.7 copy-done.10
  56.3 0.9 copy-done.8
  57.3 76.6 %experts_up.1 = (bf16[16,128,1408]{2,1,0:T(8,128)(2,1)}, bf16[16,128,1408]{2,1,0:T(8,128)(2,1)}, bf16[16,128,1408]{2,1,0:T(8,128)(2,1)}) custom-call(s32[64]{0:T(128)} %reshape.71.off_ref, s32[16]{0:T(128)} %copy-done.11, s32[16]{0:T(128)} %get-tuple-element.30.at1_ref, s32[16]{0:T(128)} %get-tuple-element.31.at2_ref, ...), custom_call_target="tpu_custom_call" | custom-call | flops 35433480192 | bytes 184549376 | tf_op jit(solution)/shard_map/experts_up/pallas_call | solution.py:329
  133.8 50.9 %shard_map.109 = (f32[2,256,1536]{2,1,0:T(8,128)}, f32[2,256,1536]{2,1,0:T(8,128)}) custom-call(s32[64]{0:T(128)} %reshape.71.off_ref, s32[16]{0:T(128)} %copy-done.11, s32[64]{0:T(128)} %reshape.72.queue_off_ref, s32[4]{0:T(128)} %copy-done, bf16[16,128,1408]{2,1,0:T(8,128)(2,1)} %get-tuple-element.41.h0_hbm, ...), custom_call_target="tpu_custom_call" | custom-call | flops 13287555072 | bytes 69206016 | tf_op jit(solution)/shard_map/pallas_call | solution.py:364
  184.8 0.1 collective-permute-start.9
  184.8 0.0 all-gather.3.cloned.1.call-done
  184.9 0.0 copy-start.13
  184.9 6.0 %fusion.28 = f32[1024,704]{0,1:T(8,128)S(1)} fusion(bf16[1024,2048]{1,0:T(8,128)(2,1)} %all-gather.3.cloned.1.call-done, bf16[2048,704]{0,1:T(8,128)(2,1)} %param.16), kind=kOutput, calls=%fused_computation.88 | convolution fusion | flops 2952790016 | bytes 9961472 | tf_op jit(solution)/shard_map/dot_general | solution.py:394
  190.9 3.4 %multiply_convert_fusion = bf16[1024,704]{0,1:T(8,128)(2,1)S(1)} fusion(f32[1024,704]{0,1:T(8,128)S(1)} %fusion.28, bf16[1024,2048]{1,0:T(8,128)(2,1)S(1)} %copy-done.12, bf16[2048,704]{0,1:T(8,128)(2,1)S(1)} %copy-done.13), kind=kOutput, calls=%fused_computation | convolution fusion | flops 2957115392 | bytes 11403264 | tf_op jit(solution)/shard_map/dot_general | solution.py:395
  194.3 1.2 copy.22
  195.5 4.8 %all-to-all-start = ((bf16[4,256,704]{1,2,0:T(8,128)(2,1)}), bf16[4,256,704]{1,2,0:T(8,128)(2,1)}, u32[]{:S(2)}, u32[]{:S(2)}) async-start(bf16[4,256,704]{1,2,0:T(8,128)(2,1)} %bitcast.53), calls=%async_computation | async-start | bytes 2883584 | tf_op jit(solution)/shard_map/all_to_all | solution.py:398
  200.2 24.1 %shard_map.110 = (f32[2,256,512]{2,1,0:T(8,128)}, f32[2,256,512]{2,1,0:T(8,128)}) custom-call(s32[64]{0:T(128)} %reshape.71.off_ref, s32[16]{0:T(128)} %copy-done.11, s32[64]{0:T(128)} %reshape.72.queue_off_ref, s32[4]{0:T(128)} %copy-done, bf16[16,128,1408]{2,1,0:T(8,128)(2,1)} %get-tuple-element.41.h0_hbm, ...), custom_call_target="tpu_custom_call" | custom-call | flops 4429185024 | bytes 23068672 | tf_op jit(solution)/shard_map/pallas_call | solution.py:364
  224.3 0.0 copy-start.3
  224.3 0.0 copy-start.1
  224.3 0.1 collective-permute-start.8
  224.4 3.4 %fusion.1 = f32[256,1536]{1,0:T(8,128)} fusion(f32[2,256,1536]{2,1,0:T(8,128)} %collective-permute-done.9, f32[2,256,1536]{2,1,0:T(8,128)} %get-tuple-element.47), kind=kLoop, calls=%fused_computation.4 | loop fusion | flops 393216 | bytes 4718592 | tf_op jit(solution)/shard_map/add | solution.py:399
  227.9 0.1 fusion.10
  228.0 0.9 copy-done.5
  228.9 2.0 collective-permute-start.11
  231.0 4.2 %all-to-all-done = bf16[4,256,704]{1,2,0:T(8,128)(2,1)} async-done(((bf16[4,256,704]{1,2,0:T(8,128)(2,1)}), bf16[4,256,704]{1,2,0:T(8,128)(2,1)}, u32[]{:S(2)}, u32[]{:S(2)}) %all-to-all-start) | async-done | bytes 1441824 | tf_op jit(solution)/shard_map/all_to_all | solution.py:398
  235.2 6.6 %fusion = f32[256,2048]{1,0:T(8,128)S(1)} fusion(bf16[4,256,704]{1,2,0:T(8,128)(2,1)} %all-to-all-done, bf16[4,704,2048]{2,1,0:T(8,128)(2,1)} %bitcast.54, bf16[256,2048]{1,0:T(8,128)(2,1)S(1)} %copy-done.1), kind=kOutput, calls=%fused_computation.2 | convolution fusion | flops 2953838592 | bytes 16121856 | tf_op jit(solution)/shard_map/sth,shd->td/dot_general | solution.py:410
  241.8 34.3 %collective-permute-done.11 = f32[256,512]{1,0:T(8,128)} collective-permute-done((f32[256,512]{1,0:T(8,128)S(1)}, f32[256,512]{1,0:T(8,128)}, u32[]{:S(2)}, u32[]{:S(2)}) %collective-permute-start.11) | collective-permute-done | bytes 524320 | tf_op jit(solution)/shard_map/ppermute | solution.py:249
  276.1 1.2 fusion.9
  277.4 2.0 fusion.5
  279.3 1.1 pad_maximum_fusion
  (44 shorter events, 0.2 us)
Async XLA Ops:
  6.5 178.3 %all-gather.3.cloned.1.call-start = ((), (), s32[]{:S(2)}) async-start(), calls=%async_computation.1 | async-start | bytes 5242880 | tf_op jit(solution)/shard_map/all_gather | solution.py:387
  7.3 223.7 %all-gather.5.cloned.1.call-start = ((), (), s32[]{:S(2)}) async-start(), calls=%async_computation.2 | async-start | bytes 11894784 | tf_op jit(solution)/shard_map/all_gather | solution.py:407
  12.2 7.9 %collective-permute-start.1 = (f32[16,256]{1,0:T(8,128)S(1)}, f32[16,256]{1,0:T(8,128)S(1)}, u32[]{:S(2)}, u32[]{:S(2)}) collective-permute-start(f32[16,256]{1,0:T(8,128)S(1)} %fusion.15), channel_id=1, source_target_pairs={{0,2},{1,3},{2,0},{3,1},{4,6},{5,7},{6,4},{7,5},{8,10},{9,11},{10,... | collective-permute-start | bytes 49160 | tf_op jit(solution)/shard_map/ppermute | solution.py:249
  15.2 5.0 %collective-permute-start = (f32[16,256]{1,0:T(8,128)S(1)}, f32[16,256]{1,0:T(8,128)S(1)}, u32[]{:S(2)}, u32[]{:S(2)}) collective-permute-start(f32[16,256]{1,0:T(8,128)S(1)} %fusion.15), channel_id=1, source_target_pairs={{0,1},{1,0},{2,3},{3,2},{4,5},{5,4},{6,7},{7,6},{8,9},{9,8},{10,11... | collective-permute-start | bytes 49160 | tf_op jit(solution)/shard_map/ppermute | solution.py:249
  15.2 40.4 %collective-permute-start.3 = (bf16[256,2048]{1,0:T(8,128)(2,1)}, bf16[256,2048]{1,0:T(8,128)(2,1)}, u32[]{:S(2)}, u32[]{:S(2)}) collective-permute-start(bf16[256,2048]{1,0:T(8,128)(2,1)} %x0_ref.1), channel_id=1, source_target_pairs={{0,1},{1,0},{2,3},{3,2},{4,5},{5,4},{6,7},{7,6},{8,9},{9,8},{10,11... | collective-permute-start | bytes 3145736 | tf_op jit(solution)/shard_map/ppermute | solution.py:249
  16.9 20.5 %collective-permute-start.4 = (bf16[256,1536]{1,0:T(8,128)(2,1)S(1)}, bf16[256,1536]{1,0:T(8,128)(2,1)S(1)}, u32[]{:S(2)}, u32[]{:S(2)}) collective-permute-start(bf16[256,1536]{1,0:T(8,128)(2,1)S(1)} %slice.48), channel_id=1, source_target_pairs={{0,2},{1,3},{2,0},{3,1},{4,6},{5,7},{6,4},{7,5},{8,10},{9,11},{10,... | collective-permute-start | bytes 2359304 | tf_op jit(solution)/shard_map/ppermute | solution.py:249
  18.0 24.0 %collective-permute-start.5 = (bf16[256,512]{1,0:T(8,128)(2,1)S(1)}, bf16[256,512]{1,0:T(8,128)(2,1)S(1)}, u32[]{:S(2)}, u32[]{:S(2)}) collective-permute-start(bf16[256,512]{1,0:T(8,128)(2,1)S(1)} %slice.49), channel_id=1, source_target_pairs={{0,2},{1,3},{2,0},{3,1},{4,6},{5,7},{6,4},{7,5},{8,10},{9,11},{10,... | collective-permute-start | bytes 786440 | tf_op jit(solution)/shard_map/ppermute | solution.py:249
  20.1 1.2 collective-permute-start.2
  21.6 35.7 %copy-start.11 = (s32[16]{0:T(128)}, s32[16]{0:T(128)S(1)}, u32[]{:S(2)}) copy-start(s32[16]{0:T(128)S(1)} %get-tuple-element.28.n_ref) | copy-start | bytes 196
  21.6 112.3 %copy-start = (s32[4]{0:T(128)}, s32[4]{0:T(128)S(1)}, u32[]{:S(2)}) copy-start(s32[4]{0:T(128)S(1)} %get-tuple-element.49.total_ref) | copy-start | bytes 52
  37.4 19.9 %copy-start.7 = (bf16[256,1536]{1,0:T(8,128)(2,1)}, bf16[256,1536]{1,0:T(8,128)(2,1)S(1)}, u32[]{:S(2)}) copy-start(bf16[256,1536]{1,0:T(8,128)(2,1)S(1)} %collective-permute-done.4.x2a_ref) | copy-start | bytes 2359300
  37.4 18.3 %collective-permute-start.6 = (bf16[256,1536]{1,0:T(8,128)(2,1)S(1)}, bf16[256,1536]{1,0:T(8,128)(2,1)S(1)}, u32[]{:S(2)}, u32[]{:S(2)}) collective-permute-start(bf16[256,1536]{1,0:T(8,128)(2,1)S(1)} %collective-permute-done.4.x2a_ref), channel_id=1, source_target_pairs={{0,1},{1,0},{2,3},{3,2},{4,5},{5,4},{6,7},{7,6},{8,9},{9,8},{10,11... | collective-permute-start | bytes 2359304 | tf_op jit(solution)/shard_map/ppermute | solution.py:249
  42.0 13.6 %copy-start.9 = (bf16[256,512]{1,0:T(8,128)(2,1)}, bf16[256,512]{1,0:T(8,128)(2,1)S(1)}, u32[]{:S(2)}) copy-start(bf16[256,512]{1,0:T(8,128)(2,1)S(1)} %collective-permute-done.5.x2b_ref) | copy-start | bytes 786436
  42.0 13.6 %collective-permute-start.7 = (bf16[256,512]{1,0:T(8,128)(2,1)S(1)}, bf16[256,512]{1,0:T(8,128)(2,1)S(1)}, u32[]{:S(2)}, u32[]{:S(2)}) collective-permute-start(bf16[256,512]{1,0:T(8,128)(2,1)S(1)} %collective-permute-done.5.x2b_ref), channel_id=1, source_target_pairs={{0,1},{1,0},{2,3},{3,2},{4,5},{5,4},{6,7},{7,6},{8,9},{9,8},{10,11... | collective-permute-start | bytes 786440 | tf_op jit(solution)/shard_map/ppermute | solution.py:249
  55.6 0.7 copy-start.10
  56.3 0.9 copy-start.8
  184.8 39.7 %collective-permute-start.9 = (f32[2,256,1536]{2,1,0:T(8,128)}, f32[2,256,1536]{2,1,0:T(8,128)}, u32[]{:S(2)}, u32[]{:S(2)}) collective-permute-start(f32[2,256,1536]{2,1,0:T(8,128)} %get-tuple-element.48), channel_id=1, source_target_pairs={{0,1},{1,0},{2,3},{3,2},{4,5},{5,4},{6,7},{7,6},{8,9},{9,8},{10,11... | collective-permute-start | bytes 9437192 | tf_op jit(solution)/shard_map/ppermute | solution.py:249
  184.9 6.0 %copy-start.12 = (bf16[1024,2048]{1,0:T(8,128)(2,1)S(1)}, bf16[1024,2048]{1,0:T(8,128)(2,1)}, u32[]{:S(2)}) copy-start(bf16[1024,2048]{1,0:T(8,128)(2,1)} %all-gather.3.cloned.1.call-done) | copy-start | bytes 12582916
  184.9 6.0 %copy-start.13 = (bf16[2048,704]{0,1:T(8,128)(2,1)S(1)}, bf16[2048,704]{0,1:T(8,128)(2,1)}, u32[]{:S(2)}) copy-start(bf16[2048,704]{0,1:T(8,128)(2,1)} %param.17) | copy-start | bytes 8650756
  195.5 39.7 %all-to-all-start = ((bf16[4,256,704]{1,2,0:T(8,128)(2,1)}), bf16[4,256,704]{1,2,0:T(8,128)(2,1)}, u32[]{:S(2)}, u32[]{:S(2)}) async-start(bf16[4,256,704]{1,2,0:T(8,128)(2,1)} %bitcast.53), calls=%async_computation | async-start | bytes 2883584 | tf_op jit(solution)/shard_map/all_to_all | solution.py:398
  224.3 3.6 %copy-start.3 = (f32[2,256,512]{2,1,0:T(8,128)S(1)}, f32[2,256,512]{2,1,0:T(8,128)}, u32[]{:S(2)}) copy-start(f32[2,256,512]{2,1,0:T(8,128)} %get-tuple-element.44) | copy-start | bytes 3145732
  224.3 10.8 %copy-start.1 = (bf16[256,2048]{1,0:T(8,128)(2,1)S(1)}, bf16[256,2048]{1,0:T(8,128)(2,1)}, u32[]{:S(2)}) copy-start(bf16[256,2048]{1,0:T(8,128)(2,1)} %x0_ref.1) | copy-start | bytes 3145732
  224.3 3.5 %collective-permute-start.8 = (f32[2,256,512]{2,1,0:T(8,128)}, f32[2,256,512]{2,1,0:T(8,128)S(1)}, u32[]{:S(2)}, u32[]{:S(2)}) collective-permute-start(f32[2,256,512]{2,1,0:T(8,128)} %get-tuple-element.45), channel_id=1, source_target_pairs={{0,1},{1,0},{2,3},{3,2},{4,5},{5,4},{6,7},{7,6},{8,9},{9,8},{10,11... | collective-permute-start | bytes 3145736 | tf_op jit(solution)/shard_map/ppermute | solution.py:249
  227.9 49.5 %collective-permute-start.10 = (f32[256,1536]{1,0:T(8,128)}, f32[256,1536]{1,0:T(8,128)S(1)}, u32[]{:S(2)}, u32[]{:S(2)}) collective-permute-start(f32[256,1536]{1,0:T(8,128)} %fusion.1), channel_id=1, source_target_pairs={{0,2},{1,3},{2,0},{3,1},{4,6},{5,7},{6,4},{7,5},{8,10},{9,11},{10,... | collective-permute-start | bytes 4718600 | tf_op jit(solution)/shard_map/ppermute | solution.py:249
  227.9 1.0 copy-start.5
  228.9 47.2 %collective-permute-start.11 = (f32[256,512]{1,0:T(8,128)S(1)}, f32[256,512]{1,0:T(8,128)}, u32[]{:S(2)}, u32[]{:S(2)}) collective-permute-start(f32[256,512]{1,0:T(8,128)S(1)} %fusion.10), channel_id=1, source_target_pairs={{0,2},{1,3},{2,0},{3,1},{4,6},{5,7},{6,4},{7,5},{8,10},{9,11},{10,... | collective-permute-start | bytes 1572872 | tf_op jit(solution)/shard_map/ppermute | solution.py:249
  235.2 40.9 %copy-start.4 = (f32[2,256,512]{2,1,0:T(8,128)S(1)}, f32[2,256,512]{2,1,0:T(8,128)}, u32[]{:S(2)}) copy-start(f32[2,256,512]{2,1,0:T(8,128)} %get-tuple-element.44) | copy-start | bytes 3145732
  235.2 40.9 %copy-start.6 = (f32[2,256,512]{2,1,0:T(8,128)S(1)}, f32[2,256,512]{2,1,0:T(8,128)}, u32[]{:S(2)}) copy-start(f32[2,256,512]{2,1,0:T(8,128)} %copy-done.5) | copy-start | bytes 3145732
  235.2 42.2 %copy-start.2 = (f32[2,256,1536]{2,1,0:T(8,128)S(1)}, f32[2,256,1536]{2,1,0:T(8,128)}, u32[]{:S(2)}) copy-start(f32[2,256,1536]{2,1,0:T(8,128)} %get-tuple-element.47) | copy-start | bytes 9437188
Sparse Core Ops, SparseCore 0:
  8.9 83.4 all-gather.2
  95.3 89.0 all-gather.4
